TPU v7x, 128 devices: a whole 4x4x4 slice. The times are simulated.
128 devices in a mesh: rows: 32 (over y, x, core), cols: 4 (over z).
Axes of the slice: x: 4, y: 4, z: 4, core: 2. Of those that a mesh axis runs over, the one named last changes fastest.
Arguments:
- token_ids: int32 [64, 2048], P('rows', 'cols'), may hold values from 0 to 524287, as said below
- lengths: int32 [64], P('rows'), may hold values from 1 to 2048
- table: bfloat16 [524288, 512], P('rows', 'cols'), may hold values from -6 to 6
- attn_gain: float32 [512], replicated, may hold values from 0.1 to 1.9
- w_qkv: bfloat16 [512, 1536], replicated, may hold values from -2 to 2
- w_out: bfloat16 [512, 512], replicated, may hold values from -0.25 to 0.25
- mlp_gain: float32 [512], replicated, may hold values from 0.1 to 1.9
- w_in: bfloat16 [512, 4096], replicated, may hold values from -0.25 to 0.25
- w_down: bfloat16 [2048, 512], replicated, may hold values from -0.125 to 0.125
Outputs:
- layer_out: bfloat16 [64, 2048, 512], P('rows', 'cols')
Inputs may be any that keep to these rules, and one draw needn't show every extreme that they name: `token_ids`: ids lie in 0 to 524287. In each aligned block of 2 histories (4096 positions) at most 341 ids fall in any one block of 16384 consecutive table rows, and in every such block of histories some block of table rows receives exactly 341.
All inputs are finite; a program needn't handle non-finite values.
Results may differ from a plain program's by a relative error of at most 0.012.
Values may be sent and summed in bfloat16 or wider, within the bound.
No kernel may reach another device: no remote copies, remote signals or barrier semaphores. Data moves between devices by JAX's collectives and lax.ppermute only.
A program may use at most 192 MiB of HBM per device.

v0:
```python
import jax
import jax.numpy as jnp
from jax import lax
from jax.sharding import PartitionSpec as P

D = 512
HEADS = 8
FF = 2048


def in_order(blocks, dim):
    blocks = jnp.moveaxis(blocks, 0, dim)
    dims = blocks.shape
    return blocks.reshape(*dims[:dim], dims[dim] * dims[dim + 1], *dims[dim + 2 :])


def sent_to_all(shard, axis):
    copies = jnp.broadcast_to(shard, (lax.axis_size(axis), *shard.shape))
    return lax.all_to_all(copies, axis, split_axis=0, concat_axis=0, tiled=True)


def gathered_copies(shard, axis, dim):
    return in_order(sent_to_all(shard, axis), dim)


def rms_norm(values_f32, gain):
    mean_sq = jnp.mean(values_f32 * values_f32, axis=-1, keepdims=True)
    return values_f32 * lax.rsqrt(mean_sq + 1e-06) * gain


def local(token_ids, lengths, table, attn_gain, w_qkv, w_out, mlp_gain, w_in, w_down):
    batch_dev, quarter = token_ids.shape
    col_count = lax.axis_size("cols")
    row_count = lax.axis_size("rows")
    full_len = quarter * col_count
    block_rows, col_width = table.shape
    zero_bf = jnp.zeros((), jnp.bfloat16)
    own_ids = gathered_copies(token_ids, "cols", 1)
    flat_ids = own_ids.reshape(-1)
    token_count = flat_ids.shape[0]
    capacity = 8 * token_count // (3 * row_count)
    owner_block = flat_ids // block_rows
    onehot = (owner_block[:, None] == jnp.arange(row_count, dtype=jnp.int32)[None, :]).astype(
        jnp.int32
    )
    slot_rank = jnp.sum((jnp.cumsum(onehot, axis=0) - 1) * onehot, axis=1)
    slot_index = owner_block * capacity + slot_rank
    requests = jnp.full((row_count * capacity,), -1, jnp.int32)
    requests = (
        requests.at[slot_index]
        .set(flat_ids - owner_block * block_rows)
        .reshape(row_count, capacity)
    )
    asked = lax.all_to_all(requests, "rows", split_axis=0, concat_axis=0, tiled=True)
    looked = jnp.take(table, jnp.maximum(asked, 0), axis=0)
    looked = jnp.where((asked >= 0)[..., None], looked, zero_bf)
    returned = lax.all_to_all(looked, "rows", split_axis=0, concat_axis=0, tiled=True)
    embedded = returned.reshape(row_count * capacity, col_width)[slot_index]
    embedded = embedded.reshape(batch_dev, full_len, col_width)
    sequence = lax.all_to_all(embedded, "cols", split_axis=1, concat_axis=2, tiled=True)
    residual = sequence.astype(jnp.float32)
    normed = rms_norm(residual, attn_gain).astype(jnp.bfloat16)
    projected = jnp.einsum("bqe,ef->bqf", normed, w_qkv, preferred_element_type=jnp.float32).astype(
        jnp.bfloat16
    )
    head_dim = D // HEADS
    queries = projected[..., :D].reshape(batch_dev, quarter, HEADS, head_dim)
    keys = projected[..., D : 2 * D]
    values = projected[..., 2 * D :]
    query_pos = lax.axis_index("cols") * quarter + jnp.arange(quarter, dtype=jnp.int32)
    running_max = jnp.full((batch_dev, HEADS, quarter), -1e30, jnp.float32)
    key_piece = lax.all_gather(keys, "cols", axis=1, tiled=True)
    value_piece = lax.all_gather(values, "cols", axis=1, tiled=True)
    piece_len = key_piece.shape[1]
    key_heads = key_piece.reshape(batch_dev, piece_len, HEADS, head_dim)
    value_heads = value_piece.reshape(batch_dev, piece_len, HEADS, head_dim)
    scores = (
        jnp.einsum("bqhd,bkhd->bhqk", queries, key_heads, preferred_element_type=jnp.float32)
        * 0.125
    )
    key_pos = jnp.arange(piece_len, dtype=jnp.int32)
    causal = key_pos[None, :] <= query_pos[:, None]
    inside = key_pos[None, :] < lengths[:, None]
    valid = causal[None, None, :, :] & inside[:, None, None, :]
    scores = jnp.where(valid, scores, -1e30)
    new_max = jnp.maximum(running_max, jnp.max(scores, axis=-1))
    probs = jnp.where(valid, jnp.exp(scores - new_max[..., None]), 0.0)
    running_sum = jnp.sum(probs, axis=-1)
    weighted = jnp.einsum(
        "bhqk,bkhd->bhqd",
        probs.astype(jnp.bfloat16),
        value_heads,
        preferred_element_type=jnp.float32,
    )
    final_max, final_sum, weighted = (new_max, running_sum, weighted)
    summed = weighted / final_sum[..., None]
    attended = (
        jnp.transpose(summed, (0, 2, 1, 3)).reshape(batch_dev, quarter, D).astype(jnp.bfloat16)
    )
    hidden = (
        residual + jnp.einsum("bqe,ef->bqf", attended, w_out, preferred_element_type=jnp.float32)
    ).astype(jnp.bfloat16)
    hidden_f32 = hidden.astype(jnp.float32)
    normed_two = rms_norm(hidden_f32, mlp_gain).astype(jnp.bfloat16)
    gate_up = jnp.einsum("bqe,ef->bqf", normed_two, w_in, preferred_element_type=jnp.float32)
    act = (jax.nn.silu(gate_up[..., :FF]) * gate_up[..., FF:]).astype(jnp.bfloat16)
    return (
        hidden_f32 + jnp.einsum("bqf,fe->bqe", act, w_down, preferred_element_type=jnp.float32)
    ).astype(jnp.bfloat16)


def solution(mesh):
    in_specs = (P("rows", "cols"), P("rows"), P("rows", "cols"), P(), P(), P(), P(), P(), P())
    out_specs = P("rows", "cols", None)
    return jax.shard_map(local, mesh=mesh, in_specs=in_specs, out_specs=out_specs, check_vma=False)
```

profile of v0, /device:TPU:0, one launch (start us, length us, event | category | flops | bytes accessed | tf_op | source)
XLA Modules:
  0.0 354.2 jit_solution(12214605746236327788)
XLA Ops:
  7.4 10.6 %all_to_all.28 = s32[4,2,512]{2,1,0:T(2,128)S(1)} all-to-all(s32[4,2,512]{2,1,0:T(2,128)S(1)} %broadcast_in_dim.67), channel_id=1, replica_groups=mesh['rows'=32,'cols'=4] {'cols'}, dimensions={0} | all-to-all | bytes 32768 | tf_op jit(solution)/shard_map/all_to_all | solution.py:19
  18.1 9.2 %reduce-window.6 = s32[32,32,128]{2,1,0:T(8,128)S(1)} reduce-window(s32[32,32,128]{2,1,0:T(8,128)S(1)} %fusion.33, s32[]{:T(128)} %constant.29.clone.1), window={size=1x1x128 pad=0_0x0_0x127_0}, to_apply=%region_0.1 | reduce-window | flops 16646144 | bytes 1048580 | tf_op jit(solution)/shard_map/reduce-window
  29.0 15.5 %scatter_custom_fusion = s32[10912]{0:T(1024)S(1)} fusion(s32[4096]{0:T(1024)S(1)} %bitcast.80, s32[4096]{0:T(1024)S(1)} %get-tuple-element.10, s32[]{:T(128)} %constant.27.clone.1), kind=kCustom, calls=%fused_computation.65 | custom fusion | bytes 43652 | tf_op jit(solution)/shard_map/scatter | solution.py:51
  44.7 14.6 %all_to_all.29 = s32[32,1,341]{2,1,0:T(1,128)S(1)} all-to-all(s32[32,1,341]{2,1,0:T(1,128)S(1)} %all_to_all.20), channel_id=1, replica_groups=mesh['rows'=32,'cols'=4] {'rows'}, dimensions={0} | all-to-all | bytes 87296 | tf_op jit(solution)/shard_map/all_to_all | solution.py:54
  59.4 23.7 %gather_fusion = bf16[10912,128]{1,0:T(8,128)(2,1)} fusion(bf16[16384,128]{1,0:T(8,128)(2,1)} %param.11, s32[11264]{0:T(1024)S(1)} %pad_clamp_fusion), kind=kCustom, calls=%fused_computation | custom fusion | bytes 5630592 | tf_op jit(solution)/shard_map/jit(_take)/gather | solution.py:55
  83.1 4.4 %reshape.254 = bf16[32,341,128]{2,1,0:T(8,128)(2,1)} reshape(bf16[10912,128]{1,0:T(8,128)(2,1)} %gather_fusion) | data formatting | bytes 5586944 | tf_op jit(solution)/shard_map/jit(_take)/gather | solution.py:55
  87.6 6.0 %select_select_fusion = bf16[32,341,128]{2,1,0:T(8,128)(2,1)} fusion(bf16[32,341,128]{2,1,0:T(8,128)(2,1)} %reshape.254, pred[32,341]{1,0:T(8,128)(4,1)S(1)} %get-tuple-element.9, pred[32,341]{1,0:T(8,128)(4,1)S(1)} %get-tuple-element.8), kind=kLoop, calls=%fused_computation.21 | loop fusion | flops 2793472 | bytes 5608768 | tf_op jit(solution)/shard_map/jit(_where)/select_n | solution.py:56
  93.6 4.8 %all-to-all-start.2 = ((bf16[32,341,128]{2,1,0:T(8,128)(2,1)}), bf16[32,341,128]{2,1,0:T(8,128)(2,1)}, u32[]{:S(2)}, u32[]{:S(2)}) async-start(bf16[32,341,128]{2,1,0:T(8,128)(2,1)} %select_select_fusion), calls=%async_computation.2 | async-start | bytes 5636096 | tf_op jit(solution)/shard_map/all_to_all | solution.py:57
  98.5 38.3 %all-to-all-done.2 = bf16[32,341,128]{2,1,0:T(8,128)(2,1)} async-done(((bf16[32,341,128]{2,1,0:T(8,128)(2,1)}), bf16[32,341,128]{2,1,0:T(8,128)(2,1)}, u32[]{:S(2)}, u32[]{:S(2)}) %all-to-all-start.2) | async-done | bytes 2793504 | tf_op jit(solution)/shard_map/all_to_all | solution.py:57
  136.8 4.4 %reshape.246 = bf16[10912,128]{1,0:T(8,128)(2,1)} reshape(bf16[32,341,128]{2,1,0:T(8,128)(2,1)} %all-to-all-done.2) | data formatting | bytes 5586944 | tf_op jit(solution)/shard_map/reshape | solution.py:58
  141.2 13.2 %gather_fusion.1 = bf16[4096,128]{1,0:T(8,128)(2,1)S(1)} fusion(bf16[10912,128]{1,0:T(8,128)(2,1)} %reshape.246, s32[4096]{0:T(1024)S(1)} %broadcast_clamp_fusion), kind=kCustom, calls=%fused_computation.1 | custom fusion | bytes 2113536 | tf_op jit(solution)/shard_map/gather | solution.py:58
  154.4 8.7 %copy.63 = bf16[2,2048,128]{2,0,1:T(2,128)(2,1)S(1)} copy(bf16[2,2048,128]{2,1,0:T(8,128)(2,1)S(1)} %bitcast.73) | data formatting | bytes 2097152 | tf_op jit(solution)/shard_map/reshape | solution.py:59
  163.1 15.8 %all_to_all.30 = bf16[2,2048,128]{2,0,1:T(2,128)(2,1)S(1)} all-to-all(bf16[2,2048,128]{2,0,1:T(2,128)(2,1)S(1)} %copy.63), channel_id=1, replica_groups=mesh['rows'=32,'cols'=4] {'cols'}, dimensions={1} | all-to-all | bytes 2097152 | tf_op jit(solution)/shard_map/all_to_all | solution.py:60
  180.4 2.9 copy.65
  185.8 3.2 convolution_convert_fusion
  195.6 40.6 %all-gather.3.cloned.1.call-done = bf16[2,2048,512]{2,1,0:T(8,128)(2,1)} async-done(((bf16[2,512,512]{2,1,0:T(8,128)(2,1)}), bf16[2,2048,512]{2,1,0:T(8,128)(2,1)}) %all-gather.3.cloned.1.call-update) | async-done | bytes 4194320 | tf_op jit(solution)/shard_map/all_gather | solution.py:72
  236.2 6.3 %copy.68 = bf16[2,2048,512]{1,2,0:T(8,128)(2,1)} copy(bf16[2,2048,512]{2,1,0:T(8,128)(2,1)} %all-gather.3.cloned.1.call-done) | data formatting | bytes 8388608 | tf_op jit(solution)/shard_map/all_gather | solution.py:72
  242.5 27.8 %fusion = (f32[2,8,512]{2,1,0:T(8,128)S(1)}, f32[2,8,512,2048]{3,2,1,0:T(8,128)}) fusion(pred[2,512,2048]{2,1,0:T(8,128)(4,1)} %broadcast_and_fusion, bf16[2,512,8,64]{1,3,2,0:T(8,128)(2,1)} %bitcast.72, bf16[2,2048,8,64]{1,3,2,0:T(8,128)(2,1)} %bitcast.70), kind=kOutput, calls=%fused_computation.5 | convolution fusion | flops 2197807104 | bytes 74481664 | tf_op jit(solution)/shard_map/bqhd,bkhd->bhqk/dot_general | solution.py:78
  270.3 22.5 %fusion.1 = f32[2,8,512]{2,1,0:T(8,128)S(1)} fusion(f32[2,8,512,2048]{3,2,1,0:T(8,128)} %get-tuple-element.15, f32[2,8,512]{2,1,0:T(8,128)S(1)} %broadcast_maximum_fusion, pred[2,512,2048]{2,1,0:T(8,128)(4,1)S(1)} %copy-done.1), kind=kLoop, calls=%fused_computation.6 | loop fusion | flops 83877888 | bytes 69271552 | tf_op jit(solution)/shard_map/reduce_sum | solution.py:88
  292.8 6.3 %copy.69 = bf16[2,2048,512]{1,2,0:T(8,128)(2,1)} copy(bf16[2,2048,512]{2,1,0:T(8,128)(2,1)} %all-gather.5.cloned.1.call-done) | data formatting | bytes 8388608 | tf_op jit(solution)/shard_map/all_gather | solution.py:73
  299.1 27.0 %fusion.16 = bf16[2,512,8,64]{1,3,2,0:T(8,128)(2,1)S(1)} fusion(bf16[2,2048,8,64]{1,3,2,0:T(8,128)(2,1)} %bitcast.74, f32[2,8,512,2048]{3,2,1,0:T(8,128)} %get-tuple-element.15, f32[2,8,512]{2,1,0:T(8,128)S(1)} %broadcast_maximum_fusion, pred[2,512,2048]{2,1,0:T(8,128)(4,1)} %broadcast_and_fusion, f32[2,512,8]{1,2,0:T(8,128)S(1)} %bitcast.84), kind=kOutput, calls=%fused_computation.28 | convolution fusion | flops 2232418304 | bytes 74514432 | tf_op jit(solution)/shard_map/bhqk,bkhd->bhqd/dot_general | solution.py:89
  326.1 2.7 fusion.11
  329.1 8.3 %fusion.7 = f32[2,512,4096]{2,1,0:T(8,128)} fusion(bf16[512,4096]{1,0:T(8,128)(2,1)S(1)} %copy-done.4, bf16[2,512,512]{1,2,0:T(8,128)(2,1)S(1)} %get-tuple-element.17, f32[512]{0:T(512)S(1)} %copy-done.5, f32[2,512]{1,0:T(2,128)S(1)} %add_rsqrt_fusion), kind=kOutput, calls=%fused_computation.12 | convolution fusion | flops 4297064448 | bytes 22026240 | tf_op jit(solution)/shard_map/bqe,ef->bqf/dot_general | solution.py:105
  337.4 8.6 %fusion.14 = bf16[2,512,512]{1,2,0:T(8,128)(2,1)S(1)} fusion(bf16[2,512,512]{1,2,0:T(8,128)(2,1)S(1)} %get-tuple-element.17, bf16[2048,512]{1,0:T(8,128)(2,1)S(1)} %copy-done, f32[2,512,4096]{2,1,0:T(8,128)} %fusion.7), kind=kOutput, calls=%fused_computation.25 | convolution fusion | flops 2161639424 | bytes 20971520 | tf_op jit(solution)/shard_map/bqf,fe->bqe/dot_general | solution.py:108
  (51 shorter events, 15.1 us)
Async XLA Ops:
  6.5 330.9 %copy-start = (bf16[2048,512]{1,0:T(8,128)(2,1)S(1)}, bf16[2048,512]{1,0:T(8,128)(2,1)}, u32[]{:S(2)}) copy-start(bf16[2048,512]{1,0:T(8,128)(2,1)} %param.17) | copy-start | bytes 6291460
  93.6 43.2 %all-to-all-start.2 = ((bf16[32,341,128]{2,1,0:T(8,128)(2,1)}), bf16[32,341,128]{2,1,0:T(8,128)(2,1)}, u32[]{:S(2)}, u32[]{:S(2)}) async-start(bf16[32,341,128]{2,1,0:T(8,128)(2,1)} %select_select_fusion), calls=%async_computation.2 | async-start | bytes 5636096 | tf_op jit(solution)/shard_map/all_to_all | solution.py:57
  98.4 137.8 %all-gather.3.cloned.1.call-start = ((), (), s32[]{:S(2)}) async-start(), calls=%async_computation.4 | async-start | bytes 5242880 | tf_op jit(solution)/shard_map/all_gather | solution.py:72
  178.9 5.1 %copy-start.2 = (f32[512]{0:T(512)S(1)}, f32[512]{0:T(512)}, u32[]{:S(2)}) copy-start(f32[512]{0:T(512)} %param.12) | copy-start | bytes 6148
  189.1 1.8 copy-start.3
  190.8 102.0 %all-gather.5.cloned.1.call-start = ((), (), s32[]{:S(2)}) async-start(), calls=%async_computation.5 | async-start | bytes 5242880 | tf_op jit(solution)/shard_map/all_gather | solution.py:73
  242.5 27.8 %copy-start.1 = (pred[2,512,2048]{2,1,0:T(8,128)(4,1)S(1)}, pred[2,512,2048]{2,1,0:T(8,128)(4,1)}, u32[]{:S(2)}) copy-start(pred[2,512,2048]{2,1,0:T(8,128)(4,1)} %broadcast_and_fusion) | copy-start | bytes 6291460
  326.1 3.0 copy-start.4
  326.1 3.0 copy-start.5
Sparse Core Ops, SparseCore 0:
  190.9 45.2 all-gather.2
  237.9 48.5 all-gather.4
where the time goes:
time: 356 us; the launch traced here: 354 us
  local copies, waits for them, and re-layouts  92 us (26%)
  waiting for transfers between devices  79 us (22%)
  matrix products  77.6 us (22%)
  other arithmetic  46 us (13%)
  blocking collectives  40.9 us (11%)
  between operations  13.7 us (4%)
  starting transfers between devices  4.88 us (1%)
    all_gather x1, waiting for transfers between devices, local(): key_piece = lax.all_gather(keys, 'cols', axis=1, tiled=True)  40.6 us
    all_to_all x1, waiting for transfers between devices, local(): lax.all_to_all(looked, 'rows', split_axis=0, concat_axis=0, tiled=True)  38.3 us
    gather x2, local copies, waits for them, and re-layouts, local(): looked = jnp.take(table, jnp.maximum(asked, 0), axis=0)  28.1 us
    dot_general x1, matrix products, local(): jnp.einsum('bqhd,bkhd->bhqk', queries, key_heads, preferred_element_type=...  27.8 us
    dot_general x1, matrix products, local(): jnp.einsum('bhqk,bkhd->bhqd', probs.astype(jnp.bfloat16), value_heads, pr...  27 us
    reduce_sum x1, other arithmetic, local(): running_sum = jnp.sum(probs, axis=-1)  22.5 us
    all_to_all x1, blocking collectives, local(): lax.all_to_all(embedded, 'cols', split_axis=1, concat_axis=2, tiled=True)  15.8 us
    scatter x1, local copies, waits for them, and re-layouts, local(): requests = requests.at[slot_index].set(flat_ids - owner_block * block_row...  15.5 us
  transfers between devices with their start and end apart: 3, of which 2 were waited for; matrix products, arithmetic and copies ran while one was open for 17% of the time, Pallas kernels for 0%

commit v1 on v0

v1 whole, which is shorter than its diff:
```python
import functools

import jax
import jax.numpy as jnp
from jax import lax
from jax.experimental import pallas as pl
from jax.experimental.pallas import tpu as pltpu
from jax.sharding import PartitionSpec as P

D = 512
HEADS = 8
FF = 2048
CAP = 344
REQ = 384
LOG2E = 1.4426950408889634
SWAP = [(0, 1), (1, 0), (2, 3), (3, 2)]
CROSS = [(0, 3), (3, 0), (1, 2), (2, 1)]
VM = pl.BlockSpec(memory_space=pltpu.VMEM)
SM = pl.BlockSpec(memory_space=pltpu.SMEM)
F32 = jnp.float32
BF = jnp.bfloat16
I32 = jnp.int32


def dot(a, b):
    return lax.dot_general(a, b, (((1,), (0,)), ((), ())), preferred_element_type=F32)


def dot_t(a, b):
    return lax.dot_general(a, b, (((1,), (1,)), ((), ())), preferred_element_type=F32)


def params(mib):
    return pltpu.CompilerParams(vmem_limit_bytes=mib * 1024 * 1024)


def route_kernel(row_bits, owners, ids_ref, slot_ref, req_ref):
    rows, width = ids_ref.shape
    parts = REQ // 128
    upper = (
        lax.broadcasted_iota(I32, (width, width), 0) < lax.broadcasted_iota(I32, (width, width), 1)
    ).astype(BF)
    owner_iota = lax.broadcasted_iota(I32, (owners, width), 0)
    group_iota = lax.broadcasted_iota(I32, (owners * parts, width), 0)
    lane_iota = lax.broadcasted_iota(I32, (128, width), 0)
    carry = jnp.zeros((owners, 1), F32)
    total = jnp.zeros((owners * parts, 256), F32)
    for r in range(rows):
        ids = ids_ref[r : r + 1, :]
        owner = lax.shift_right_logical(ids, row_bits)
        offset = ids & ((1 << row_bits) - 1)
        hot = (owner_iota == owner).astype(F32)
        before = dot(hot.astype(BF), upper) + carry
        rank = jnp.sum(hot * before, axis=0, keepdims=True).astype(I32)
        carry = carry + jnp.sum(hot, axis=1, keepdims=True)
        slot_ref[r : r + 1, :] = owner * CAP + rank
        group = owner * parts + lax.shift_right_logical(rank, 7)
        in_group = (group_iota == group).astype(BF)
        at_lane = lane_iota == (rank & 127)
        high = jnp.where(at_lane, lax.shift_right_logical(offset, 7), 0).astype(F32).astype(BF)
        low = jnp.where(at_lane, offset & 127, 0).astype(F32).astype(BF)
        total = total + dot_t(in_group, jnp.concatenate([high, low], axis=0))
    count = carry.astype(I32)
    last_group = (
        lax.broadcasted_iota(I32, (owners * parts, owners), 0)
        == lax.broadcasted_iota(I32, (owners * parts, owners), 1) * parts + parts - 1
    ).astype(BF)
    lane = lax.broadcasted_iota(I32, (owners, 256), 1)
    digits = jnp.where(
        lane == 127,
        lax.shift_right_logical(count, 7),
        jnp.where(lane == 255, count & 127, 0),
    )
    total = total + dot(last_group, digits.astype(F32).astype(BF))
    req_ref[...] = total[:, :128].astype(I32) * 128 + total[:, 128:].astype(I32)


def route(ids, row_bits, owners):
    return pl.pallas_call(
        functools.partial(route_kernel, row_bits, owners),
        out_shape=(
            jax.ShapeDtypeStruct(ids.shape, I32),
            jax.ShapeDtypeStruct((owners * (REQ // 128), 128), I32),
        ),
        in_specs=[VM],
        out_specs=(VM, VM),
        compiler_params=params(16),
        name="route",
    )(ids)


def lookup_kernel(asked_ref, table_ref, out_ref, wide_ref, row_ref):
    block_rows = table_ref.shape[0]
    owners = asked_ref.shape[0]
    step = 512

    def widen(i, _):
        at = pl.ds(pl.multiple_of(i * step, step), step)
        wide_ref[at, :] = table_ref[at, :].astype(F32)
        return 0

    lax.fori_loop(0, block_rows // step, widen, 0)

    def one(d, _):
        count = asked_ref[d, REQ - 1]

        def eight(i, _):
            base = pl.multiple_of(i * 8, 8)
            for k in range(8):
                row_ref[pl.ds(base + k, 1), :] = wide_ref[pl.ds(asked_ref[d, base + k], 1), :]
            return 0

        lax.fori_loop(0, (count + 7) // 8, eight, 0)
        out_ref[d] = row_ref[...].astype(BF)
        return 0

    lax.fori_loop(0, owners, one, 0)


def lookup(asked, table):
    owners = asked.shape[0]
    return pl.pallas_call(
        lookup_kernel,
        out_shape=jax.ShapeDtypeStruct((owners, CAP, table.shape[1]), BF),
        in_specs=[SM, VM],
        out_specs=VM,
        scratch_shapes=[
            pltpu.VMEM(table.shape, F32),
            pltpu.VMEM((CAP, table.shape[1]), F32),
        ],
        compiler_params=params(24),
        name="lookup",
    )(asked, table)


def unpermute_kernel(slot_ref, got_ref, out_ref, wide_ref, row_ref):
    total = got_ref.shape[0]
    count = out_ref.shape[0]
    step = CAP * 2
    block = row_ref.shape[0]

    def widen(i, _):
        at = pl.ds(pl.multiple_of(i * step, step), step)
        wide_ref[at, :] = got_ref[at, :].astype(F32)
        return 0

    lax.fori_loop(0, total // step, widen, 0)

    def chunk(j, _):
        def eight(i, _):
            base = pl.multiple_of(i * 16, 16)
            for k in range(16):
                row_ref[pl.ds(base + k, 1), :] = wide_ref[pl.ds(slot_ref[j, base + k], 1), :]
            return 0

        lax.fori_loop(0, block // 16, eight, 0)
        out_ref[pl.ds(pl.multiple_of(j * block, block), block), :] = row_ref[...].astype(BF)
        return 0

    lax.fori_loop(0, count // block, chunk, 0)


def unpermute(slots, got):
    rows, width = slots.shape
    return pl.pallas_call(
        unpermute_kernel,
        out_shape=jax.ShapeDtypeStruct((rows * width, got.shape[1]), BF),
        in_specs=[SM, VM],
        out_specs=VM,
        scratch_shapes=[pltpu.VMEM(got.shape, F32), pltpu.VMEM((width, got.shape[1]), F32)],
        compiler_params=params(16),
        name="unpermute",
    )(slots, got)


def attend_quarter(q, length, qkv_ref, out_ref, where, s_ref, v_ref):
    n = s_ref.shape[1]
    full = jnp.minimum(q, length // n)
    some = jnp.minimum(q + 1, (length + n - 1) // n)
    lane = lax.broadcasted_iota(I32, (n, 128), 1)
    rows = pl.ds(pl.multiple_of(q * n, n), n)
    row_pos = q * n + lax.broadcasted_iota(I32, (n, n), 0)
    limit = jnp.minimum(row_pos + 1, length)
    for pair in range(2):
        qp = qkv_ref[rows, pair * 128 : pair * 128 + 128]
        halves = []
        for h in range(2):
            qh = jnp.where((lane < 64) == (h == 0), qp, jnp.zeros_like(qp))

            def block(j, masked):
                at = pl.ds(pl.multiple_of(j * n, n), n)
                s = dot_t(qh, qkv_ref[at, 256 + pair * 128 : 384 + pair * 128]) * (0.125 * LOG2E)
                if masked:
                    col = j * n + lax.broadcasted_iota(I32, (n, n), 1)
                    s = jnp.where(col < limit, s, -1e30)
                s_ref[j] = s
                part = jnp.maximum(
                    jnp.maximum(s[:, 0:128], s[:, 128:256]), jnp.maximum(s[:, 256:384], s[:, 384:512])
                )
                return part

            m = jnp.full((n, 128), -1e30, F32)
            m = lax.fori_loop(0, full, lambda j, m: jnp.maximum(m, block(j, False)), m)
            m = lax.fori_loop(full, some, lambda j, m: jnp.maximum(m, block(j, True)), m)
            top = jnp.max(m, axis=1, keepdims=True)

            def weigh(j, acc):
                at = pl.ds(pl.multiple_of(j * n, n), n)
                p = jnp.exp2(s_ref[j] - top).astype(BF)
                return acc + dot(p, v_ref[pair, at, :])

            acc = lax.fori_loop(0, some, weigh, jnp.zeros((n, 256), F32))
            halves.append(acc[:, :128] / acc[:, 128:])
        out_ref[where, :, pair * 128 : pair * 128 + 128] = jnp.where(
            lane < 64, halves[0], halves[1]
        ).astype(BF)


def fill_values(qkv_ref, v_ref):
    for pair in range(2):
        v_ref[pair, :, 0:128] = qkv_ref[:, 512 + pair * 128 : 640 + pair * 128]
        v_ref[pair, :, 128:256] = jnp.ones((v_ref.shape[1], 128), BF)


def first_kernel(
    meta_ref, s0, s1, s2, s3, gain_ref, w_ref, qkv_ref, att_ref, res_ref, own_w_ref, s_ref, v_ref
):
    c = meta_ref[0]
    length = meta_ref[1]
    n = s_ref.shape[1]
    g = lax.rem(c, 2)
    mate = c + 1 - 2 * g
    slices = ((s0, c), (s1, mate), (s2, 3 - c), (s3, 3 - mate))

    def project(q, keep):
        rows = pl.ds(pl.multiple_of(q * n, n), n)
        wide = [ref[rows, :].astype(F32) for ref, _ in slices]
        square = sum(x * x for x in wide)
        scale = lax.rsqrt(jnp.sum(square, axis=1, keepdims=True) * (1.0 / D) + 1e-06)
        for x, (ref, i) in zip(wide, slices):
            lanes = pl.ds(pl.multiple_of(i * 128, 128), 128)
            if keep is not None:
                res_ref[keep, :, lanes] = ref[rows, :]
        normed = jnp.concatenate(
            [
                (x * scale * gain_ref[pl.ds(i, 1), :]).astype(BF)
                for x, (_, i) in zip(wide, slices)
            ],
            axis=1,
        )
        for k in range(3):
            part = slice(k * 256, k * 256 + 256)
            qkv_ref[rows, part] = dot(normed, own_w_ref[:, part]).astype(BF)

    for at, (_, i) in enumerate(slices):
        for k in range(3):
            lanes = pl.ds(pl.multiple_of(k * D + g * 256, 256), 256)
            own_w_ref[at * 128 : at * 128 + 128, k * 256 : k * 256 + 256] = w_ref[
                pl.ds(pl.multiple_of(i * 128, 128), 128), lanes
            ]
    project(3 - c, 0)
    project(c, 1)
    project(3 - mate, None)
    project(mate, None)
    fill_values(qkv_ref, v_ref)
    for where in range(2):
        q = 3 - mate if where == 0 else mate
        attend_quarter(q, length, qkv_ref, att_ref, where, s_ref, v_ref)


def second_kernel(meta_ref, qkv_ref, att_ref, s_ref, v_ref):
    c = meta_ref[0]
    fill_values(qkv_ref, v_ref)
    for where in range(2):
        q = 3 - c if where == 0 else c
        attend_quarter(q, meta_ref[1], qkv_ref, att_ref, where, s_ref, v_ref)


def first(meta, slices, gain, w_qkv, quarter):
    length = slices[0].shape[0]
    return pl.pallas_call(
        first_kernel,
        out_shape=(
            jax.ShapeDtypeStruct((length, 768), BF),
            jax.ShapeDtypeStruct((2, quarter, 256), BF),
            jax.ShapeDtypeStruct((2, quarter, D), BF),
        ),
        in_specs=[SM] + [VM] * 6,
        out_specs=(VM, VM, VM),
        scratch_shapes=[
            pltpu.VMEM((D, 768), BF),
            pltpu.VMEM((length // quarter, quarter, quarter), F32),
            pltpu.VMEM((2, length, 256), BF),
        ],
        compiler_params=params(40),
        name="project_attend",
    )(meta, *slices, gain, w_qkv)


def second(meta, qkv, quarter):
    length = qkv.shape[0]
    return pl.pallas_call(
        second_kernel,
        out_shape=jax.ShapeDtypeStruct((2, quarter, 256), BF),
        in_specs=[SM, VM],
        out_specs=VM,
        scratch_shapes=[
            pltpu.VMEM((length // quarter, quarter, quarter), F32),
            pltpu.VMEM((2, length, 256), BF),
        ],
        compiler_params=params(32),
        name="attend",
    )(meta, qkv)


def mlp_kernel(meta_ref, own_ref, other_ref, res_ref, wo_ref, gain_ref, wi_ref, wd_ref, out_ref):
    g = lax.rem(meta_ref[0], 2)
    hidden = (
        res_ref[...].astype(F32) + dot(own_ref[...], wo_ref[g]) + dot(other_ref[...], wo_ref[1 - g])
    ).astype(BF)
    hidden = hidden.astype(F32)
    scale = lax.rsqrt(jnp.mean(hidden * hidden, axis=1, keepdims=True) + 1e-06)
    normed = (hidden * scale * gain_ref[...]).astype(BF)
    acc = hidden
    step = 512
    for k in range(FF // step):
        gate = dot(normed, wi_ref[:, k * step : k * step + step])
        up = dot(normed, wi_ref[:, FF + k * step : FF + k * step + step])
        half = 0.5 * gate
        act = ((half + half * jnp.tanh(half)) * up).astype(BF)
        acc = acc + dot(act, wd_ref[k * step : k * step + step, :])
    out_ref[...] = acc.astype(BF)


def mlp(meta, own, other, res, w_out, gain, w_in, w_down):
    return pl.pallas_call(
        mlp_kernel,
        out_shape=jax.ShapeDtypeStruct(res.shape, BF),
        in_specs=[SM] + [VM] * 7,
        out_specs=VM,
        compiler_params=params(24),
        name="mlp",
    )(meta, own, other, res, w_out, gain, w_in, w_down)


def exchange(x, pairs):
    return lax.ppermute(x, "cols", pairs)


def local(token_ids, lengths, table, attn_gain, w_qkv, w_out, mlp_gain, w_in, w_down):
    batch_dev, quarter = token_ids.shape
    owners = lax.axis_size("rows")
    col_count = lax.axis_size("cols")
    c = lax.axis_index("cols")
    h = c // 2
    meta = jnp.stack([c, lax.dynamic_index_in_dim(lengths, h, 0, False)]).astype(I32)
    row_bits = (table.shape[0] - 1).bit_length()

    copies = jnp.broadcast_to(token_ids, (col_count, *token_ids.shape))
    ids = lax.all_to_all(copies, "cols", split_axis=0, concat_axis=0, tiled=True)
    ids = jnp.transpose(ids, (1, 0, 2)).reshape(batch_dev * col_count, quarter)
    slots, requests = route(ids, row_bits, owners)
    asked = lax.all_to_all(
        requests.reshape(owners, REQ), "rows", split_axis=0, concat_axis=0, tiled=True
    )
    looked = lookup(asked, table)
    got = lax.all_to_all(looked, "rows", split_axis=0, concat_axis=0, tiled=True)
    got = got.reshape(owners * CAP, table.shape[1])
    slots = slots.reshape(batch_dev, col_count, quarter)
    theirs = unpermute(lax.dynamic_index_in_dim(slots, 1 - h, 0, False), got)
    mine = unpermute(lax.dynamic_index_in_dim(slots, h, 0, False), got)
    crossed = exchange(theirs, CROSS)
    swapped = exchange(mine, SWAP)
    relayed = exchange(crossed, SWAP)

    qkv, att_mate, res = first(
        meta, (mine, swapped, crossed, relayed), attn_gain.reshape(4, 128), w_qkv, quarter
    )
    other_0 = exchange(att_mate[0], SWAP)
    other_1 = exchange(att_mate[1], SWAP)
    att = second(meta, qkv, quarter)
    halves = w_out.reshape(2, 256, D)
    gain = mlp_gain.reshape(1, D)
    sent = mlp(meta, att[0], other_0, res[0], halves, gain, w_in, w_down)
    came = exchange(sent, CROSS)
    kept = mlp(meta, att[1], other_1, res[1], halves, gain, w_in, w_down)
    mine_first = h == 0
    return jnp.stack([jnp.where(mine_first, kept, came), jnp.where(mine_first, came, kept)])


def solution(mesh):
    in_specs = (P("rows", "cols"), P("rows"), P("rows", "cols"), P(), P(), P(), P(), P(), P())
    out_specs = P("rows", "cols", None)
    return jax.shard_map(local, mesh=mesh, in_specs=in_specs, out_specs=out_specs, check_vma=False)
```

time: 356 us -> 197 us (0.55)
  local copies, waits for them, and re-layouts: 92 us -> 8.12 us
  matrix products: 77.6 us -> 0 us
  Pallas kernels: 0 us -> 69.3 us
  other arithmetic: 46 us -> 2.88 us
  blocking collectives: 40.9 us -> 25.1 us
  between operations: 13.7 us -> 0.2 us
  starting transfers between devices: 4.88 us -> 16.3 us
  waiting for transfers between devices: 79 us -> 74 us
    dot_general x6 -> x0, matrix products: 77.6 us -> none  [the longest x1 27.8 us: local(): jnp.einsum('bqhd,bkhd->bhqk', queries, key_heads, preferred_element_type=...]
    pallas_call x0 -> x8, Pallas kernels: none -> 69.3 us  [the longest x1 16.6 us: first(): pl.pallas_call(first_kernel, out_shape=(jax.ShapeDtypeStruct((length, 768...]
    gather x3 -> x0, local copies, waits for them, and re-layouts: 41.3 us -> none  [the longest x2 28.1 us: local(): looked = jnp.take(table, jnp.maximum(asked, 0), axis=0)]
    all_gather x2 -> x0, waiting for transfers between devices: 40.6 us -> none  [the longest x1 40.6 us: local(): key_piece = lax.all_gather(keys, 'cols', axis=1, tiled=True)]
    ppermute x0 -> x6, waiting for transfers between devices: none -> 35.7 us  [exchange(): return lax.ppermute(x, 'cols', pairs)]
    reduce_sum x4 -> x0, other arithmetic: 23.5 us -> none  [the longest x1 22.5 us: local(): running_sum = jnp.sum(probs, axis=-1)]
    all_to_all x3 -> x2, blocking collectives: 40.9 us -> 25.1 us  [the longest x1 14.6 us: local(): lax.all_to_all(requests.reshape(owners, REQ), 'rows', split_axis=0, conca...]
    scatter x1 -> x0, local copies, waits for them, and re-layouts: 15.5 us -> none  [local(): requests = requests.at[slot_index].set(flat_ids - owner_block * block_row...]
  transfers between devices with their start and end apart: 3 -> 7, of which waited for: 2 -> 6; matrix products, arithmetic and copies ran while one was open for 17% -> 1% of each run, Pallas kernels for 0% -> 6%
where the time goes in v1:
time: 197 us; the launch traced here: 196 us
  waiting for transfers between devices  74 us (38%)
  Pallas kernels  69.3 us (35%)
  blocking collectives  25.1 us (13%)
  starting transfers between devices  16.3 us (8%)
  local copies, waits for them, and re-layouts  8.12 us (4%)
  other arithmetic  2.88 us (1%)
    all_to_all x1, waiting for transfers between devices, local(): lax.all_to_all(looked, 'rows', split_axis=0, concat_axis=0, tiled=True)  38.3 us
    ppermute x6, waiting for transfers between devices, exchange(): return lax.ppermute(x, 'cols', pairs)  35.7 us
    pallas_call x1, Pallas kernels, first(): pl.pallas_call(first_kernel, out_shape=(jax.ShapeDtypeStruct((length, 768...  16.6 us
    pallas_call x1, Pallas kernels, lookup(): pl.pallas_call(lookup_kernel, out_shape=jax.ShapeDtypeStruct((owners, CAP...  14.6 us
    all_to_all x1, blocking collectives, local(): lax.all_to_all(requests.reshape(owners, REQ), 'rows', split_axis=0, conca...  14.6 us
    pallas_call x2, Pallas kernels, unpermute(): pl.pallas_call(unpermute_kernel, out_shape=jax.ShapeDtypeStruct((rows * w...  13.6 us
    pallas_call x1, Pallas kernels, second(): pl.pallas_call(second_kernel, out_shape=jax.ShapeDtypeStruct((2, quarter,...  11.6 us
    pallas_call x2, Pallas kernels, mlp(): pl.pallas_call(mlp_kernel, out_shape=jax.ShapeDtypeStruct(res.shape, BF),...  11.2 us
  transfers between devices with their start and end apart: 7, of which 6 were waited for; matrix products, arithmetic and copies ran while one was open for 1% of the time, Pallas kernels for 6%

profile of v1, /device:TPU:0, one launch (start us, length us, event | category | flops | bytes accessed | tf_op | source)
XLA Modules:
  0.0 196.0 jit_solution(5991772736572570394)
XLA Ops:
  0.7 10.6 %all_to_all.21 = s32[4,2,512]{2,1,0:T(2,128)S(1)} all-to-all(s32[4,2,512]{2,1,0:T(2,128)S(1)} %broadcast_in_dim.3), channel_id=1, replica_groups=mesh['rows'=32,'cols'=4] {'cols'}, dimensions={0} | all-to-all | bytes 32768 | tf_op jit(solution)/shard_map/all_to_all | solution.py:360
  11.3 1.7 route.1
  13.0 14.6 %all_to_all.22 = s32[32,1,384]{2,1,0:T(1,128)S(1)} all-to-all(s32[32,1,384]{2,1,0:T(1,128)S(1)} %bitcast.35), channel_id=1, replica_groups=mesh['rows'=32,'cols'=4] {'rows'}, dimensions={0} | all-to-all | bytes 98304 | tf_op jit(solution)/shard_map/all_to_all | solution.py:363
  27.6 2.2 %copy-done.4 = bf16[16384,128]{1,0:T(8,128)(2,1)S(1)} copy-done((bf16[16384,128]{1,0:T(8,128)(2,1)S(1)}, bf16[16384,128]{1,0:T(8,128)(2,1)}, u32[]{:S(2)}) %copy-start.4) | copy-done | bytes 4194328
  29.8 14.6 %lookup.1 = bf16[32,344,128]{2,1,0:T(8,128)(2,1)S(1)} custom-call(s32[32,384]{1,0:T(8,128)S(1)} %bitcast.34, bf16[16384,128]{1,0:T(8,128)(2,1)S(1)} %copy-done.4), custom_call_target="tpu_custom_call" | custom-call | tf_op jit(solution)/shard_map/lookup/pallas_call | solution.py:122
  44.4 1.5 copy-done.2
  46.0 6.2 %all-to-all-start.2 = ((bf16[32,344,128]{2,1,0:T(8,128)(2,1)}), bf16[32,344,128]{2,1,0:T(8,128)(2,1)S(1)}, u32[]{:S(2)}, u32[]{:S(2)}) async-start(bf16[32,344,128]{2,1,0:T(8,128)(2,1)} %copy-done.2), calls=%async_computation.2 | async-start | bytes 5636096 | tf_op jit(solution)/shard_map/all_to_all | solution.py:367
  52.2 38.3 %all-to-all-done.2 = bf16[32,344,128]{2,1,0:T(8,128)(2,1)S(1)} async-done(((bf16[32,344,128]{2,1,0:T(8,128)(2,1)}), bf16[32,344,128]{2,1,0:T(8,128)(2,1)S(1)}, u32[]{:S(2)}, u32[]{:S(2)}) %all-to-all-start.2) | async-done | bytes 2818080 | tf_op jit(solution)/shard_map/all_to_all | solution.py:367
  90.6 6.8 %unpermute.3 = bf16[2048,128]{1,0:T(8,128)(2,1)S(1)} custom-call(s32[4,512]{1,0:T(4,128)S(1)} %get-tuple-element.23.slot_ref, bf16[11008,128]{1,0:T(8,128)(2,1)S(1)} %bitcast.30), custom_call_target="tpu_custom_call" | custom-call | tf_op jit(solution)/shard_map/unpermute/pallas_call | solution.py:165
  97.4 1.2 collective-permute-start.1
  98.6 6.8 %unpermute.2.s0 = bf16[2048,128]{1,0:T(8,128)(2,1)S(1)} custom-call(s32[4,512]{1,0:T(4,128)S(1)} %get-tuple-element.24.slot_ref, bf16[11008,128]{1,0:T(8,128)(2,1)S(1)} %bitcast.31), custom_call_target="tpu_custom_call" | custom-call | tf_op jit(solution)/shard_map/unpermute/pallas_call | solution.py:165
  105.5 4.8 %collective-permute-done.1.s2 = bf16[2048,128]{1,0:T(8,128)(2,1)S(1)} collective-permute-done((bf16[2048,128]{1,0:T(8,128)(2,1)S(1)}, bf16[2048,128]{1,0:T(8,128)(2,1)S(1)}, u32[]{:S(2)}, u32[]{:S(2)}) %collective-permute-start.1) | collective-permute-done | bytes 524320 | tf_op jit(solution)/shard_map/ppermute | solution.py:347
  111.7 8.6 %collective-permute-done.s1 = bf16[2048,128]{1,0:T(8,128)(2,1)S(1)} collective-permute-done((bf16[2048,128]{1,0:T(8,128)(2,1)S(1)}, bf16[2048,128]{1,0:T(8,128)(2,1)S(1)}, u32[]{:S(2)}, u32[]{:S(2)}) %collective-permute-start) | collective-permute-done | bytes 524320 | tf_op jit(solution)/shard_map/ppermute | solution.py:347
  120.3 7.9 %collective-permute-done.2.s3 = bf16[2048,128]{1,0:T(8,128)(2,1)S(1)} collective-permute-done((bf16[2048,128]{1,0:T(8,128)(2,1)S(1)}, bf16[2048,128]{1,0:T(8,128)(2,1)S(1)}, u32[]{:S(2)}, u32[]{:S(2)}) %collective-permute-start.2) | collective-permute-done | bytes 524320 | tf_op jit(solution)/shard_map/ppermute | solution.py:347
  128.2 16.6 %project_attend.1 = (bf16[2048,768]{1,0:T(8,128)(2,1)S(1)}, bf16[2,512,256]{2,1,0:T(8,128)(2,1)S(1)}, bf16[2,512,512]{2,1,0:T(8,128)(2,1)S(1)}) custom-call(s32[2]{0:T(128)S(1)} %pad_add_fusion.meta_ref, bf16[2048,128]{1,0:T(8,128)(2,1)S(1)} %unpermute.2.s0, bf16[2048,128]{1,0:T(8,128)(2,1)S(1)} %collective-permute-done.s1, ...), custom_call_target="tpu_custom_call" | custom-call | tf_op jit(solution)/shard_map/project_attend/pallas_call | solution.py:281
  144.9 11.6 %attend.1 = bf16[2,512,256]{2,1,0:T(8,128)(2,1)S(1)} custom-call(s32[2]{0:T(128)S(1)} %pad_add_fusion.meta_ref, bf16[2048,768]{1,0:T(8,128)(2,1)S(1)} %get-tuple-element.12.qkv_ref), custom_call_target="tpu_custom_call" | custom-call | tf_op jit(solution)/shard_map/attend/pallas_call | solution.py:302
  157.7 7.6 %collective-permute-done.4.other_ref = bf16[512,256]{1,0:T(8,128)(2,1)S(1)} collective-permute-done((bf16[512,256]{1,0:T(8,128)(2,1)S(1)}, bf16[512,256]{1,0:T(8,128)(2,1)S(1)}, u32[]{:S(2)}, u32[]{:S(2)}) %collective-permute-start.4) | collective-permute-done | bytes 262176 | tf_op jit(solution)/shard_map/ppermute | solution.py:347
  165.4 5.8 %mlp.3 = bf16[512,512]{1,0:T(8,128)(2,1)} custom-call(s32[2]{0:T(128)S(1)} %pad_add_fusion.meta_ref, bf16[512,256]{1,0:T(8,128)(2,1)S(1)} %get-tuple-element.22.own_ref, bf16[512,256]{1,0:T(8,128)(2,1)S(1)} %collective-permute-done.4.other_ref, bf16[512,512]{1,0:T(8,128)(2,1)S(1)} %get-tuple-element.18.res_ref, bf16[2,256,512]{2,1,0:T(8,128)(2,1)S(1)} %bitcast.32, ...), custom_call_target="tpu_custom_call" | custom-call | tf_op jit(solution)/shard_map/mlp/pallas_call | solution.py:336
  171.1 8.4 %collective-permute-start.5 = (bf16[512,512]{1,0:T(8,128)(2,1)}, bf16[512,512]{1,0:T(8,128)(2,1)}, u32[]{:S(2)}, u32[]{:S(2)}) collective-permute-start(bf16[512,512]{1,0:T(8,128)(2,1)} %mlp.3), channel_id=1, source_target_pairs={{0,3},{3,0},{1,2},{2,1},{4,7},{7,4},{5,6},{6,5},{8,11},{11,8},{9,1... | collective-permute-start | bytes 1572872 | tf_op jit(solution)/shard_map/ppermute | solution.py:347
  179.5 6.7 %collective-permute-done.3.other_ref = bf16[512,256]{1,0:T(8,128)(2,1)} collective-permute-done((bf16[512,256]{1,0:T(8,128)(2,1)}, bf16[512,256]{1,0:T(8,128)(2,1)}, u32[]{:S(2)}, u32[]{:S(2)}) %collective-permute-start.3) | collective-permute-done | bytes 262176 | tf_op jit(solution)/shard_map/ppermute | solution.py:347
  186.2 2.2 %copy-done.1 = bf16[512,4096]{1,0:T(8,128)(2,1)S(1)} copy-done((bf16[512,4096]{1,0:T(8,128)(2,1)S(1)}, bf16[512,4096]{1,0:T(8,128)(2,1)}, u32[]{:S(2)}) %copy-start.1) | copy-done | bytes 4194328
  188.4 5.4 %mlp.2 = bf16[512,512]{1,0:T(8,128)(2,1)S(1)} custom-call(s32[2]{0:T(128)S(1)} %pad_add_fusion.meta_ref, bf16[512,256]{1,0:T(8,128)(2,1)S(1)} %get-tuple-element.21.own_ref, bf16[512,256]{1,0:T(8,128)(2,1)} %collective-permute-done.3.other_ref, bf16[512,512]{1,0:T(8,128)(2,1)S(1)} %get-tuple-element.17.res_ref, bf16[2,256,512]{2,1,0:T(8,128)(2,1)S(1)} %bitcast.33, ...), custom_call_target="tpu_custom_call" | custom-call | tf_op jit(solution)/shard_map/mlp/pallas_call | solution.py:336
  193.8 1.1 select_bitcast_fusion.1
  194.9 1.1 pad_maximum_fusion
  (33 shorter events, 3.4 us)
Async XLA Ops:
  27.6 2.2 %copy-start.4 = (bf16[16384,128]{1,0:T(8,128)(2,1)S(1)}, bf16[16384,128]{1,0:T(8,128)(2,1)}, u32[]{:S(2)}) copy-start(bf16[16384,128]{1,0:T(8,128)(2,1)} %table_ref.1) | copy-start | bytes 12582916
  44.4 1.5 copy-start.2
  46.0 44.6 %all-to-all-start.2 = ((bf16[32,344,128]{2,1,0:T(8,128)(2,1)}), bf16[32,344,128]{2,1,0:T(8,128)(2,1)S(1)}, u32[]{:S(2)}, u32[]{:S(2)}) async-start(bf16[32,344,128]{2,1,0:T(8,128)(2,1)} %copy-done.2), calls=%async_computation.2 | async-start | bytes 5636096 | tf_op jit(solution)/shard_map/all_to_all | solution.py:367
  90.5 19.9 %copy-start.9 = (s32[2]{0:T(128)S(1)}, s32[2]{0:T(128)}, u32[]{:S(2)}) copy-start(s32[2]{0:T(128)} %param.10) | copy-start | bytes 28
  90.5 37.7 %copy-start.6 = (bf16[512,1536]{1,0:T(8,128)(2,1)S(1)}, bf16[512,1536]{1,0:T(8,128)(2,1)}, u32[]{:S(2)}) copy-start(bf16[512,1536]{1,0:T(8,128)(2,1)} %w_ref.1) | copy-start | bytes 4718596
  90.5 37.7 %copy-start.8 = (f32[512]{0:T(512)S(1)}, f32[512]{0:T(512)}, u32[]{:S(2)}) copy-start(f32[512]{0:T(512)} %param.12) | copy-start | bytes 6148
  97.4 13.0 %collective-permute-start.1 = (bf16[2048,128]{1,0:T(8,128)(2,1)S(1)}, bf16[2048,128]{1,0:T(8,128)(2,1)S(1)}, u32[]{:S(2)}, u32[]{:S(2)}) collective-permute-start(bf16[2048,128]{1,0:T(8,128)(2,1)S(1)} %unpermute.3), channel_id=1, source_target_pairs={{0,3},{3,0},{1,2},{2,1},{4,7},{7,4},{5,6},{6,5},{8,11},{11,8},{9,1... | collective-permute-start | bytes 1572872 | tf_op jit(solution)/shard_map/ppermute | solution.py:347
  105.4 14.9 %collective-permute-start = (bf16[2048,128]{1,0:T(8,128)(2,1)S(1)}, bf16[2048,128]{1,0:T(8,128)(2,1)S(1)}, u32[]{:S(2)}, u32[]{:S(2)}) collective-permute-start(bf16[2048,128]{1,0:T(8,128)(2,1)S(1)} %unpermute.2.s0), channel_id=1, source_target_pairs={{0,1},{1,0},{2,3},{3,2},{4,5},{5,4},{6,7},{7,6},{8,9},{9,8},{10,11... | collective-permute-start | bytes 1572872 | tf_op jit(solution)/shard_map/ppermute | solution.py:347
  110.4 17.8 %collective-permute-start.2 = (bf16[2048,128]{1,0:T(8,128)(2,1)S(1)}, bf16[2048,128]{1,0:T(8,128)(2,1)S(1)}, u32[]{:S(2)}, u32[]{:S(2)}) collective-permute-start(bf16[2048,128]{1,0:T(8,128)(2,1)S(1)} %collective-permute-done.1.s2), channel_id=1, source_target_pairs={{0,1},{1,0},{2,3},{3,2},{4,5},{5,4},{6,7},{7,6},{8,9},{9,8},{10,11... | collective-permute-start | bytes 1572872 | tf_op jit(solution)/shard_map/ppermute | solution.py:347
  144.9 20.5 %copy-start.3 = (bf16[2048,512]{1,0:T(8,128)(2,1)S(1)}, bf16[2048,512]{1,0:T(8,128)(2,1)}, u32[]{:S(2)}) copy-start(bf16[2048,512]{1,0:T(8,128)(2,1)} %wd_ref.3) | copy-start | bytes 6291460
  144.9 20.5 %copy-start.5 = (bf16[512,512]{1,0:T(8,128)(2,1)S(1)}, bf16[512,512]{1,0:T(8,128)(2,1)}, u32[]{:S(2)}) copy-start(bf16[512,512]{1,0:T(8,128)(2,1)} %param.14) | copy-start | bytes 1572868
  156.4 8.9 %copy-start = (bf16[512,4096]{1,0:T(8,128)(2,1)S(1)}, bf16[512,4096]{1,0:T(8,128)(2,1)}, u32[]{:S(2)}) copy-start(bf16[512,4096]{1,0:T(8,128)(2,1)} %wi_ref.3) | copy-start | bytes 12582916
  156.4 8.9 %copy-start.7 = (f32[512]{0:T(512)S(1)}, f32[512]{0:T(512)}, u32[]{:S(2)}) copy-start(f32[512]{0:T(512)} %param.15) | copy-start | bytes 6148
  157.2 8.1 %collective-permute-start.4 = (bf16[512,256]{1,0:T(8,128)(2,1)S(1)}, bf16[512,256]{1,0:T(8,128)(2,1)S(1)}, u32[]{:S(2)}, u32[]{:S(2)}) collective-permute-start(bf16[512,256]{1,0:T(8,128)(2,1)S(1)} %get-tuple-element.20), channel_id=1, source_target_pairs={{0,1},{1,0},{2,3},{3,2},{4,5},{5,4},{6,7},{7,6},{8,9},{9,8},{10,11... | collective-permute-start | bytes 786440 | tf_op jit(solution)/shard_map/ppermute | solution.py:347
  171.1 22.7 %collective-permute-start.5 = (bf16[512,512]{1,0:T(8,128)(2,1)}, bf16[512,512]{1,0:T(8,128)(2,1)}, u32[]{:S(2)}, u32[]{:S(2)}) collective-permute-start(bf16[512,512]{1,0:T(8,128)(2,1)} %mlp.3), channel_id=1, source_target_pairs={{0,3},{3,0},{1,2},{2,1},{4,7},{7,4},{5,6},{6,5},{8,11},{11,8},{9,1... | collective-permute-start | bytes 1572872 | tf_op jit(solution)/shard_map/ppermute | solution.py:347
  179.5 6.7 %collective-permute-start.3 = (bf16[512,256]{1,0:T(8,128)(2,1)}, bf16[512,256]{1,0:T(8,128)(2,1)}, u32[]{:S(2)}, u32[]{:S(2)}) collective-permute-start(bf16[512,256]{1,0:T(8,128)(2,1)} %get-tuple-element.19), channel_id=1, source_target_pairs={{0,1},{1,0},{2,3},{3,2},{4,5},{5,4},{6,7},{7,6},{8,9},{9,8},{10,11... | collective-permute-start | bytes 786440 | tf_op jit(solution)/shard_map/ppermute | solution.py:347
  186.2 2.2 %copy-start.1 = (bf16[512,4096]{1,0:T(8,128)(2,1)S(1)}, bf16[512,4096]{1,0:T(8,128)(2,1)}, u32[]{:S(2)}) copy-start(bf16[512,4096]{1,0:T(8,128)(2,1)} %wi_ref.3) | copy-start | bytes 12582916

commit v2 on v1

v2 whole, which is shorter than its diff:
```python
import functools

import jax
import jax.numpy as jnp
from jax import lax
from jax.experimental import pallas as pl
from jax.experimental.pallas import tpu as pltpu
from jax.sharding import PartitionSpec as P

D = 512
FF = 2048
CAP = 344
REQ = 384
LOG2E = 1.4426950408889634
SWAP = [(0, 1), (1, 0), (2, 3), (3, 2)]
CROSS = [(0, 3), (3, 0), (1, 2), (2, 1)]
VM = pl.BlockSpec(memory_space=pltpu.VMEM)
SM = pl.BlockSpec(memory_space=pltpu.SMEM)
HB = pl.BlockSpec(memory_space=pl.ANY)
F32 = jnp.float32
BF = jnp.bfloat16
I32 = jnp.int32


def dot(a, b):
    return lax.dot_general(a, b, (((1,), (0,)), ((), ())), preferred_element_type=F32)


def dot_t(a, b):
    return lax.dot_general(a, b, (((1,), (1,)), ((), ())), preferred_element_type=F32)


def params(mib):
    return pltpu.CompilerParams(vmem_limit_bytes=mib * 1024 * 1024)


def route_kernel(row_bits, owners, ids_ref, slot_ref, req_ref):
    rows, width = ids_ref.shape
    parts = REQ // 128
    upper = (
        lax.broadcasted_iota(I32, (width, width), 0) < lax.broadcasted_iota(I32, (width, width), 1)
    ).astype(BF)
    owner_iota = lax.broadcasted_iota(I32, (owners, width), 0)
    group_iota = lax.broadcasted_iota(I32, (owners * parts, width), 0)
    lane_iota = lax.broadcasted_iota(I32, (128, width), 0)
    carry = jnp.zeros((owners, 1), F32)
    total = jnp.zeros((owners * parts, 256), F32)
    for r in range(rows):
        ids = ids_ref[r : r + 1, :]
        owner = lax.shift_right_logical(ids, row_bits)
        offset = ids & ((1 << row_bits) - 1)
        hot = (owner_iota == owner).astype(F32)
        before = dot(hot.astype(BF), upper) + carry
        rank = jnp.sum(hot * before, axis=0, keepdims=True).astype(I32)
        carry = carry + jnp.sum(hot, axis=1, keepdims=True)
        slot_ref[r : r + 1, :] = owner * CAP + rank
        group = owner * parts + lax.shift_right_logical(rank, 7)
        in_group = (group_iota == group).astype(BF)
        at_lane = lane_iota == (rank & 127)
        high = jnp.where(at_lane, lax.shift_right_logical(offset, 7), 0).astype(F32).astype(BF)
        low = jnp.where(at_lane, offset & 127, 0).astype(F32).astype(BF)
        total = total + dot_t(in_group, jnp.concatenate([high, low], axis=0))
    count = carry.astype(I32)
    last_group = (
        lax.broadcasted_iota(I32, (owners * parts, owners), 0)
        == lax.broadcasted_iota(I32, (owners * parts, owners), 1) * parts + parts - 1
    ).astype(BF)
    lane = lax.broadcasted_iota(I32, (owners, 256), 1)
    digits = jnp.where(
        lane == 127,
        lax.shift_right_logical(count, 7),
        jnp.where(lane == 255, count & 127, 0),
    )
    total = total + dot(last_group, digits.astype(F32).astype(BF))
    req_ref[...] = total[:, :128].astype(I32) * 128 + total[:, 128:].astype(I32)


def route(ids, row_bits, owners):
    return pl.pallas_call(
        functools.partial(route_kernel, row_bits, owners),
        out_shape=(
            jax.ShapeDtypeStruct(ids.shape, I32),
            jax.ShapeDtypeStruct((owners * (REQ // 128), 128), I32),
        ),
        in_specs=[VM],
        out_specs=(VM, VM),
        compiler_params=params(16),
        name="route",
    )(ids)


def lookup_kernel(asked_ref, table_ref, out_ref, part_ref, wide_ref, row_ref, send_ref, in_sem, out_sem):
    step = part_ref.shape[1]
    chunks = part_ref.shape[0]
    owners = out_ref.shape[0]

    def fetch(i):
        return pltpu.make_async_copy(
            table_ref.at[pl.ds(i * step, step)], part_ref.at[i], in_sem.at[i]
        )

    def store(d):
        return pltpu.make_async_copy(send_ref.at[d], out_ref.at[d], out_sem.at[d])

    for i in range(chunks):
        fetch(i).start()
    for i in range(chunks):
        fetch(i).wait()
        piece = 512

        def widen(j, _):
            at = pl.multiple_of(j * piece, piece)
            wide_ref[pl.ds(i * step + at, piece), :] = part_ref[i, pl.ds(at, piece), :].astype(F32)
            return 0

        lax.fori_loop(0, step // piece, widen, 0)

    def one(d, _):
        start = d * REQ
        count = asked_ref[start + REQ - 1]

        def some(i, _):
            base = pl.multiple_of(i * 8, 8)
            first = start + base
            for k in range(8):
                row_ref[pl.ds(base + k, 1), :] = wide_ref[pl.ds(asked_ref[first + k], 1), :]
            return 0

        lax.fori_loop(0, lax.shift_right_logical(count + 7, 3), some, 0)
        send_ref[d] = row_ref[...].astype(BF)
        store(d).start()
        return 0

    lax.fori_loop(0, owners, one, 0)

    def finish(d, _):
        store(d).wait()
        return 0

    lax.fori_loop(0, owners, finish, 0)


def lookup(asked, table, owners):
    rows, width = table.shape
    chunks = 8
    return pl.pallas_call(
        lookup_kernel,
        out_shape=jax.ShapeDtypeStruct((owners, CAP, width), BF),
        in_specs=[SM, HB],
        out_specs=HB,
        scratch_shapes=[
            pltpu.VMEM((chunks, rows // chunks, width), BF),
            pltpu.VMEM((rows, width), F32),
            pltpu.VMEM((CAP, width), F32),
            pltpu.VMEM((owners, CAP, width), BF),
            pltpu.SemaphoreType.DMA((chunks,)),
            pltpu.SemaphoreType.DMA((owners,)),
        ],
        compiler_params=params(24),
        name="lookup",
    )(asked, table)


def pick(slot_ref, start, wide_ref, row_ref, out_ref):
    block = row_ref.shape[0]

    def chunk(j, _):
        first = start + j * block

        def some(i, _):
            base = pl.multiple_of(i * 8, 8)
            at = first + base
            for k in range(8):
                row_ref[pl.ds(base + k, 1), :] = wide_ref[pl.ds(slot_ref[at + k], 1), :]
            return 0

        lax.fori_loop(0, block // 8, some, 0)
        out_ref[pl.ds(pl.multiple_of(j * block, block), block), :] = row_ref[...].astype(BF)
        return 0

    lax.fori_loop(0, out_ref.shape[0] // block, chunk, 0)


def pick_first_kernel(meta_ref, slot_ref, got_ref, out_ref, wide_ref, part_ref, row_ref, sem):
    chunks, step, _ = part_ref.shape

    def fetch(i):
        return pltpu.make_async_copy(got_ref.at[pl.ds(i * step, step)], part_ref.at[i], sem.at[i])

    for i in range(chunks):
        fetch(i).start()
    for i in range(chunks):
        fetch(i).wait()
        wide_ref[pl.ds(i * step, step), :] = part_ref[i].astype(F32)
    pick(slot_ref, meta_ref[2], wide_ref, row_ref, out_ref)


def pick_more_kernel(where, meta_ref, slot_ref, wide_ref, *refs):
    outs, row_ref = refs[:-1], refs[-1]
    for (of, late), out_ref in zip(where, outs):
        start = meta_ref[2 + of] + late * out_ref.shape[0]
        pick(slot_ref, start, wide_ref, row_ref, out_ref)


def pick_first(meta, slots, got, half):
    rows, width = got.shape
    chunks = 8
    return pl.pallas_call(
        pick_first_kernel,
        out_shape=(
            jax.ShapeDtypeStruct((half, width), BF),
            jax.ShapeDtypeStruct((rows, width), F32),
        ),
        in_specs=[SM, SM, HB],
        out_specs=(VM, VM),
        scratch_shapes=[
            pltpu.VMEM((chunks, rows // chunks, width), BF),
            pltpu.VMEM((512, width), F32),
            pltpu.SemaphoreType.DMA((chunks,)),
        ],
        compiler_params=params(16),
        name="pick_first",
    )(meta, slots, got)


def pick_more(meta, slots, wide, half, where):
    width = wide.shape[1]
    return pl.pallas_call(
        functools.partial(pick_more_kernel, where),
        out_shape=[jax.ShapeDtypeStruct((half, width), BF) for _ in where],
        in_specs=[SM, SM, VM],
        out_specs=[VM for _ in where],
        scratch_shapes=[pltpu.VMEM((512, width), F32)],
        compiler_params=params(16),
        name="pick_more",
    )(meta, slots, wide)


def project(c, slices, gain_ref, w_ref, norm_ref, k_ref, v_ref, res_ref, mine):
    n = norm_ref.shape[1]
    mate = lax.bitwise_xor(c, 1)
    order = (c, mate, 3 - c, 3 - mate)
    for b in range(2):
        rows = slice(b * n, b * n + n)
        wide = [ref[rows, :].astype(F32) for ref in slices]
        square = sum(x * x for x in wide)
        scale = lax.rsqrt(jnp.sum(square, axis=1, keepdims=True) * (1.0 / D) + 1e-06)
        normed = jnp.concatenate(
            [(x * scale * gain_ref[pl.ds(i, 1), :]).astype(BF) for x, i in zip(wide, order)],
            axis=1,
        )
        norm_ref[b] = normed
        keys = dot(normed, w_ref[:, D : 2 * D]).astype(BF)
        values = dot(normed, w_ref[:, 2 * D :]).astype(BF)
        for pair in range(4):
            k_ref[pair, rows, :] = keys[:, pair * 128 : pair * 128 + 128]
            v_ref[pair, rows, 0:128] = values[:, pair * 128 : pair * 128 + 128]
            v_ref[pair, rows, 128:256] = jnp.ones((n, 128), BF)
    own = pl.ds(pl.multiple_of(mine * n, n), n)
    for ref, i in zip(slices, order):
        res_ref[:, pl.ds(pl.multiple_of(i * 128, 128), 128)] = ref[own, :]
    return (dot(norm_ref[mine], w_ref[:, 0:D]) * (0.125 * LOG2E)).astype(BF)


def attend(quarter, length, q, q_ref, keys, values, s_ref, out_ref):
    size = s_ref.shape[2]
    for pair in range(4):
        q_ref[pair] = q[:, pair * 128 : pair * 128 + 128]
    subs = q_ref.shape[1] // size
    per_half = keys[0].shape[1] // size
    lane = lax.broadcasted_iota(I32, (size, 128), 1)
    row = lax.broadcasted_iota(I32, (size, size), 0)
    col = lax.broadcasted_iota(I32, (size, size), 1)

    def item(it, _):
        pair = lax.shift_right_logical(it, 1)
        sub = it & 1
        rows = pl.ds(pl.multiple_of(sub * size, size), size)
        block = quarter * subs + sub
        need = jnp.minimum(block + 1, lax.shift_right_logical(length + size - 1, 8))

        def body(n):
            qp = q_ref[pair, rows, :]
            limit = jnp.minimum(block * size + row + 1, length) - (n - 1) * size
            tops = []
            for head in range(2):
                qh = jnp.where((lane < 64) == (head == 0), qp, jnp.zeros_like(qp))
                m = None
                for j in range(n):
                    at = slice(j % per_half * size, j % per_half * size + size)
                    s = dot_t(qh, keys[j // per_half][pair, at, :])
                    if j == n - 1:
                        s = jnp.where(col < limit, s, -1e30)
                    s_ref[head, j] = s
                    t = jnp.maximum(s[:, 0:128], s[:, 128:256])
                    m = t if m is None else jnp.maximum(m, t)
                tops.append(jnp.max(m, axis=1, keepdims=True))
            outs = []
            for head in range(2):
                acc = None
                for j in range(n):
                    at = slice(j % per_half * size, j % per_half * size + size)
                    p = jnp.exp2(s_ref[head, j] - tops[head]).astype(BF)
                    d = dot(p, values[j // per_half][pair, at, :])
                    acc = d if acc is None else acc + d
                outs.append(acc[:, :128] / acc[:, 128:])
            out_ref[pair, rows, :] = jnp.where(lane < 64, outs[0], outs[1]).astype(BF)

        for n in range(1, s_ref.shape[1] + 1):
            pl.when(need == n)(functools.partial(body, n))
        return 0

    lax.fori_loop(0, 4 * subs, item, 0)


def early_kernel(
    meta_ref, s0, s1, s2, s3, gain_ref, w_ref,
    k_ref, v_ref, own_w_ref, att_ref, res_ref, norm_ref, q_ref, s_ref,
):
    c = meta_ref[0]
    mate = lax.bitwise_xor(c, 1)
    for at, i in enumerate((c, mate, 3 - c, 3 - mate)):
        own_w_ref[at * 128 : at * 128 + 128, :] = w_ref[pl.ds(pl.multiple_of(i * 128, 128), 128), :]
    quarter = jnp.minimum(c, 3 - c)
    q = project(c, (s0, s1, s2, s3), gain_ref, own_w_ref, norm_ref, k_ref, v_ref, res_ref, quarter)
    attend(quarter, meta_ref[1], q, q_ref, (k_ref,), (v_ref,), s_ref, att_ref)


def late_kernel(
    meta_ref, s0, s1, s2, s3, gain_ref, own_w_ref, k0_ref, v0_ref,
    att_ref, res_ref, norm_ref, q_ref, s_ref, k_ref, v_ref,
):
    c = meta_ref[0]
    quarter = jnp.maximum(c, 3 - c)
    q = project(
        c, (s0, s1, s2, s3), gain_ref, own_w_ref, norm_ref, k_ref, v_ref, res_ref, quarter - 2
    )
    attend(quarter, meta_ref[1], q, q_ref, (k0_ref, k_ref), (v0_ref, v_ref), s_ref, att_ref)


def attention_scratch(quarter, blocks):
    return [
        pltpu.VMEM((2, quarter, D), BF),
        pltpu.VMEM((4, quarter, 128), BF),
        pltpu.VMEM((2, blocks, 256, 256), F32),
    ]


def early(meta, slices, gain, w_qkv, quarter):
    half = 2 * quarter
    return pl.pallas_call(
        early_kernel,
        out_shape=(
            jax.ShapeDtypeStruct((4, half, 128), BF),
            jax.ShapeDtypeStruct((4, half, 256), BF),
            jax.ShapeDtypeStruct(w_qkv.shape, BF),
            jax.ShapeDtypeStruct((4, quarter, 128), BF),
            jax.ShapeDtypeStruct((quarter, D), BF),
        ),
        in_specs=[SM] + [VM] * 6,
        out_specs=(VM,) * 5,
        scratch_shapes=attention_scratch(quarter, half // 256),
        compiler_params=params(24),
        name="early",
    )(meta, *slices, gain, w_qkv)


def late(meta, slices, gain, own_w, keys, values, quarter):
    half = 2 * quarter
    return pl.pallas_call(
        late_kernel,
        out_shape=(
            jax.ShapeDtypeStruct((4, quarter, 128), BF),
            jax.ShapeDtypeStruct((quarter, D), BF),
        ),
        in_specs=[SM] + [VM] * 8,
        out_specs=(VM, VM),
        scratch_shapes=attention_scratch(quarter, 2 * half // 256)
        + [pltpu.VMEM((4, half, 128), BF), pltpu.VMEM((4, half, 256), BF)],
        compiler_params=params(24),
        name="late",
    )(meta, *slices, gain, own_w, keys, values)


def mlp_kernel(start, att_ref, res_ref, wo_ref, gain_ref, wi_ref, wd_ref, out_ref):
    rows = slice(start, start + out_ref.shape[0])
    attended = jnp.concatenate([att_ref[pair, rows, :] for pair in range(4)], axis=1)
    hidden = (res_ref[rows, :].astype(F32) + dot(attended, wo_ref[...])).astype(BF)
    hidden = hidden.astype(F32)
    scale = lax.rsqrt(jnp.mean(hidden * hidden, axis=1, keepdims=True) + 1e-06)
    normed = (hidden * scale * gain_ref[...]).astype(BF)
    acc = hidden
    step = 512
    for k in range(FF // step):
        gate = dot(normed, wi_ref[:, k * step : k * step + step])
        up = dot(normed, wi_ref[:, FF + k * step : FF + k * step + step])
        half = 0.5 * gate
        act = ((half + half * jnp.tanh(half)) * up).astype(BF)
        acc = acc + dot(act, wd_ref[k * step : k * step + step, :])
    out_ref[...] = acc.astype(BF)


def mlp(att, res, weights, start, count):
    return pl.pallas_call(
        functools.partial(mlp_kernel, start),
        out_shape=jax.ShapeDtypeStruct((count, D), BF),
        in_specs=[VM] * 6,
        out_specs=VM,
        compiler_params=params(20),
        name="mlp",
    )(att, res, *weights)


def exchange(x, pairs):
    return lax.ppermute(x, "cols", pairs)


def local(token_ids, lengths, table, attn_gain, w_qkv, w_out, mlp_gain, w_in, w_down):
    batch_dev, quarter = token_ids.shape
    owners = lax.axis_size("rows")
    col_count = lax.axis_size("cols")
    half = 2 * quarter
    length = col_count * quarter
    c = lax.axis_index("cols")
    h = c // 2
    row_bits = (table.shape[0] - 1).bit_length()
    meta = jnp.stack([c, jnp.where(h == 0, lengths[0], lengths[1]), (1 - h) * length, h * length])
    meta = meta.astype(I32)

    copies = jnp.broadcast_to(token_ids, (col_count, *token_ids.shape))
    ids = lax.all_to_all(copies, "cols", split_axis=0, concat_axis=0, tiled=True)
    ids = jnp.transpose(ids, (1, 0, 2)).reshape(batch_dev * col_count, quarter)
    slots, requests = route(ids, row_bits, owners)
    asked = lax.all_to_all(
        requests.reshape(owners, REQ), "rows", split_axis=0, concat_axis=0, tiled=True
    )
    looked = lookup(asked.reshape(-1), table, owners)
    got = lax.all_to_all(looked, "rows", split_axis=0, concat_axis=0, tiled=True)
    got = got.reshape(owners * CAP, table.shape[1])
    slots = slots.reshape(-1)

    theirs_0, wide = pick_first(meta, slots, got, half)
    crossed_0 = exchange(theirs_0, CROSS)
    mine_0, theirs_1 = pick_more(meta, slots, wide, half, ((1, 0), (0, 1)))
    swapped_0 = exchange(mine_0, SWAP)
    crossed_1 = exchange(theirs_1, CROSS)
    (mine_1,) = pick_more(meta, slots, wide, half, ((1, 1),))
    relayed_0 = exchange(crossed_0, SWAP)
    swapped_1 = exchange(mine_1, SWAP)
    relayed_1 = exchange(crossed_1, SWAP)

    gain = attn_gain.reshape(col_count, -1)
    keys, values, own_w, att_0, res_0 = early(
        meta, (mine_0, swapped_0, crossed_0, relayed_0), gain, w_qkv, quarter
    )
    weights = (w_out, mlp_gain.reshape(1, -1), w_in, w_down)
    out_0 = mlp(att_0, res_0, weights, 0, quarter)
    came_0 = exchange(out_0, [(2, 1), (3, 0)])
    att_1, res_1 = late(
        meta, (mine_1, swapped_1, crossed_1, relayed_1), gain, own_w, keys, values, quarter
    )
    out_1a = mlp(att_1, res_1, weights, 0, quarter // 2)
    came_1a = exchange(out_1a, [(0, 3), (1, 2)])
    out_1b = mlp(att_1, res_1, weights, quarter // 2, quarter // 2)
    came_1b = exchange(out_1b, [(0, 3), (1, 2)])
    first = h == 0
    halves = []
    for at, own_1, came_1 in ((0, out_1a, came_1a), (quarter // 2, out_1b, came_1b)):
        rows = slice(at, at + quarter // 2)
        own = jnp.where(first, out_0[rows], own_1)
        came = jnp.where(first, came_0[rows], came_1)
        which = lax.broadcasted_iota(I32, (batch_dev, quarter // 2, D), 0)
        halves.append(jnp.where(which == h, own[None], came[None]))
    return jnp.concatenate(halves, axis=1)


def solution(mesh):
    in_specs = (P("rows", "cols"), P("rows"), P("rows", "cols"), P(), P(), P(), P(), P(), P())
    out_specs = P("rows", "cols", None)
    return jax.shard_map(local, mesh=mesh, in_specs=in_specs, out_specs=out_specs, check_vma=False)
```

time: 197 us -> 152 us (0.77)
  waiting for transfers between devices: 74 us -> 52.4 us
  Pallas kernels: 69.3 us -> 51.5 us
  local copies, waits for them, and re-layouts: 8.12 us -> 3.52 us
    ppermute x6 -> x9, waiting for transfers between devices: 35.7 us -> 15.9 us  [exchange(): return lax.ppermute(x, 'cols', pairs)]
    pallas_call x6 -> x8, Pallas kernels: 53 us -> 40.4 us  [the longest x1 13.8 us: late(): pl.pallas_call(late_kernel, out_shape=(jax.ShapeDtypeStruct((4, quarter,...]
    pallas_call x1, Pallas kernels: 14.6 us -> 9.4 us  [lookup(): pl.pallas_call(lookup_kernel, out_shape=jax.ShapeDtypeStruct((owners, CAP...]
    unnamed x21 -> x17, local copies, waits for them, and re-layouts: 5.95 us -> 2.23 us
    another operation x3 -> x1, other arithmetic: 2.88 us -> 0.08 us  [local(): jnp.stack([c, jnp.where(h == 0, lengths[0], lengths[1]), (1 - h) * length...]
    ppermute x6 -> x9, starting transfers between devices: 10.1 us -> 10.3 us  [exchange(): return lax.ppermute(x, 'cols', pairs)]
  transfers between devices with their start and end apart: 7 -> 10, of which waited for: 6 -> 6; matrix products, arithmetic and copies ran while one was open for 1% -> 0% of each run, Pallas kernels for 6% -> 24%
where the time goes in v2:
time: 152 us; the launch traced here: 150 us
  waiting for transfers between devices  52.4 us (34%)
  Pallas kernels  51.5 us (34%)
  blocking collectives  25.1 us (17%)
  starting transfers between devices  14.6 us (10%)
  local copies, waits for them, and re-layouts  3.52 us (2%)
    all_to_all x1, waiting for transfers between devices, local(): lax.all_to_all(looked, 'rows', split_axis=0, concat_axis=0, tiled=True)  36.5 us
    ppermute x9, waiting for transfers between devices, exchange(): return lax.ppermute(x, 'cols', pairs)  15.9 us
    all_to_all x1, blocking collectives, local(): lax.all_to_all(requests.reshape(owners, REQ), 'rows', split_axis=0, conca...  14.6 us
    pallas_call x1, Pallas kernels, late(): pl.pallas_call(late_kernel, out_shape=(jax.ShapeDtypeStruct((4, quarter,...  13.8 us
    all_to_all x1, blocking collectives, local(): lax.all_to_all(copies, 'cols', split_axis=0, concat_axis=0, tiled=True)  10.6 us
    ppermute x9, starting transfers between devices, exchange(): return lax.ppermute(x, 'cols', pairs)  10.3 us
    pallas_call x3, Pallas kernels, mlp(): pl.pallas_call(functools.partial(mlp_kernel, start), out_shape=jax.ShapeD...  9.7 us
    pallas_call x1, Pallas kernels, lookup(): pl.pallas_call(lookup_kernel, out_shape=jax.ShapeDtypeStruct((owners, CAP...  9.4 us
  transfers between devices with their start and end apart: 10, of which 6 were waited for; matrix products, arithmetic and copies ran while one was open for 0% of the time, Pallas kernels for 24%

profile of v2, /device:TPU:0, one launch (start us, length us, event | category | flops | bytes accessed | tf_op | source)
XLA Modules:
  0.0 150.1 jit_solution(11252606966665373556)
XLA Ops:
  0.7 10.6 %all_to_all.19 = s32[4,2,512]{2,1,0:T(2,128)S(1)} all-to-all(s32[4,2,512]{2,1,0:T(2,128)S(1)} %broadcast_in_dim.33), channel_id=1, replica_groups=mesh['rows'=32,'cols'=4] {'cols'}, dimensions={0} | all-to-all | bytes 32768 | tf_op jit(solution)/shard_map/all_to_all | solution.py:431
  11.3 1.7 %route.1 = (s32[8,512]{1,0:T(8,128)S(1)}, s32[96,128]{1,0:T(8,128)S(1)}) custom-call(s32[8,512]{1,0:T(8,128)S(1)} %reshape.27.ids_ref), custom_call_target="tpu_custom_call" | custom-call | tf_op jit(solution)/shard_map/route/pallas_call | solution.py:79
  13.0 14.6 %all_to_all.20 = s32[32,1,384]{2,1,0:T(1,128)S(1)} all-to-all(s32[32,1,384]{2,1,0:T(1,128)S(1)} %bitcast.19), channel_id=1, replica_groups=mesh['rows'=32,'cols'=4] {'rows'}, dimensions={0} | all-to-all | bytes 98304 | tf_op jit(solution)/shard_map/all_to_all | solution.py:434
  27.6 2.2 %copy-done.3 = bf16[16384,128]{1,0:T(8,128)(2,1)S(1)} copy-done((bf16[16384,128]{1,0:T(8,128)(2,1)S(1)}, bf16[16384,128]{1,0:T(8,128)(2,1)}, u32[]{:S(2)}) %copy-start.3) | copy-done | bytes 4194328
  29.8 9.4 %lookup.1 = bf16[32,344,128]{2,1,0:T(8,128)(2,1)} custom-call(s32[12288]{0:T(1024)S(1)} %bitcast.18, bf16[16384,128]{1,0:T(8,128)(2,1)S(1)} %copy-done.3), custom_call_target="tpu_custom_call" | custom-call | tf_op jit(solution)/shard_map/lookup/pallas_call | solution.py:146
  39.2 4.3 %all-to-all-start.2 = ((bf16[32,344,128]{2,1,0:T(8,128)(2,1)}), bf16[32,344,128]{2,1,0:T(8,128)(2,1)S(1)}, u32[]{:S(2)}, u32[]{:S(2)}) async-start(bf16[32,344,128]{2,1,0:T(8,128)(2,1)} %lookup.1), calls=%async_computation.2 | async-start | bytes 5636096 | tf_op jit(solution)/shard_map/all_to_all | solution.py:438
  45.4 36.5 %all-to-all-done.2 = bf16[32,344,128]{2,1,0:T(8,128)(2,1)S(1)} async-done(((bf16[32,344,128]{2,1,0:T(8,128)(2,1)}), bf16[32,344,128]{2,1,0:T(8,128)(2,1)S(1)}, u32[]{:S(2)}, u32[]{:S(2)}) %all-to-all-start.2) | async-done | bytes 2818080 | tf_op jit(solution)/shard_map/all_to_all | solution.py:438
  81.9 3.8 %pick_first.1 = (bf16[1024,128]{1,0:T(8,128)(2,1)S(1)}, f32[11008,128]{1,0:T(8,128)S(1)}) custom-call(s32[4]{0:T(128)S(1)} %pad_add_fusion.meta_ref, s32[4096]{0:T(1024)S(1)} %bitcast.15, bf16[11008,128]{1,0:T(8,128)(2,1)S(1)} %bitcast.14), custom_call_target="tpu_custom_call" | custom-call | tf_op jit(solution)/shard_map/pick_first/pallas_call | solution.py:208
  86.9 3.7 %pick_more.2 = (bf16[1024,128]{1,0:T(8,128)(2,1)S(1)}, bf16[1024,128]{1,0:T(8,128)(2,1)S(1)}) custom-call(s32[4]{0:T(128)S(1)} %pad_add_fusion.meta_ref, s32[4096]{0:T(1024)S(1)} %bitcast.16, f32[11008,128]{1,0:T(8,128)S(1)} %get-tuple-element.20.wide_ref), custom_call_target="tpu_custom_call" | custom-call | tf_op jit(solution)/shard_map/pick_more/pallas_call | solution.py:228
  90.6 2.1 %collective-permute-start.4 = (bf16[1024,128]{1,0:T(8,128)(2,1)S(1)}, bf16[1024,128]{1,0:T(8,128)(2,1)S(1)}, u32[]{:S(2)}, u32[]{:S(2)}) collective-permute-start(bf16[1024,128]{1,0:T(8,128)(2,1)S(1)} %get-tuple-element.25), channel_id=1, source_target_pairs={{0,3},{3,0},{1,2},{2,1},{4,7},{7,4},{5,6},{6,5},{8,11},{11,8},{9,1... | collective-permute-start | bytes 786440 | tf_op jit(solution)/shard_map/ppermute | solution.py:415
  92.8 1.8 %collective-permute-done.1.s2 = bf16[1024,128]{1,0:T(8,128)(2,1)S(1)} collective-permute-done((bf16[1024,128]{1,0:T(8,128)(2,1)S(1)}, bf16[1024,128]{1,0:T(8,128)(2,1)S(1)}, u32[]{:S(2)}, u32[]{:S(2)}) %collective-permute-start.1) | collective-permute-done | bytes 262176 | tf_op jit(solution)/shard_map/ppermute | solution.py:415
  94.8 2.3 %pick_more.3.s0 = bf16[1024,128]{1,0:T(8,128)(2,1)S(1)} custom-call(s32[4]{0:T(128)S(1)} %pad_add_fusion.meta_ref, s32[4096]{0:T(1024)S(1)} %bitcast.17, f32[11008,128]{1,0:T(8,128)S(1)} %get-tuple-element.20.wide_ref), custom_call_target="tpu_custom_call" | custom-call | tf_op jit(solution)/shard_map/pick_more/pallas_call | solution.py:228
  97.1 1.8 %collective-permute-start.3 = (bf16[1024,128]{1,0:T(8,128)(2,1)S(1)}, bf16[1024,128]{1,0:T(8,128)(2,1)S(1)}, u32[]{:S(2)}, u32[]{:S(2)}) collective-permute-start(bf16[1024,128]{1,0:T(8,128)(2,1)S(1)} %pick_more.3.s0), channel_id=1, source_target_pairs={{0,1},{1,0},{2,3},{3,2},{4,5},{5,4},{6,7},{7,6},{8,9},{9,8},{10,11... | collective-permute-start | bytes 786440 | tf_op jit(solution)/shard_map/ppermute | solution.py:415
  99.2 2.7 %collective-permute-done.s1 = bf16[1024,128]{1,0:T(8,128)(2,1)S(1)} collective-permute-done((bf16[1024,128]{1,0:T(8,128)(2,1)S(1)}, bf16[1024,128]{1,0:T(8,128)(2,1)S(1)}, u32[]{:S(2)}, u32[]{:S(2)}) %collective-permute-start) | collective-permute-done | bytes 262176 | tf_op jit(solution)/shard_map/ppermute | solution.py:415
  102.0 5.6 %collective-permute-done.2.s3 = bf16[1024,128]{1,0:T(8,128)(2,1)S(1)} collective-permute-done((bf16[1024,128]{1,0:T(8,128)(2,1)S(1)}, bf16[1024,128]{1,0:T(8,128)(2,1)S(1)}, u32[]{:S(2)}, u32[]{:S(2)}) %collective-permute-start.2) | collective-permute-done | bytes 262176 | tf_op jit(solution)/shard_map/ppermute | solution.py:415
  107.6 7.2 %early.1 = (bf16[4,1024,128]{2,1,0:T(8,128)(2,1)S(1)}, bf16[4,1024,256]{2,1,0:T(8,128)(2,1)S(1)}, bf16[512,1536]{1,0:T(8,128)(2,1)S(1)}, bf16[4,512,128]{2,1,0:T(8,128)(2,1)S(1)}, bf16[512,512]{1,0:T(8,128)(2,1)S(1)}) custom-call(s32[4]{0:T(128)S(1)} %pad_add_fusion.meta_ref, bf16[1024,128]{1,0:T(8,128)(2,1)S(1)} %get-tuple-element.21.s0, ...), custom_call_target="tpu_custom_call" | custom-call | tf_op jit(solution)/shard_map/early/pallas_call | solution.py:351
  114.8 4.4 %mlp.3 = bf16[512,512]{1,0:T(8,128)(2,1)S(1)} custom-call(bf16[4,512,128]{2,1,0:T(8,128)(2,1)S(1)} %get-tuple-element.23.att_ref, bf16[512,512]{1,0:T(8,128)(2,1)S(1)} %get-tuple-element.24.res_ref, bf16[512,512]{1,0:T(8,128)(2,1)S(1)} %copy-done.2, f32[1,512]{1,0:T(1,128)S(1)} %bitcast.20, bf16[512,4096]{1,0:T(8,128)(2,1)S(1)} %copy-done, ...), custom_call_target="tpu_custom_call" | custom-call | tf_op jit(solution)/shard_map/mlp/pallas_call | solution.py:404
  119.3 1.5 %collective-permute-start.6 = (bf16[512,512]{1,0:T(8,128)(2,1)S(1)}, bf16[512,512]{1,0:T(8,128)(2,1)S(1)}, u32[]{:S(2)}, u32[]{:S(2)}) collective-permute-start(bf16[512,512]{1,0:T(8,128)(2,1)S(1)} %mlp.3), channel_id=1, source_target_pairs={{2,1},{3,0},{6,5},{7,4},{10,9},{11,8},{14,13},{15,12},{18,17},{19,... | collective-permute-start | bytes 1572872 | tf_op jit(solution)/shard_map/ppermute | solution.py:415
  120.8 13.8 %late.1 = (bf16[4,512,128]{2,1,0:T(8,128)(2,1)S(1)}, bf16[512,512]{1,0:T(8,128)(2,1)S(1)}) custom-call(s32[4]{0:T(128)S(1)} %pad_add_fusion.meta_ref, bf16[1024,128]{1,0:T(8,128)(2,1)S(1)} %pick_more.3.s0, bf16[1024,128]{1,0:T(8,128)(2,1)S(1)} %collective-permute-done.3.s1, bf16[1024,128]{1,0:T(8,128)(2,1)S(1)} %collective-permute-done.4.s2, ...), custom_call_target="tpu_custom_call" | custom-call | tf_op jit(solution)/shard_map/late/pallas_call | solution.py:370
  134.6 2.6 %mlp.5 = bf16[256,512]{1,0:T(8,128)(2,1)S(1)} custom-call(bf16[4,512,128]{2,1,0:T(8,128)(2,1)S(1)} %get-tuple-element.29.att_ref, bf16[512,512]{1,0:T(8,128)(2,1)S(1)} %get-tuple-element.30.res_ref, bf16[512,512]{1,0:T(8,128)(2,1)S(1)} %copy-done.2, f32[1,512]{1,0:T(1,128)S(1)} %bitcast.21, bf16[512,4096]{1,0:T(8,128)(2,1)S(1)} %copy-done, ...), custom_call_target="tpu_custom_call" | custom-call | tf_op jit(solution)/shard_map/mlp/pallas_call | solution.py:404
  137.3 2.6 %mlp.4 = bf16[256,512]{1,0:T(8,128)(2,1)S(1)} custom-call(bf16[4,512,128]{2,1,0:T(8,128)(2,1)S(1)} %get-tuple-element.29.att_ref, bf16[512,512]{1,0:T(8,128)(2,1)S(1)} %get-tuple-element.30.res_ref, bf16[512,512]{1,0:T(8,128)(2,1)S(1)} %copy-done.2, f32[1,512]{1,0:T(1,128)S(1)} %bitcast.22, bf16[512,4096]{1,0:T(8,128)(2,1)S(1)} %copy-done, ...), custom_call_target="tpu_custom_call" | custom-call | tf_op jit(solution)/shard_map/mlp/pallas_call | solution.py:404
  139.9 1.7 %collective-permute-start.7 = (bf16[256,512]{1,0:T(8,128)(2,1)S(1)}, bf16[256,512]{1,0:T(8,128)(2,1)S(1)}, u32[]{:S(2)}, u32[]{:S(2)}) collective-permute-start(bf16[256,512]{1,0:T(8,128)(2,1)S(1)} %mlp.4), channel_id=1, source_target_pairs={{0,3},{1,2},{4,7},{5,6},{8,11},{9,10},{12,15},{13,14},{16,19},{17,... | collective-permute-start | bytes 786440 | tf_op jit(solution)/shard_map/ppermute | solution.py:415
  143.0 3.0 %collective-permute-done.7 = bf16[256,512]{1,0:T(8,128)(2,1)S(1)} collective-permute-done((bf16[256,512]{1,0:T(8,128)(2,1)S(1)}, bf16[256,512]{1,0:T(8,128)(2,1)S(1)}, u32[]{:S(2)}, u32[]{:S(2)}) %collective-permute-start.7) | collective-permute-done | bytes 262176 | tf_op jit(solution)/shard_map/ppermute | solution.py:415
  146.0 2.8 %collective-permute-done.8 = bf16[256,512]{1,0:T(8,128)(2,1)S(1)} collective-permute-done((bf16[256,512]{1,0:T(8,128)(2,1)S(1)}, bf16[256,512]{1,0:T(8,128)(2,1)S(1)}, u32[]{:S(2)}, u32[]{:S(2)}) %collective-permute-start.8) | collective-permute-done | bytes 262176 | tf_op jit(solution)/shard_map/ppermute | solution.py:415
  (35 shorter events, 5.9 us)
Async XLA Ops:
  27.6 2.2 %copy-start.3 = (bf16[16384,128]{1,0:T(8,128)(2,1)S(1)}, bf16[16384,128]{1,0:T(8,128)(2,1)}, u32[]{:S(2)}) copy-start(bf16[16384,128]{1,0:T(8,128)(2,1)} %table_ref.1) | copy-start | bytes 12582916
  39.2 4.4 %copy-start.7 = (s32[2]{0:T(128)S(1)}, s32[2]{0:T(128)}, u32[]{:S(2)}) copy-start(s32[2]{0:T(128)} %param.10) | copy-start | bytes 28
  39.2 42.7 %all-to-all-start.2 = ((bf16[32,344,128]{2,1,0:T(8,128)(2,1)}), bf16[32,344,128]{2,1,0:T(8,128)(2,1)S(1)}, u32[]{:S(2)}, u32[]{:S(2)}) async-start(bf16[32,344,128]{2,1,0:T(8,128)(2,1)} %lookup.1), calls=%async_computation.2 | async-start | bytes 5636096 | tf_op jit(solution)/shard_map/all_to_all | solution.py:438
  85.7 8.9 %collective-permute-start.1 = (bf16[1024,128]{1,0:T(8,128)(2,1)S(1)}, bf16[1024,128]{1,0:T(8,128)(2,1)S(1)}, u32[]{:S(2)}, u32[]{:S(2)}) collective-permute-start(bf16[1024,128]{1,0:T(8,128)(2,1)S(1)} %get-tuple-element.22), channel_id=1, source_target_pairs={{0,3},{3,0},{1,2},{2,1},{4,7},{7,4},{5,6},{6,5},{8,11},{11,8},{9,1... | collective-permute-start | bytes 786440 | tf_op jit(solution)/shard_map/ppermute | solution.py:415
  90.6 8.3 %collective-permute-start.4 = (bf16[1024,128]{1,0:T(8,128)(2,1)S(1)}, bf16[1024,128]{1,0:T(8,128)(2,1)S(1)}, u32[]{:S(2)}, u32[]{:S(2)}) collective-permute-start(bf16[1024,128]{1,0:T(8,128)(2,1)S(1)} %get-tuple-element.25), channel_id=1, source_target_pairs={{0,3},{3,0},{1,2},{2,1},{4,7},{7,4},{5,6},{6,5},{8,11},{11,8},{9,1... | collective-permute-start | bytes 786440 | tf_op jit(solution)/shard_map/ppermute | solution.py:415
  92.8 14.8 %copy-start.4 = (bf16[512,1536]{1,0:T(8,128)(2,1)S(1)}, bf16[512,1536]{1,0:T(8,128)(2,1)}, u32[]{:S(2)}) copy-start(bf16[512,1536]{1,0:T(8,128)(2,1)} %w_ref.1) | copy-start | bytes 4718596
  92.8 14.8 %copy-start.6 = (f32[512]{0:T(512)S(1)}, f32[512]{0:T(512)}, u32[]{:S(2)}) copy-start(f32[512]{0:T(512)} %param.12) | copy-start | bytes 6148
  92.8 9.2 %collective-permute-start = (bf16[1024,128]{1,0:T(8,128)(2,1)S(1)}, bf16[1024,128]{1,0:T(8,128)(2,1)S(1)}, u32[]{:S(2)}, u32[]{:S(2)}) collective-permute-start(bf16[1024,128]{1,0:T(8,128)(2,1)S(1)} %get-tuple-element.21.s0), channel_id=1, source_target_pairs={{0,1},{1,0},{2,3},{3,2},{4,5},{5,4},{6,7},{7,6},{8,9},{9,8},{10,11... | collective-permute-start | bytes 786440 | tf_op jit(solution)/shard_map/ppermute | solution.py:415
  94.5 13.0 %collective-permute-start.2 = (bf16[1024,128]{1,0:T(8,128)(2,1)S(1)}, bf16[1024,128]{1,0:T(8,128)(2,1)S(1)}, u32[]{:S(2)}, u32[]{:S(2)}) collective-permute-start(bf16[1024,128]{1,0:T(8,128)(2,1)S(1)} %collective-permute-done.1.s2), channel_id=1, source_target_pairs={{0,1},{1,0},{2,3},{3,2},{4,5},{5,4},{6,7},{7,6},{8,9},{9,8},{10,11... | collective-permute-start | bytes 786440 | tf_op jit(solution)/shard_map/ppermute | solution.py:415
  94.8 20.0 %copy-start = (bf16[512,4096]{1,0:T(8,128)(2,1)S(1)}, bf16[512,4096]{1,0:T(8,128)(2,1)}, u32[]{:S(2)}) copy-start(bf16[512,4096]{1,0:T(8,128)(2,1)} %wi_ref.5) | copy-start | bytes 12582916
  97.1 17.7 %copy-start.1 = (bf16[2048,512]{1,0:T(8,128)(2,1)S(1)}, bf16[2048,512]{1,0:T(8,128)(2,1)}, u32[]{:S(2)}) copy-start(bf16[2048,512]{1,0:T(8,128)(2,1)} %wd_ref.5) | copy-start | bytes 6291460
  97.1 17.7 %copy-start.2 = (bf16[512,512]{1,0:T(8,128)(2,1)S(1)}, bf16[512,512]{1,0:T(8,128)(2,1)}, u32[]{:S(2)}) copy-start(bf16[512,512]{1,0:T(8,128)(2,1)} %wo_ref.5) | copy-start | bytes 1572868
  97.1 17.7 %copy-start.5 = (f32[512]{0:T(512)S(1)}, f32[512]{0:T(512)}, u32[]{:S(2)}) copy-start(f32[512]{0:T(512)} %param.15) | copy-start | bytes 6148
  97.1 23.7 %collective-permute-start.3 = (bf16[1024,128]{1,0:T(8,128)(2,1)S(1)}, bf16[1024,128]{1,0:T(8,128)(2,1)S(1)}, u32[]{:S(2)}, u32[]{:S(2)}) collective-permute-start(bf16[1024,128]{1,0:T(8,128)(2,1)S(1)} %pick_more.3.s0), channel_id=1, source_target_pairs={{0,1},{1,0},{2,3},{3,2},{4,5},{5,4},{6,7},{7,6},{8,9},{9,8},{10,11... | collective-permute-start | bytes 786440 | tf_op jit(solution)/shard_map/ppermute | solution.py:415
  99.0 21.9 %collective-permute-start.5 = (bf16[1024,128]{1,0:T(8,128)(2,1)S(1)}, bf16[1024,128]{1,0:T(8,128)(2,1)S(1)}, u32[]{:S(2)}, u32[]{:S(2)}) collective-permute-start(bf16[1024,128]{1,0:T(8,128)(2,1)S(1)} %collective-permute-done.4.s2), channel_id=1, source_target_pairs={{0,1},{1,0},{2,3},{3,2},{4,5},{5,4},{6,7},{7,6},{8,9},{9,8},{10,11... | collective-permute-start | bytes 786440 | tf_op jit(solution)/shard_map/ppermute | solution.py:415
  119.3 29.5 %collective-permute-start.6 = (bf16[512,512]{1,0:T(8,128)(2,1)S(1)}, bf16[512,512]{1,0:T(8,128)(2,1)S(1)}, u32[]{:S(2)}, u32[]{:S(2)}) collective-permute-start(bf16[512,512]{1,0:T(8,128)(2,1)S(1)} %mlp.3), channel_id=1, source_target_pairs={{2,1},{3,0},{6,5},{7,4},{10,9},{11,8},{14,13},{15,12},{18,17},{19,... | collective-permute-start | bytes 1572872 | tf_op jit(solution)/shard_map/ppermute | solution.py:415
  139.9 6.1 %collective-permute-start.7 = (bf16[256,512]{1,0:T(8,128)(2,1)S(1)}, bf16[256,512]{1,0:T(8,128)(2,1)S(1)}, u32[]{:S(2)}, u32[]{:S(2)}) collective-permute-start(bf16[256,512]{1,0:T(8,128)(2,1)S(1)} %mlp.4), channel_id=1, source_target_pairs={{0,3},{1,2},{4,7},{5,6},{8,11},{9,10},{12,15},{13,14},{16,19},{17,... | collective-permute-start | bytes 786440 | tf_op jit(solution)/shard_map/ppermute | solution.py:415
  141.6 7.2 %collective-permute-start.8 = (bf16[256,512]{1,0:T(8,128)(2,1)S(1)}, bf16[256,512]{1,0:T(8,128)(2,1)S(1)}, u32[]{:S(2)}, u32[]{:S(2)}) collective-permute-start(bf16[256,512]{1,0:T(8,128)(2,1)S(1)} %mlp.5), channel_id=1, source_target_pairs={{0,3},{1,2},{4,7},{5,6},{8,11},{9,10},{12,15},{13,14},{16,19},{17,... | collective-permute-start | bytes 786440 | tf_op jit(solution)/shard_map/ppermute | solution.py:415

commit v3 on v2

v3 whole, which is shorter than its diff:
```python
import functools

import jax
import jax.numpy as jnp
from jax import lax
from jax.experimental import pallas as pl
from jax.experimental.pallas import tpu as pltpu
from jax.sharding import PartitionSpec as P

D = 512
FF = 2048
CAP = 344
REQ = 384
LOG2E = 1.4426950408889634
SWAP = [(0, 1), (1, 0), (2, 3), (3, 2)]
CROSS = [(0, 3), (3, 0), (1, 2), (2, 1)]
VM = pl.BlockSpec(memory_space=pltpu.VMEM)
SM = pl.BlockSpec(memory_space=pltpu.SMEM)
AN = pl.BlockSpec(memory_space=pl.ANY)
F32 = jnp.float32
BF = jnp.bfloat16
I32 = jnp.int32


def dot(a, b):
    return lax.dot_general(a, b, (((1,), (0,)), ((), ())), preferred_element_type=F32)


def dot_t(a, b):
    return lax.dot_general(a, b, (((1,), (1,)), ((), ())), preferred_element_type=F32)


def cost(flops, moved=0):
    return pl.CostEstimate(flops=int(flops), bytes_accessed=int(moved), transcendentals=0)


def params(mib):
    return pltpu.CompilerParams(vmem_limit_bytes=mib * 1024 * 1024)


def route_kernel(row_bits, owners, ids_ref, slot_ref, req_ref):
    rows, width = ids_ref.shape
    parts = REQ // 128
    upper = (
        lax.broadcasted_iota(I32, (width, width), 0) < lax.broadcasted_iota(I32, (width, width), 1)
    ).astype(BF)
    owner_iota = lax.broadcasted_iota(I32, (owners, width), 0)
    group_iota = lax.broadcasted_iota(I32, (owners * parts, width), 0)
    lane_iota = lax.broadcasted_iota(I32, (128, width), 0)
    carry = jnp.zeros((owners, 1), F32)
    total = jnp.zeros((owners * parts, 256), F32)
    for r in range(rows):
        ids = ids_ref[r : r + 1, :]
        owner = lax.shift_right_logical(ids, row_bits)
        offset = ids & ((1 << row_bits) - 1)
        hot = (owner_iota == owner).astype(F32)
        before = dot(hot.astype(BF), upper) + carry
        rank = jnp.sum(hot * before, axis=0, keepdims=True).astype(I32)
        carry = carry + jnp.sum(hot, axis=1, keepdims=True)
        slot_ref[r : r + 1, :] = owner * CAP + rank
        place = rank + 1
        group = owner * parts + lax.shift_right_logical(place, 7)
        in_group = (group_iota == group).astype(BF)
        at_lane = lane_iota == (place & 127)
        high = jnp.where(at_lane, lax.shift_right_logical(offset, 7), 0).astype(F32).astype(BF)
        low = jnp.where(at_lane, offset & 127, 0).astype(F32).astype(BF)
        total = total + dot_t(in_group, jnp.concatenate([high, low], axis=0))
    count = carry.astype(I32)
    first_group = (
        lax.broadcasted_iota(I32, (owners * parts, owners), 0)
        == lax.broadcasted_iota(I32, (owners * parts, owners), 1) * parts
    ).astype(BF)
    lane = lax.broadcasted_iota(I32, (owners, 256), 1)
    digits = jnp.where(
        lane == 0,
        lax.shift_right_logical(count, 7),
        jnp.where(lane == 128, count & 127, 0),
    )
    total = total + dot(first_group, digits.astype(F32).astype(BF))
    req_ref[...] = total[:, :128].astype(I32) * 128 + total[:, 128:].astype(I32)


def route(ids, row_bits, owners):
    return pl.pallas_call(
        functools.partial(route_kernel, row_bits, owners),
        out_shape=(
            jax.ShapeDtypeStruct(ids.shape, I32),
            jax.ShapeDtypeStruct((owners * (REQ // 128), 128), I32),
        ),
        in_specs=[VM],
        out_specs=(VM, VM),
        compiler_params=params(16),
        name="route",
    )(ids)


def lookup_kernel(
    asked_ref, table_ref, out_ref,
    ask_ref, part_ref, wide_ref, row_ref, send_ref, ask_sem, in_sem, out_sem,
):
    owners = out_ref.shape[0]
    chunks, step, _ = part_ref.shape
    batches = 4
    batch = owners // batches

    def ask(i):
        at = pl.ds(i * batch * REQ, batch * REQ)
        return pltpu.make_async_copy(asked_ref.at[at], ask_ref.at[at], ask_sem.at[i])

    def fetch(i):
        return pltpu.make_async_copy(table_ref.at[pl.ds(i * step, step)], part_ref.at[i], in_sem.at[i])

    def store(d):
        return pltpu.make_async_copy(send_ref.at[d], out_ref.at[d], out_sem.at[d])

    for i in range(chunks):
        fetch(i).start()
    for i in range(batches):
        ask(i).start()
    piece = 512
    for i in range(chunks):
        fetch(i).wait()

        def widen(j, _):
            at = pl.multiple_of(j * piece, piece)
            wide_ref[pl.ds(i * step + at, piece), :] = part_ref[i, pl.ds(at, piece), :].astype(F32)
            return 0

        lax.fori_loop(0, step // piece, widen, 0)

    def one(d, _):
        start = d * REQ
        groups = lax.shift_right_logical(ask_ref[start] + 31, 5)

        def some(i, _):
            base = pl.multiple_of(i * 32, 32)
            first = start + base + 1
            for k in range(32):
                row_ref[pl.ds(base + k, 1), :] = wide_ref[pl.ds(ask_ref[first + k], 1), :]
            return 0

        lax.fori_loop(0, groups, some, 0)

        def narrow(i, _):
            at = pl.ds(pl.multiple_of(i * 32, 32), 32)
            send_ref[d, at, :] = row_ref[at, :].astype(BF)
            return 0

        lax.fori_loop(0, jnp.minimum(groups, CAP // 32), narrow, 0)

        @pl.when(groups > CAP // 32)
        def _():
            at = slice(CAP // 32 * 32, CAP)
            send_ref[d, at, :] = row_ref[at, :].astype(BF)

        store(d).start()
        return 0

    for i in range(batches):
        ask(i).wait()
        lax.fori_loop(i * batch, i * batch + batch, one, 0)

    def finish(d, _):
        store(d).wait()
        return 0

    lax.fori_loop(0, owners, finish, 0)


def lookup(asked, table, owners):
    rows, width = table.shape
    chunks = 8
    return pl.pallas_call(
        lookup_kernel,
        out_shape=jax.ShapeDtypeStruct((owners, CAP, width), BF),
        in_specs=[AN, AN],
        out_specs=AN,
        scratch_shapes=[
            pltpu.SMEM((owners * REQ,), I32),
            pltpu.VMEM((chunks, rows // chunks, width), BF),
            pltpu.VMEM((rows, width), F32),
            pltpu.VMEM((352, width), F32),
            pltpu.VMEM((owners, CAP, width), BF),
            pltpu.SemaphoreType.DMA((4,)),
            pltpu.SemaphoreType.DMA((chunks,)),
            pltpu.SemaphoreType.DMA((owners,)),
        ],
        compiler_params=params(62),
        cost_estimate=cost(6e9, 4e6),
        name="lookup",
    )(asked, table)


def slots_of(other, late, meta_ref, slot_ref, here_ref, sem):
    half = here_ref.shape[0]
    history = lax.shift_right_logical(meta_ref[0], 1)
    history = 1 - history if other else history
    start = pl.multiple_of((history * 2 + late) * half, half)
    return pltpu.make_async_copy(slot_ref.at[pl.ds(start, half)], here_ref, sem)


def pick(here_ref, wide_ref, row_ref, out_ref):
    block = row_ref.shape[0]
    for j in range(out_ref.shape[0] // block):

        def some(i, _):
            base = pl.multiple_of(i * 32, 32)
            at = j * block + base
            for k in range(32):
                row_ref[pl.ds(base + k, 1), :] = wide_ref[pl.ds(here_ref[at + k], 1), :]
            return 0

        lax.fori_loop(0, block // 32, some, 0)
        out_ref[j * block : j * block + block, :] = row_ref[...].astype(BF)


def pick_first_kernel(meta_ref, slot_ref, got_ref, out_ref, wide_ref, row_ref, here_ref, sem):
    step = 2 * CAP
    copy = slots_of(True, 0, meta_ref, slot_ref, here_ref, sem)
    copy.start()

    def widen(i, _):
        at = pl.ds(pl.multiple_of(i * step, step), step)
        wide_ref[at, :] = got_ref[at, :].astype(F32)
        return 0

    lax.fori_loop(0, wide_ref.shape[0] // step, widen, 0)
    copy.wait()
    pick(here_ref, wide_ref, row_ref, out_ref)


def pick_more_kernel(
    other, late, meta_ref, slot_ref, wide_ref, after_ref, out_ref, row_ref, here_ref, sem
):
    copy = slots_of(other, late, meta_ref, slot_ref, here_ref, sem)
    copy.start()
    copy.wait()
    pick(here_ref, wide_ref, row_ref, out_ref)


def pick_scratch(half, quarter, width):
    return [
        pltpu.VMEM((quarter, width), F32),
        pltpu.SMEM((half,), I32),
        pltpu.SemaphoreType.DMA,
    ]


def pick_first(meta, slots, got, half, quarter):
    rows, width = got.shape
    return pl.pallas_call(
        pick_first_kernel,
        out_shape=(
            jax.ShapeDtypeStruct((half, width), BF),
            jax.ShapeDtypeStruct((rows, width), F32),
        ),
        in_specs=[SM, AN, VM],
        out_specs=(VM, VM),
        scratch_shapes=pick_scratch(half, quarter, width),
        compiler_params=params(14),
        cost_estimate=cost(3e9, 4e6),
        name="pick_first",
    )(meta, slots, got)


def pick_more(meta, slots, wide, after, half, quarter, other, late):
    width = wide.shape[1]
    return pl.pallas_call(
        functools.partial(pick_more_kernel, other, late),
        out_shape=jax.ShapeDtypeStruct((half, width), BF),
        in_specs=[SM, AN, VM, AN],
        out_specs=VM,
        scratch_shapes=pick_scratch(half, quarter, width),
        compiler_params=params(14),
        cost_estimate=cost(2e9, 4e6),
        name="pick_more",
    )(meta, slots, wide, after)


def project(c, slices, gain_ref, w_ref, norm_ref, k_ref, v_ref, res_ref, mine):
    n = norm_ref.shape[1]
    mate = lax.bitwise_xor(c, 1)
    order = (c, mate, 3 - c, 3 - mate)
    for b in range(2):
        rows = slice(b * n, b * n + n)
        wide = [ref[rows, :].astype(F32) for ref in slices]
        square = sum(x * x for x in wide)
        scale = lax.rsqrt(jnp.sum(square, axis=1, keepdims=True) * (1.0 / D) + 1e-06)
        normed = jnp.concatenate(
            [(x * scale * gain_ref[pl.ds(i, 1), :]).astype(BF) for x, i in zip(wide, order)],
            axis=1,
        )
        norm_ref[b] = normed
        keys = dot(normed, w_ref[:, D : 2 * D]).astype(BF)
        values = dot(normed, w_ref[:, 2 * D :]).astype(BF)
        for pair in range(4):
            k_ref[pair, rows, :] = keys[:, pair * 128 : pair * 128 + 128]
            v_ref[pair, rows, 0:128] = values[:, pair * 128 : pair * 128 + 128]
            v_ref[pair, rows, 128:256] = jnp.ones((n, 128), BF)
    own = pl.ds(pl.multiple_of(mine * n, n), n)
    for ref, i in zip(slices, order):
        res_ref[:, pl.ds(pl.multiple_of(i * 128, 128), 128)] = ref[own, :]
    return (dot(norm_ref[mine], w_ref[:, 0:D]) * (0.125 * LOG2E)).astype(BF)


def keep_queries(q, q_ref):
    for pair in range(4):
        q_ref[pair] = q[:, pair * 128 : pair * 128 + 128]


def attend(quarter, length, q_ref, keys, values, s_ref, out_ref, skip=0):
    size = s_ref.shape[2]
    subs = q_ref.shape[1] // size
    todo = out_ref.shape[1] // size
    per_half = keys[0].shape[1] // size
    lane = lax.broadcasted_iota(I32, (size, 128), 1)
    row = lax.broadcasted_iota(I32, (size, size), 0)
    col = lax.broadcasted_iota(I32, (size, size), 1)

    def item(it, _):
        pair = it & 3
        at_sub = lax.shift_right_logical(it, 2)
        put = pl.ds(pl.multiple_of(at_sub * size, size), size)
        rows = pl.ds(pl.multiple_of((at_sub + skip) * size, size), size)
        block = quarter * subs + at_sub + skip
        need = jnp.minimum(block + 1, lax.shift_right_logical(length + size - 1, 8))

        def body(n):
            qp = q_ref[pair, rows, :]
            limit = jnp.minimum(block * size + row + 1, length) - (n - 1) * size
            tops = []
            for head in range(2):
                qh = jnp.where((lane < 64) == (head == 0), qp, jnp.zeros_like(qp))
                m = None
                for j in range(n):
                    at = slice(j % per_half * size, j % per_half * size + size)
                    s = dot_t(qh, keys[j // per_half][pair, at, :])
                    if j == n - 1:
                        s = jnp.where(col < limit, s, -1e30)
                    s_ref[head, j] = s
                    t = jnp.maximum(s[:, 0:128], s[:, 128:256])
                    m = t if m is None else jnp.maximum(m, t)
                tops.append(jnp.max(m, axis=1, keepdims=True))
            outs = []
            for head in range(2):
                acc = None
                for j in range(n):
                    at = slice(j % per_half * size, j % per_half * size + size)
                    p = jnp.exp2(s_ref[head, j] - tops[head]).astype(BF)
                    d = dot(p, values[j // per_half][pair, at, :])
                    acc = d if acc is None else acc + d
                outs.append(acc[:, :128] / acc[:, 128:])
            out_ref[pair, put, :] = jnp.where(lane < 64, outs[0], outs[1]).astype(BF)

        for n in range(1, s_ref.shape[1] + 1):
            pl.when(need == n)(functools.partial(body, n))
        return 0

    lax.fori_loop(0, 4 * todo, item, 0)


def early_kernel(
    meta_ref, s0, s1, s2, s3, gain_ref, w_ref,
    k_ref, v_ref, own_w_ref, att_ref, res_ref, norm_ref, q_ref, s_ref,
):
    c = meta_ref[0]
    mate = lax.bitwise_xor(c, 1)
    for at, i in enumerate((c, mate, 3 - c, 3 - mate)):
        own_w_ref[at * 128 : at * 128 + 128, :] = w_ref[pl.ds(pl.multiple_of(i * 128, 128), 128), :]
    quarter = jnp.minimum(c, 3 - c)
    q = project(c, (s0, s1, s2, s3), gain_ref, own_w_ref, norm_ref, k_ref, v_ref, res_ref, quarter)
    keep_queries(q, q_ref)
    attend(quarter, meta_ref[1], q_ref, (k_ref,), (v_ref,), s_ref, att_ref)


def late_kernel(
    meta_ref, s0, s1, s2, s3, gain_ref, own_w_ref, k0_ref, v0_ref,
    k_ref, v_ref, q_ref, att_ref, res_ref, norm_ref, s_ref,
):
    c = meta_ref[0]
    quarter = jnp.maximum(c, 3 - c)
    q = project(
        c, (s0, s1, s2, s3), gain_ref, own_w_ref, norm_ref, k_ref, v_ref, res_ref, quarter - 2
    )
    keep_queries(q, q_ref)
    attend(quarter, meta_ref[1], q_ref, (k0_ref, k_ref), (v0_ref, v_ref), s_ref, att_ref)


def last_kernel(meta_ref, q_ref, k0_ref, v0_ref, k_ref, v_ref, after_ref, att_ref, s_ref):
    c = meta_ref[0]
    quarter = jnp.maximum(c, 3 - c)
    attend(quarter, meta_ref[1], q_ref, (k0_ref, k_ref), (v0_ref, v_ref), s_ref, att_ref, 1)


def early(meta, slices, gain, w_qkv, quarter):
    half = 2 * quarter
    return pl.pallas_call(
        early_kernel,
        out_shape=(
            jax.ShapeDtypeStruct((4, half, 128), BF),
            jax.ShapeDtypeStruct((4, half, 256), BF),
            jax.ShapeDtypeStruct(w_qkv.shape, BF),
            jax.ShapeDtypeStruct((4, quarter, 128), BF),
            jax.ShapeDtypeStruct((quarter, D), BF),
        ),
        in_specs=[SM] + [VM] * 6,
        out_specs=(VM,) * 5,
        scratch_shapes=[
            pltpu.VMEM((2, quarter, D), BF),
            pltpu.VMEM((4, quarter, 128), BF),
            pltpu.VMEM((2, half // 256, 256, 256), F32),
        ],
        compiler_params=params(20),
        cost_estimate=cost(7e9, 6e6),
        name="early",
    )(meta, *slices, gain, w_qkv)


def late(meta, slices, gain, own_w, keys, values, quarter):
    half = 2 * quarter
    return pl.pallas_call(
        late_kernel,
        out_shape=(
            jax.ShapeDtypeStruct((4, half, 128), BF),
            jax.ShapeDtypeStruct((4, half, 256), BF),
            jax.ShapeDtypeStruct((4, quarter, 128), BF),
            jax.ShapeDtypeStruct((4, quarter // 2, 128), BF),
            jax.ShapeDtypeStruct((quarter, D), BF),
        ),
        in_specs=[SM] + [VM] * 8,
        out_specs=(VM,) * 5,
        scratch_shapes=[
            pltpu.VMEM((2, quarter, D), BF),
            pltpu.VMEM((2, 2 * half // 256, 256, 256), F32),
        ],
        compiler_params=params(22),
        cost_estimate=cost(7e9, 6e6),
        name="late",
    )(meta, *slices, gain, own_w, keys, values)


def last(meta, q, keys_0, values_0, keys_1, values_1, after):
    quarter = q.shape[1]
    return pl.pallas_call(
        last_kernel,
        out_shape=jax.ShapeDtypeStruct((4, quarter // 2, 128), BF),
        in_specs=[SM] + [VM] * 5 + [AN],
        out_specs=VM,
        scratch_shapes=[pltpu.VMEM((2, 4 * quarter // 256, 256, 256), F32)],
        compiler_params=params(18),
        cost_estimate=cost(5e9, 6e6),
        name="last",
    )(meta, q, keys_0, values_0, keys_1, values_1, after)


def mlp_kernel(kept, start, meta_ref, after_ref, early_ref, res0_ref, res1_ref, *refs):
    late_refs = refs[:-7]
    wo_ref, gain_ref, wi_ref, wd_ref, out_ref, att_ref, res_ref = refs[-7:]
    count = out_ref.shape[0]
    rows = slice(start, start + count)
    second = lax.shift_right_logical(meta_ref[0], 1)

    @pl.when(second == (1 if kept else 0))
    def _():
        piece = late_refs[0].shape[1]
        for at, ref in enumerate(late_refs):
            for pair in range(4):
                att_ref[at * piece : at * piece + piece, pair * 128 : pair * 128 + 128] = ref[pair]
        res_ref[...] = res1_ref[rows, :]

    @pl.when(second == (0 if kept else 1))
    def _():
        for pair in range(4):
            att_ref[:, pair * 128 : pair * 128 + 128] = early_ref[pair, rows, :]
        res_ref[...] = res0_ref[rows, :]

    hidden = (res_ref[...].astype(F32) + dot(att_ref[...], wo_ref[...])).astype(BF)
    hidden = hidden.astype(F32)
    scale = lax.rsqrt(jnp.mean(hidden * hidden, axis=1, keepdims=True) + 1e-06)
    normed = (hidden * scale * gain_ref[...]).astype(BF)
    acc = hidden
    step = 512
    for k in range(FF // step):
        gate = dot(normed, wi_ref[:, k * step : k * step + step])
        up = dot(normed, wi_ref[:, FF + k * step : FF + k * step + step])
        half = 0.5 * gate
        act = ((half + half * jnp.tanh(half)) * up).astype(BF)
        acc = acc + dot(act, wd_ref[k * step : k * step + step, :])
    out_ref[...] = acc.astype(BF)


def mlp(kept, start, meta, after, att_0, res_0, res_1, lates, weights):
    count = sum(x.shape[1] for x in lates)
    return pl.pallas_call(
        functools.partial(mlp_kernel, kept, start),
        out_shape=jax.ShapeDtypeStruct((count, D), BF),
        in_specs=[SM, AN] + [VM] * (7 + len(lates)),
        out_specs=VM,
        scratch_shapes=[pltpu.VMEM((count, D), BF), pltpu.VMEM((count, D), BF)],
        compiler_params=params(20),
        cost_estimate=cost(count * 7e6, 6e6),
        name="mlp",
    )(meta, after, att_0, res_0, res_1, *lates, *weights)


def exchange(x, pairs):
    return lax.ppermute(x, "cols", pairs)


def local(token_ids, lengths, table, attn_gain, w_qkv, w_out, mlp_gain, w_in, w_down):
    batch_dev, quarter = token_ids.shape
    owners = lax.axis_size("rows")
    col_count = lax.axis_size("cols")
    half = 2 * quarter
    c = lax.axis_index("cols")
    h = c // 2
    row_bits = (table.shape[0] - 1).bit_length()
    meta = jnp.stack([c, jnp.where(h == 0, lengths[0], lengths[1])]).astype(I32)

    copies = jnp.broadcast_to(token_ids, (col_count, *token_ids.shape))
    ids = lax.all_to_all(copies, "cols", split_axis=0, concat_axis=0, tiled=True)
    ids = jnp.transpose(ids, (1, 0, 2)).reshape(batch_dev * col_count, quarter)
    slots, requests = route(ids, row_bits, owners)
    asked = lax.all_to_all(
        requests.reshape(owners, REQ), "rows", split_axis=0, concat_axis=0, tiled=True
    )
    looked = lookup(asked.reshape(-1), table, owners)
    got = lax.all_to_all(looked, "rows", split_axis=0, concat_axis=0, tiled=True)
    got = got.reshape(owners * CAP, table.shape[1])
    slots = slots.reshape(-1)

    theirs_0, wide = pick_first(meta, slots, got, half, quarter)
    crossed_0 = exchange(theirs_0, CROSS)
    mine_0 = pick_more(meta, slots, wide, theirs_0, half, quarter, False, 0)
    swapped_0 = exchange(mine_0, SWAP)
    theirs_1 = pick_more(meta, slots, wide, mine_0, half, quarter, True, 1)
    crossed_1 = exchange(theirs_1, CROSS)
    relayed_0 = exchange(crossed_0, SWAP)
    mine_1 = pick_more(meta, slots, wide, crossed_0, half, quarter, False, 1)
    swapped_1 = exchange(mine_1, SWAP)
    relayed_1 = exchange(crossed_1, SWAP)

    gain = attn_gain.reshape(col_count, -1)
    keys_0, values_0, own_w, att_0, res_0 = early(
        meta, (mine_0, swapped_0, crossed_0, relayed_0), gain, w_qkv, quarter
    )
    keys_1, values_1, q, att_1a, res_1 = late(
        meta, (mine_1, swapped_1, crossed_1, relayed_1), gain, own_w, keys_0, values_0, quarter
    )
    weights = (w_out, mlp_gain.reshape(1, -1), w_in, w_down)
    sent_a = mlp(False, 0, meta, res_1, att_0, res_0, res_1, (att_1a,), weights)
    came_a = exchange(sent_a, CROSS)
    att_1b = last(meta, q, keys_0, values_0, keys_1, values_1, sent_a)
    sent_b = mlp(False, quarter // 2, meta, att_1b, att_0, res_0, res_1, (att_1b,), weights)
    came_b = exchange(sent_b, CROSS)
    kept = mlp(True, 0, meta, sent_b, att_0, res_0, res_1, (att_1a, att_1b), weights)
    which = lax.broadcasted_iota(I32, (batch_dev, quarter // 2, D), 0) == h
    return jnp.concatenate(
        [
            jnp.where(which, kept[None, : quarter // 2], came_a[None]),
            jnp.where(which, kept[None, quarter // 2 :], came_b[None]),
        ],
        axis=1,
    )


def solution(mesh):
    in_specs = (P("rows", "cols"), P("rows"), P("rows", "cols"), P(), P(), P(), P(), P(), P())
    out_specs = P("rows", "cols", None)
    return jax.shard_map(local, mesh=mesh, in_specs=in_specs, out_specs=out_specs, check_vma=False)
```

time: 152 us -> 139 us (0.914); the launches traced: 150 us -> 139 us
  waiting for transfers between devices: 52.4 us -> 44.2 us
  starting transfers between devices: 14.6 us -> 12.2 us
  local copies, waits for them, and re-layouts: 3.52 us -> 1.36 us
  Pallas kernels: 51.5 us -> 53.1 us
    ppermute x9 -> x8, waiting for transfers between devices: 15.9 us -> 7.71 us  [exchange(): return lax.ppermute(x, 'cols', pairs)]
    pallas_call x6 -> x8, Pallas kernels: 29.4 us -> 32.9 us  [the longest x3 12.1 us: mlp(): pl.pallas_call(functools.partial(mlp_kernel, kept, start), out_shape=jax....]
    unnamed x17 -> x15, local copies, waits for them, and re-layouts: 2.23 us -> 0.04 us
    ppermute x9 -> x8, starting transfers between devices: 10.3 us -> 8.12 us  [exchange(): return lax.ppermute(x, 'cols', pairs)]
    pallas_call x1, Pallas kernels: 3.77 us -> 2.13 us  [pick_first(): pl.pallas_call(pick_first_kernel, out_shape=(jax.ShapeDtypeStruct((half,...]
  transfers between devices with their start and end apart: 10 -> 9, of which waited for: 6 -> 6; matrix products, arithmetic and copies ran while one was open for 0% -> 1% of each run, Pallas kernels for 24% -> 21%
where the time goes in v3:
time: 139 us
  Pallas kernels  53.1 us (38%)
  waiting for transfers between devices  44.2 us (32%)
  blocking collectives  25.1 us (18%)
  starting transfers between devices  12.2 us (9%)
  between operations  1.44 us (1%)
    all_to_all x1, waiting for transfers between devices, local(): lax.all_to_all(looked, 'rows', split_axis=0, concat_axis=0, tiled=True)  36.5 us
    all_to_all x1, blocking collectives, local(): lax.all_to_all(requests.reshape(owners, REQ), 'rows', split_axis=0, conca...  14.5 us
    pallas_call x3, Pallas kernels, mlp(): pl.pallas_call(functools.partial(mlp_kernel, kept, start), out_shape=jax....  12.1 us
    all_to_all x1, blocking collectives, local(): lax.all_to_all(copies, 'cols', split_axis=0, concat_axis=0, tiled=True)  10.6 us
    pallas_call x1, Pallas kernels, lookup(): pl.pallas_call(lookup_kernel, out_shape=jax.ShapeDtypeStruct((owners, CAP...  8.92 us
    ppermute x8, starting transfers between devices, exchange(): return lax.ppermute(x, 'cols', pairs)  8.12 us
    pallas_call x1, Pallas kernels, late(): pl.pallas_call(late_kernel, out_shape=(jax.ShapeDtypeStruct((4, half, 128...  7.89 us
    ppermute x8, waiting for transfers between devices, exchange(): return lax.ppermute(x, 'cols', pairs)  7.71 us
  transfers between devices with their start and end apart: 9, of which 6 were waited for; matrix products, arithmetic and copies ran while one was open for 1% of the time, Pallas kernels for 21%

profile of v3, /device:TPU:0, one launch (start us, length us, event | category | flops | bytes accessed | tf_op | source)
XLA Modules:
  0.0 138.6 jit_solution(3636973515269301728)
XLA Ops:
  0.7 10.6 %all_to_all.19 = s32[4,2,512]{2,1,0:T(2,128)S(1)} all-to-all(s32[4,2,512]{2,1,0:T(2,128)S(1)} %broadcast_in_dim.33), channel_id=1, replica_groups=mesh['rows'=32,'cols'=4] {'cols'}, dimensions={0} | all-to-all | bytes 32768 | tf_op jit(solution)/shard_map/all_to_all | solution.py:521
  11.3 1.7 %route.1 = (s32[8,512]{1,0:T(8,128)S(1)}, s32[96,128]{1,0:T(8,128)S(1)}) custom-call(s32[8,512]{1,0:T(8,128)S(1)} %reshape.27.ids_ref), custom_call_target="tpu_custom_call" | custom-call | tf_op jit(solution)/shard_map/route/pallas_call | solution.py:84
  13.0 14.5 %all_to_all.20 = s32[32,1,384]{2,1,0:T(1,128)} all-to-all(s32[32,1,384]{2,1,0:T(1,128)S(1)} %bitcast.13), channel_id=1, replica_groups=mesh['rows'=32,'cols'=4] {'rows'}, dimensions={0} | all-to-all | bytes 98304 | tf_op jit(solution)/shard_map/all_to_all | solution.py:524
  27.5 8.9 %lookup.1 = bf16[32,344,128]{2,1,0:T(8,128)(2,1)} custom-call(s32[12288]{0:T(1024)} %bitcast.25, bf16[16384,128]{1,0:T(8,128)(2,1)} %table_ref.1), custom_call_target="tpu_custom_call" | custom-call | flops 6000000000 | bytes 4000000 | tf_op jit(solution)/shard_map/lookup/pallas_call | solution.py:173
  36.5 4.1 %all-to-all-start.2 = ((bf16[32,344,128]{2,1,0:T(8,128)(2,1)}), bf16[32,344,128]{2,1,0:T(8,128)(2,1)S(1)}, u32[]{:S(2)}, u32[]{:S(2)}) async-start(bf16[32,344,128]{2,1,0:T(8,128)(2,1)} %lookup.1), calls=%async_computation.2 | async-start | bytes 5636096 | tf_op jit(solution)/shard_map/all_to_all | solution.py:528
  42.5 36.5 %all-to-all-done.2 = bf16[32,344,128]{2,1,0:T(8,128)(2,1)S(1)} async-done(((bf16[32,344,128]{2,1,0:T(8,128)(2,1)}), bf16[32,344,128]{2,1,0:T(8,128)(2,1)S(1)}, u32[]{:S(2)}, u32[]{:S(2)}) %all-to-all-start.2) | async-done | bytes 2818080 | tf_op jit(solution)/shard_map/all_to_all | solution.py:528
  78.9 2.1 %pick_first.1 = (bf16[1024,128]{1,0:T(8,128)(2,1)S(1)}, f32[11008,128]{1,0:T(8,128)S(1)}) custom-call(s32[2]{0:T(128)S(1)} %pad_add_fusion.meta_ref, s32[4096]{0:T(1024)S(1)} %bitcast.15, bf16[11008,128]{1,0:T(8,128)(2,1)S(1)} %bitcast.12), custom_call_target="tpu_custom_call" | custom-call | flops 3000000000 | bytes 4000000 | tf_op jit(solution)/shard_map/pick_first/pallas_call | solution.py:251
  81.1 1.2 collective-permute-start
  82.3 2.1 %pick_more.4.after_ref.s0 = bf16[1024,128]{1,0:T(8,128)(2,1)S(1)} custom-call(s32[2]{0:T(128)S(1)} %pad_add_fusion.meta_ref, s32[4096]{0:T(1024)S(1)} %bitcast.16, f32[11008,128]{1,0:T(8,128)S(1)} %get-tuple-element.21.wide_ref, bf16[1024,128]{1,0:T(8,128)(2,1)S(1)} %get-tuple-element.22.after_ref), custom_call_target="tpu_custom_call" | custom-call | flops 2000000000 | bytes 4000000 | tf_op jit(solution)/shard_map/pick_more/pallas_call | solution.py:268
  84.5 2.1 %pick_more.5 = bf16[1024,128]{1,0:T(8,128)(2,1)S(1)} custom-call(s32[2]{0:T(128)S(1)} %pad_add_fusion.meta_ref, s32[4096]{0:T(1024)S(1)} %bitcast.17, f32[11008,128]{1,0:T(8,128)S(1)} %get-tuple-element.21.wide_ref, bf16[1024,128]{1,0:T(8,128)(2,1)S(1)} %pick_more.4.after_ref.s0), custom_call_target="tpu_custom_call" | custom-call | flops 2000000000 | bytes 4000000 | tf_op jit(solution)/shard_map/pick_more/pallas_call | solution.py:268
  86.7 2.1 %collective-permute-start.2 = (bf16[1024,128]{1,0:T(8,128)(2,1)S(1)}, bf16[1024,128]{1,0:T(8,128)(2,1)S(1)}, u32[]{:S(2)}, u32[]{:S(2)}) collective-permute-start(bf16[1024,128]{1,0:T(8,128)(2,1)S(1)} %pick_more.5), channel_id=1, source_target_pairs={{0,3},{3,0},{1,2},{2,1},{4,7},{7,4},{5,6},{6,5},{8,11},{11,8},{9,1... | collective-permute-start | bytes 786440 | tf_op jit(solution)/shard_map/ppermute | solution.py:507
  90.2 2.1 %pick_more.3.s0 = bf16[1024,128]{1,0:T(8,128)(2,1)S(1)} custom-call(s32[2]{0:T(128)S(1)} %pad_add_fusion.meta_ref, s32[4096]{0:T(1024)S(1)} %bitcast.18, f32[11008,128]{1,0:T(8,128)S(1)} %get-tuple-element.21.wide_ref, bf16[1024,128]{1,0:T(8,128)(2,1)S(1)} %collective-permute-done.after_ref.s2), custom_call_target="tpu_custom_call" | custom-call | flops 2000000000 | bytes 4000000 | tf_op jit(solution)/shard_map/pick_more/pallas_call | solution.py:268
  92.4 1.2 collective-permute-start.1
  95.1 3.6 %collective-permute-done.5.s3 = bf16[1024,128]{1,0:T(8,128)(2,1)S(1)} collective-permute-done((bf16[1024,128]{1,0:T(8,128)(2,1)S(1)}, bf16[1024,128]{1,0:T(8,128)(2,1)S(1)}, u32[]{:S(2)}, u32[]{:S(2)}) %collective-permute-start.5) | collective-permute-done | bytes 262176 | tf_op jit(solution)/shard_map/ppermute | solution.py:507
  98.7 7.4 %early.1 = (bf16[4,1024,128]{2,1,0:T(8,128)(2,1)S(1)}, bf16[4,1024,256]{2,1,0:T(8,128)(2,1)S(1)}, bf16[512,1536]{1,0:T(8,128)(2,1)S(1)}, bf16[4,512,128]{2,1,0:T(8,128)(2,1)S(1)}, bf16[512,512]{1,0:T(8,128)(2,1)S(1)}) custom-call(s32[2]{0:T(128)S(1)} %pad_add_fusion.meta_ref, bf16[1024,128]{1,0:T(8,128)(2,1)S(1)} %pick_more.4.after_ref.s0, ...), custom_call_target="tpu_custom_call" | custom-call | flops 7000000000 | bytes 6000000 | tf_op jit(solution)/shard_map/early/pallas_call | solution.py:397
  106.1 1.6 %collective-permute-done.3.s3 = bf16[1024,128]{1,0:T(8,128)(2,1)S(1)} collective-permute-done((bf16[1024,128]{1,0:T(8,128)(2,1)S(1)}, bf16[1024,128]{1,0:T(8,128)(2,1)S(1)}, u32[]{:S(2)}, u32[]{:S(2)}) %collective-permute-start.3) | collective-permute-done | bytes 262176 | tf_op jit(solution)/shard_map/ppermute | solution.py:507
  107.8 7.9 %late.1 = (bf16[4,1024,128]{2,1,0:T(8,128)(2,1)S(1)}, bf16[4,1024,256]{2,1,0:T(8,128)(2,1)S(1)}, bf16[4,512,128]{2,1,0:T(8,128)(2,1)S(1)}, bf16[4,256,128]{2,1,0:T(8,128)(2,1)S(1)}, bf16[512,512]{1,0:T(8,128)(2,1)S(1)}) custom-call(s32[2]{0:T(128)S(1)} %pad_add_fusion.meta_ref, bf16[1024,128]{1,0:T(8,128)(2,1)S(1)} %pick_more.3.s0, ...), custom_call_target="tpu_custom_call" | custom-call | flops 7000000000 | bytes 6000000 | tf_op jit(solution)/shard_map/late/pallas_call | solution.py:421
  115.7 3.5 %mlp.3.after_ref = bf16[256,512]{1,0:T(8,128)(2,1)S(1)} custom-call(s32[2]{0:T(128)S(1)} %pad_add_fusion.meta_ref, bf16[512,512]{1,0:T(8,128)(2,1)S(1)} %get-tuple-element.29.after_ref.res1_ref, bf16[4,512,128]{2,1,0:T(8,128)(2,1)S(1)} %get-tuple-element.30.early_ref, bf16[512,512]{1,0:T(8,128)(2,1)S(1)} %get-tuple-element.31.res0_ref, ...), custom_call_target="tpu_custom_call" | custom-call | flops 1792000000 | bytes 6000000 | tf_op jit(solution)/shard_map/mlp/pallas_call | solution.py:494
  120.0 6.5 %last.1.after_ref.refs_0_.refs_1_ = bf16[4,256,128]{2,1,0:T(8,128)(2,1)S(1)} custom-call(s32[2]{0:T(128)S(1)} %pad_add_fusion.meta_ref, bf16[4,512,128]{2,1,0:T(8,128)(2,1)S(1)} %get-tuple-element.26.q_ref, bf16[4,1024,128]{2,1,0:T(8,128)(2,1)S(1)} %get-tuple-element.24.k0_ref, bf16[4,1024,256]{2,1,0:T(8,128)(2,1)S(1)} %get-tuple-element.25.v0_ref, ...), custom_call_target="tpu_custom_call" | custom-call | flops 5000000000 | bytes 6000000 | tf_op jit(solution)/shard_map/last/pallas_call | solution.py:444
  126.5 3.2 %mlp.4.after_ref = bf16[256,512]{1,0:T(8,128)(2,1)S(1)} custom-call(s32[2]{0:T(128)S(1)} %pad_add_fusion.meta_ref, bf16[4,256,128]{2,1,0:T(8,128)(2,1)S(1)} %last.1.after_ref.refs_0_.refs_1_, bf16[4,512,128]{2,1,0:T(8,128)(2,1)S(1)} %get-tuple-element.30.early_ref, bf16[512,512]{1,0:T(8,128)(2,1)S(1)} %get-tuple-element.31.res0_ref, ...), custom_call_target="tpu_custom_call" | custom-call | flops 1792000000 | bytes 6000000 | tf_op jit(solution)/shard_map/mlp/pallas_call | solution.py:494
  129.7 1.0 collective-permute-start.7
  130.7 5.4 %mlp.5 = bf16[512,512]{1,0:T(8,128)(2,1)S(1)} custom-call(s32[2]{0:T(128)S(1)} %pad_add_fusion.meta_ref, bf16[256,512]{1,0:T(8,128)(2,1)S(1)} %mlp.4.after_ref, bf16[4,512,128]{2,1,0:T(8,128)(2,1)S(1)} %get-tuple-element.30.early_ref, bf16[512,512]{1,0:T(8,128)(2,1)S(1)} %get-tuple-element.31.res0_ref, ...), custom_call_target="tpu_custom_call" | custom-call | flops 3584000000 | bytes 6000000 | tf_op jit(solution)/shard_map/mlp/pallas_call | solution.py:494
  136.2 1.2 collective-permute-done.7
  137.6 1.0 pad_maximum_fusion
  (32 shorter events, 5.4 us)
Async XLA Ops:
  36.5 4.1 %copy-start.6 = (s32[2]{0:T(128)S(1)}, s32[2]{0:T(128)}, u32[]{:S(2)}) copy-start(s32[2]{0:T(128)} %param.10) | copy-start | bytes 28
  36.5 42.5 %all-to-all-start.2 = ((bf16[32,344,128]{2,1,0:T(8,128)(2,1)}), bf16[32,344,128]{2,1,0:T(8,128)(2,1)S(1)}, u32[]{:S(2)}, u32[]{:S(2)}) async-start(bf16[32,344,128]{2,1,0:T(8,128)(2,1)} %lookup.1), calls=%async_computation.2 | async-start | bytes 5636096 | tf_op jit(solution)/shard_map/all_to_all | solution.py:528
  81.1 8.3 %collective-permute-start = (bf16[1024,128]{1,0:T(8,128)(2,1)S(1)}, bf16[1024,128]{1,0:T(8,128)(2,1)S(1)}, u32[]{:S(2)}, u32[]{:S(2)}) collective-permute-start(bf16[1024,128]{1,0:T(8,128)(2,1)S(1)} %get-tuple-element.22.after_ref), channel_id=1, source_target_pairs={{0,3},{3,0},{1,2},{2,1},{4,7},{7,4},{5,6},{6,5},{8,11},{11,8},{9,1... | collective-permute-start | bytes 786440 | tf_op jit(solution)/shard_map/ppermute | solution.py:507
  84.5 10.7 %collective-permute-start.4 = (bf16[1024,128]{1,0:T(8,128)(2,1)S(1)}, bf16[1024,128]{1,0:T(8,128)(2,1)S(1)}, u32[]{:S(2)}, u32[]{:S(2)}) collective-permute-start(bf16[1024,128]{1,0:T(8,128)(2,1)S(1)} %pick_more.4.after_ref.s0), channel_id=1, source_target_pairs={{0,1},{1,0},{2,3},{3,2},{4,5},{5,4},{6,7},{7,6},{8,9},{9,8},{10,11... | collective-permute-start | bytes 786440 | tf_op jit(solution)/shard_map/ppermute | solution.py:507
  86.7 7.7 %collective-permute-start.2 = (bf16[1024,128]{1,0:T(8,128)(2,1)S(1)}, bf16[1024,128]{1,0:T(8,128)(2,1)S(1)}, u32[]{:S(2)}, u32[]{:S(2)}) collective-permute-start(bf16[1024,128]{1,0:T(8,128)(2,1)S(1)} %pick_more.5), channel_id=1, source_target_pairs={{0,3},{3,0},{1,2},{2,1},{4,7},{7,4},{5,6},{6,5},{8,11},{11,8},{9,1... | collective-permute-start | bytes 786440 | tf_op jit(solution)/shard_map/ppermute | solution.py:507
  89.3 9.4 %collective-permute-start.5 = (bf16[1024,128]{1,0:T(8,128)(2,1)S(1)}, bf16[1024,128]{1,0:T(8,128)(2,1)S(1)}, u32[]{:S(2)}, u32[]{:S(2)}) collective-permute-start(bf16[1024,128]{1,0:T(8,128)(2,1)S(1)} %collective-permute-done.after_ref.s2), channel_id=1, source_target_pairs={{0,1},{1,0},{2,3},{3,2},{4,5},{5,4},{6,7},{7,6},{8,9},{9,8},{10,11... | collective-permute-start | bytes 786440 | tf_op jit(solution)/shard_map/ppermute | solution.py:507
  90.2 8.5 %copy-start.4 = (bf16[512,1536]{1,0:T(8,128)(2,1)S(1)}, bf16[512,1536]{1,0:T(8,128)(2,1)}, u32[]{:S(2)}) copy-start(bf16[512,1536]{1,0:T(8,128)(2,1)} %w_ref.1) | copy-start | bytes 4718596
  90.2 8.5 %copy-start.5 = (f32[512]{0:T(512)S(1)}, f32[512]{0:T(512)}, u32[]{:S(2)}) copy-start(f32[512]{0:T(512)} %param.12) | copy-start | bytes 6148
  92.4 15.4 %collective-permute-start.1 = (bf16[1024,128]{1,0:T(8,128)(2,1)S(1)}, bf16[1024,128]{1,0:T(8,128)(2,1)S(1)}, u32[]{:S(2)}, u32[]{:S(2)}) collective-permute-start(bf16[1024,128]{1,0:T(8,128)(2,1)S(1)} %pick_more.3.s0), channel_id=1, source_target_pairs={{0,1},{1,0},{2,3},{3,2},{4,5},{5,4},{6,7},{7,6},{8,9},{9,8},{10,11... | collective-permute-start | bytes 786440 | tf_op jit(solution)/shard_map/ppermute | solution.py:507
  94.4 13.4 %collective-permute-start.3 = (bf16[1024,128]{1,0:T(8,128)(2,1)S(1)}, bf16[1024,128]{1,0:T(8,128)(2,1)S(1)}, u32[]{:S(2)}, u32[]{:S(2)}) collective-permute-start(bf16[1024,128]{1,0:T(8,128)(2,1)S(1)} %collective-permute-done.2.s2), channel_id=1, source_target_pairs={{0,1},{1,0},{2,3},{3,2},{4,5},{5,4},{6,7},{7,6},{8,9},{9,8},{10,11... | collective-permute-start | bytes 786440 | tf_op jit(solution)/shard_map/ppermute | solution.py:507
  107.8 7.9 %copy-start = (bf16[512,4096]{1,0:T(8,128)(2,1)S(1)}, bf16[512,4096]{1,0:T(8,128)(2,1)}, u32[]{:S(2)}) copy-start(bf16[512,4096]{1,0:T(8,128)(2,1)} %refs_4_.5) | copy-start | bytes 12582916
  107.8 7.9 %copy-start.1 = (bf16[2048,512]{1,0:T(8,128)(2,1)S(1)}, bf16[2048,512]{1,0:T(8,128)(2,1)}, u32[]{:S(2)}) copy-start(bf16[2048,512]{1,0:T(8,128)(2,1)} %refs_5_.1) | copy-start | bytes 6291460
  107.8 7.9 %copy-start.2 = (bf16[512,512]{1,0:T(8,128)(2,1)S(1)}, bf16[512,512]{1,0:T(8,128)(2,1)}, u32[]{:S(2)}) copy-start(bf16[512,512]{1,0:T(8,128)(2,1)} %refs_2_.1) | copy-start | bytes 1572868
  107.8 7.9 %copy-start.3 = (f32[512]{0:T(512)S(1)}, f32[512]{0:T(512)}, u32[]{:S(2)}) copy-start(f32[512]{0:T(512)} %param.15) | copy-start | bytes 6148
  119.2 18.2 %collective-permute-start.6 = (bf16[256,512]{1,0:T(8,128)(2,1)S(1)}, bf16[256,512]{1,0:T(8,128)(2,1)S(1)}, u32[]{:S(2)}, u32[]{:S(2)}) collective-permute-start(bf16[256,512]{1,0:T(8,128)(2,1)S(1)} %mlp.3.after_ref), channel_id=1, source_target_pairs={{0,3},{3,0},{1,2},{2,1},{4,7},{7,4},{5,6},{6,5},{8,11},{11,8},{9,1... | collective-permute-start | bytes 786440 | tf_op jit(solution)/shard_map/ppermute | solution.py:507
  129.7 7.7 %collective-permute-start.7 = (bf16[256,512]{1,0:T(8,128)(2,1)S(1)}, bf16[256,512]{1,0:T(8,128)(2,1)S(1)}, u32[]{:S(2)}, u32[]{:S(2)}) collective-permute-start(bf16[256,512]{1,0:T(8,128)(2,1)S(1)} %mlp.4.after_ref), channel_id=1, source_target_pairs={{0,3},{3,0},{1,2},{2,1},{4,7},{7,4},{5,6},{6,5},{8,11},{11,8},{9,1... | collective-permute-start | bytes 786440 | tf_op jit(solution)/shard_map/ppermute | solution.py:507

commit v4 on v3

--- a/solution.py
+++ b/solution.py
@@ -191,21 +191,21 @@
     )(asked, table)
 
 
-def slots_of(other, late, meta_ref, slot_ref, here_ref, sem):
+def slots_of(other, late, slot_ref, here_ref, sem):
     half = here_ref.shape[0]
-    history = lax.shift_right_logical(meta_ref[0], 1)
+    history = lax.shift_right_logical(lax.axis_index("cols"), 1)
     history = 1 - history if other else history
     start = pl.multiple_of((history * 2 + late) * half, half)
     return pltpu.make_async_copy(slot_ref.at[pl.ds(start, half)], here_ref, sem)
 
 
-def pick(here_ref, wide_ref, row_ref, out_ref):
+def pick(here_ref, start, wide_ref, row_ref, out_ref):
     block = row_ref.shape[0]
     for j in range(out_ref.shape[0] // block):
 
         def some(i, _):
             base = pl.multiple_of(i * 32, 32)
-            at = j * block + base
+            at = start + j * block + base
             for k in range(32):
                 row_ref[pl.ds(base + k, 1), :] = wide_ref[pl.ds(here_ref[at + k], 1), :]
             return 0
@@ -214,9 +214,9 @@
         out_ref[j * block : j * block + block, :] = row_ref[...].astype(BF)
 
 
-def pick_first_kernel(meta_ref, slot_ref, got_ref, out_ref, wide_ref, row_ref, here_ref, sem):
+def pick_first_kernel(slot_ref, got_ref, out_ref, wide_ref, row_ref, here_ref, sem):
     step = 2 * CAP
-    copy = slots_of(True, 0, meta_ref, slot_ref, here_ref, sem)
+    copy = slots_of(True, 0, slot_ref, here_ref, sem)
     copy.start()
 
     def widen(i, _):
@@ -226,27 +226,24 @@
 
     lax.fori_loop(0, wide_ref.shape[0] // step, widen, 0)
     copy.wait()
-    pick(here_ref, wide_ref, row_ref, out_ref)
-
-
-def pick_more_kernel(
-    other, late, meta_ref, slot_ref, wide_ref, after_ref, out_ref, row_ref, here_ref, sem
-):
-    copy = slots_of(other, late, meta_ref, slot_ref, here_ref, sem)
-    copy.start()
-    copy.wait()
-    pick(here_ref, wide_ref, row_ref, out_ref)
-
-
-def pick_scratch(half, quarter, width):
-    return [
-        pltpu.VMEM((quarter, width), F32),
-        pltpu.SMEM((half,), I32),
-        pltpu.SemaphoreType.DMA,
+    pick(here_ref, 0, wide_ref, row_ref, out_ref)
+
+
+def pick_more_kernel(which, slot_ref, wide_ref, after_ref, *refs):
+    outs, (row_ref, here_ref, sem) = refs[: len(which)], refs[len(which) :]
+    half = outs[0].shape[0]
+    copies = [
+        slots_of(other, late, slot_ref, here_ref.at[pl.ds(i * half, half)], sem.at[i])
+        for i, (other, late) in enumerate(which)
     ]
-
-
-def pick_first(meta, slots, got, half, quarter):
+    for copy in copies:
+        copy.start()
+    for i, copy in enumerate(copies):
+        copy.wait()
+        pick(here_ref, i * half, wide_ref, row_ref, outs[i])
+
+
+def pick_first(slots, got, half, quarter):
     rows, width = got.shape
     return pl.pallas_call(
         pick_first_kernel,
@@ -254,53 +251,77 @@
             jax.ShapeDtypeStruct((half, width), BF),
             jax.ShapeDtypeStruct((rows, width), F32),
         ),
-        in_specs=[SM, AN, VM],
+        in_specs=[AN, VM],
         out_specs=(VM, VM),
-        scratch_shapes=pick_scratch(half, quarter, width),
+        scratch_shapes=[
+            pltpu.VMEM((quarter, width), F32),
+            pltpu.SMEM((half,), I32),
+            pltpu.SemaphoreType.DMA,
+        ],
         compiler_params=params(14),
         cost_estimate=cost(3e9, 4e6),
         name="pick_first",
-    )(meta, slots, got)
-
-
-def pick_more(meta, slots, wide, after, half, quarter, other, late):
+    )(slots, got)
+
+
+def pick_more(slots, wide, after, half, quarter, which):
     width = wide.shape[1]
     return pl.pallas_call(
-        functools.partial(pick_more_kernel, other, late),
-        out_shape=jax.ShapeDtypeStruct((half, width), BF),
-        in_specs=[SM, AN, VM, AN],
-        out_specs=VM,
-        scratch_shapes=pick_scratch(half, quarter, width),
+        functools.partial(pick_more_kernel, which),
+        out_shape=[jax.ShapeDtypeStruct((half, width), BF) for _ in which],
+        in_specs=[AN, VM, AN],
+        out_specs=[VM for _ in which],
+        scratch_shapes=[
+            pltpu.VMEM((quarter, width), F32),
+            pltpu.SMEM((len(which) * half,), I32),
+            pltpu.SemaphoreType.DMA((len(which),)),
+        ],
         compiler_params=params(14),
-        cost_estimate=cost(2e9, 4e6),
+        cost_estimate=cost(2e9 * len(which), 4e6),
         name="pick_more",
-    )(meta, slots, wide, after)
+    )(slots, wide, after)
 
 
 def project(c, slices, gain_ref, w_ref, norm_ref, k_ref, v_ref, res_ref, mine):
     n = norm_ref.shape[1]
-    mate = lax.bitwise_xor(c, 1)
-    order = (c, mate, 3 - c, 3 - mate)
+    odd = c & 1
+    first = lax.shift_right_logical(c, 1)
+    blocks = (first, 1 - first)
+    w_rows = [pl.ds(pl.multiple_of(i * 256, 256), 256) for i in blocks]
+
+    def project_rows(normed, part):
+        return dot(normed[0], w_ref[w_rows[0], part]) + dot(normed[1], w_ref[w_rows[1], part])
+
     for b in range(2):
         rows = slice(b * n, b * n + n)
-        wide = [ref[rows, :].astype(F32) for ref in slices]
-        square = sum(x * x for x in wide)
+        x0, x1, x2, x3 = [ref[rows, :].astype(F32) for ref in slices]
+        square = x0 * x0 + x1 * x1 + x2 * x2 + x3 * x3
         scale = lax.rsqrt(jnp.sum(square, axis=1, keepdims=True) * (1.0 / D) + 1e-06)
-        normed = jnp.concatenate(
-            [(x * scale * gain_ref[pl.ds(i, 1), :]).astype(BF) for x, i in zip(wide, order)],
-            axis=1,
+        wide = (
+            jnp.concatenate([jnp.where(odd == 1, x1, x0), jnp.where(odd == 1, x0, x1)], axis=1),
+            jnp.concatenate([jnp.where(odd == 1, x2, x3), jnp.where(odd == 1, x3, x2)], axis=1),
         )
-        norm_ref[b] = normed
-        keys = dot(normed, w_ref[:, D : 2 * D]).astype(BF)
-        values = dot(normed, w_ref[:, 2 * D :]).astype(BF)
+
+        @pl.when(mine == b)
+        def _():
+            for x, lanes in zip(wide, w_rows):
+                res_ref[:, lanes] = x.astype(BF)
+
+        normed = [
+            (x * scale * gain_ref[pl.ds(i, 1), :]).astype(BF) for x, i in zip(wide, blocks)
+        ]
+        norm_ref[b, :, 0:256] = normed[0]
+        norm_ref[b, :, 256:512] = normed[1]
         for pair in range(4):
-            k_ref[pair, rows, :] = keys[:, pair * 128 : pair * 128 + 128]
-            v_ref[pair, rows, 0:128] = values[:, pair * 128 : pair * 128 + 128]
+            if pair % 2 == 0:
+                keys = project_rows(normed, slice(D + pair * 128, D + pair * 128 + 256))
+                values = project_rows(normed, slice(2 * D + pair * 128, 2 * D + pair * 128 + 256))
+            part = slice(pair % 2 * 128, pair % 2 * 128 + 128)
+            k_ref[pair, rows, :] = keys[:, part].astype(BF)
+            v_ref[pair, rows, 0:128] = values[:, part].astype(BF)
             v_ref[pair, rows, 128:256] = jnp.ones((n, 128), BF)
-    own = pl.ds(pl.multiple_of(mine * n, n), n)
-    for ref, i in zip(slices, order):
-        res_ref[:, pl.ds(pl.multiple_of(i * 128, 128), 128)] = ref[own, :]
-    return (dot(norm_ref[mine], w_ref[:, 0:D]) * (0.125 * LOG2E)).astype(BF)
+    chosen = (norm_ref[mine, :, 0:256], norm_ref[mine, :, 256:512])
+    return (project_rows(chosen, slice(0, D)) * (0.125 * LOG2E)).astype(BF)
 
 
 def keep_queries(q, q_ref):
@@ -360,51 +381,49 @@
 
 
 def early_kernel(
-    meta_ref, s0, s1, s2, s3, gain_ref, w_ref,
-    k_ref, v_ref, own_w_ref, att_ref, res_ref, norm_ref, q_ref, s_ref,
+    length_ref, s0, s1, s2, s3, gain_ref, w_ref,
+    k_ref, v_ref, att_ref, res_ref, norm_ref, q_ref, s_ref,
 ):
-    c = meta_ref[0]
-    mate = lax.bitwise_xor(c, 1)
-    for at, i in enumerate((c, mate, 3 - c, 3 - mate)):
-        own_w_ref[at * 128 : at * 128 + 128, :] = w_ref[pl.ds(pl.multiple_of(i * 128, 128), 128), :]
+    c = lax.axis_index("cols")
     quarter = jnp.minimum(c, 3 - c)
-    q = project(c, (s0, s1, s2, s3), gain_ref, own_w_ref, norm_ref, k_ref, v_ref, res_ref, quarter)
+    q = project(c, (s0, s1, s2, s3), gain_ref, w_ref, norm_ref, k_ref, v_ref, res_ref, quarter)
     keep_queries(q, q_ref)
-    attend(quarter, meta_ref[1], q_ref, (k_ref,), (v_ref,), s_ref, att_ref)
+    attend(quarter, length_ref[c // 2], q_ref, (k_ref,), (v_ref,), s_ref, att_ref)
 
 
 def late_kernel(
-    meta_ref, s0, s1, s2, s3, gain_ref, own_w_ref, k0_ref, v0_ref,
+    length_ref, s0, s1, s2, s3, gain_ref, w_ref, k0_ref, v0_ref,
     k_ref, v_ref, q_ref, att_ref, res_ref, norm_ref, s_ref,
 ):
-    c = meta_ref[0]
+    c = lax.axis_index("cols")
     quarter = jnp.maximum(c, 3 - c)
-    q = project(
-        c, (s0, s1, s2, s3), gain_ref, own_w_ref, norm_ref, k_ref, v_ref, res_ref, quarter - 2
-    )
+    q = project(c, (s0, s1, s2, s3), gain_ref, w_ref, norm_ref, k_ref, v_ref, res_ref, quarter - 2)
     keep_queries(q, q_ref)
-    attend(quarter, meta_ref[1], q_ref, (k0_ref, k_ref), (v0_ref, v_ref), s_ref, att_ref)
-
-
-def last_kernel(meta_ref, q_ref, k0_ref, v0_ref, k_ref, v_ref, after_ref, att_ref, s_ref):
-    c = meta_ref[0]
+    attend(
+        quarter, length_ref[c // 2], q_ref, (k0_ref, k_ref), (v0_ref, v_ref), s_ref, att_ref
+    )
+
+
+def last_kernel(length_ref, q_ref, k0_ref, v0_ref, k_ref, v_ref, after_ref, att_ref, s_ref):
+    c = lax.axis_index("cols")
     quarter = jnp.maximum(c, 3 - c)
-    attend(quarter, meta_ref[1], q_ref, (k0_ref, k_ref), (v0_ref, v_ref), s_ref, att_ref, 1)
-
-
-def early(meta, slices, gain, w_qkv, quarter):
+    attend(
+        quarter, length_ref[c // 2], q_ref, (k0_ref, k_ref), (v0_ref, v_ref), s_ref, att_ref, 1
+    )
+
+
+def early(lengths, slices, gain, w_qkv, quarter):
     half = 2 * quarter
     return pl.pallas_call(
         early_kernel,
         out_shape=(
             jax.ShapeDtypeStruct((4, half, 128), BF),
             jax.ShapeDtypeStruct((4, half, 256), BF),
-            jax.ShapeDtypeStruct(w_qkv.shape, BF),
             jax.ShapeDtypeStruct((4, quarter, 128), BF),
             jax.ShapeDtypeStruct((quarter, D), BF),
         ),
         in_specs=[SM] + [VM] * 6,
-        out_specs=(VM,) * 5,
+        out_specs=(VM,) * 4,
         scratch_shapes=[
             pltpu.VMEM((2, quarter, D), BF),
             pltpu.VMEM((4, quarter, 128), BF),
@@ -413,10 +432,10 @@
         compiler_params=params(20),
         cost_estimate=cost(7e9, 6e6),
         name="early",
-    )(meta, *slices, gain, w_qkv)
-
-
-def late(meta, slices, gain, own_w, keys, values, quarter):
+    )(lengths, *slices, gain, w_qkv)
+
+
+def late(lengths, slices, gain, w_qkv, keys, values, quarter):
     half = 2 * quarter
     return pl.pallas_call(
         late_kernel,
@@ -436,10 +455,10 @@
         compiler_params=params(22),
         cost_estimate=cost(7e9, 6e6),
         name="late",
-    )(meta, *slices, gain, own_w, keys, values)
-
-
-def last(meta, q, keys_0, values_0, keys_1, values_1, after):
+    )(lengths, *slices, gain, w_qkv, keys, values)
+
+
+def last(lengths, q, keys_0, values_0, keys_1, values_1, after):
     quarter = q.shape[1]
     return pl.pallas_call(
         last_kernel,
@@ -450,15 +469,15 @@
         compiler_params=params(18),
         cost_estimate=cost(5e9, 6e6),
         name="last",
-    )(meta, q, keys_0, values_0, keys_1, values_1, after)
-
-
-def mlp_kernel(kept, start, meta_ref, after_ref, early_ref, res0_ref, res1_ref, *refs):
+    )(lengths, q, keys_0, values_0, keys_1, values_1, after)
+
+
+def mlp_kernel(kept, start, after_ref, early_ref, res0_ref, res1_ref, *refs):
     late_refs = refs[:-7]
     wo_ref, gain_ref, wi_ref, wd_ref, out_ref, att_ref, res_ref = refs[-7:]
     count = out_ref.shape[0]
     rows = slice(start, start + count)
-    second = lax.shift_right_logical(meta_ref[0], 1)
+    second = lax.shift_right_logical(lax.axis_index("cols"), 1)
 
     @pl.when(second == (1 if kept else 0))
     def _():
@@ -489,18 +508,18 @@
     out_ref[...] = acc.astype(BF)
 
 
-def mlp(kept, start, meta, after, att_0, res_0, res_1, lates, weights):
+def mlp(kept, start, after, att_0, res_0, res_1, lates, weights):
     count = sum(x.shape[1] for x in lates)
     return pl.pallas_call(
         functools.partial(mlp_kernel, kept, start),
         out_shape=jax.ShapeDtypeStruct((count, D), BF),
-        in_specs=[SM, AN] + [VM] * (7 + len(lates)),
+        in_specs=[AN] + [VM] * (7 + len(lates)),
         out_specs=VM,
         scratch_shapes=[pltpu.VMEM((count, D), BF), pltpu.VMEM((count, D), BF)],
         compiler_params=params(20),
         cost_estimate=cost(count * 7e6, 6e6),
         name="mlp",
-    )(meta, after, att_0, res_0, res_1, *lates, *weights)
+    )(after, att_0, res_0, res_1, *lates, *weights)
 
 
 def exchange(x, pairs):
@@ -515,7 +534,6 @@
     c = lax.axis_index("cols")
     h = c // 2
     row_bits = (table.shape[0] - 1).bit_length()
-    meta = jnp.stack([c, jnp.where(h == 0, lengths[0], lengths[1])]).astype(I32)
 
     copies = jnp.broadcast_to(token_ids, (col_count, *token_ids.shape))
     ids = lax.all_to_all(copies, "cols", split_axis=0, concat_axis=0, tiled=True)
@@ -529,31 +547,32 @@
     got = got.reshape(owners * CAP, table.shape[1])
     slots = slots.reshape(-1)
 
-    theirs_0, wide = pick_first(meta, slots, got, half, quarter)
+    theirs_0, wide = pick_first(slots, got, half, quarter)
     crossed_0 = exchange(theirs_0, CROSS)
-    mine_0 = pick_more(meta, slots, wide, theirs_0, half, quarter, False, 0)
+    (mine_0,) = pick_more(slots, wide, theirs_0, half, quarter, ((False, 0),))
     swapped_0 = exchange(mine_0, SWAP)
-    theirs_1 = pick_more(meta, slots, wide, mine_0, half, quarter, True, 1)
+    (theirs_1,) = pick_more(slots, wide, mine_0, half, quarter, ((True, 1),))
     crossed_1 = exchange(theirs_1, CROSS)
     relayed_0 = exchange(crossed_0, SWAP)
-    mine_1 = pick_more(meta, slots, wide, crossed_0, half, quarter, False, 1)
+    (mine_1,) = pick_more(slots, wide, crossed_0, half, quarter, ((False, 1),))
     swapped_1 = exchange(mine_1, SWAP)
+    relayed_0, crossed_1 = lax.optimization_barrier((relayed_0, crossed_1))
     relayed_1 = exchange(crossed_1, SWAP)
 
-    gain = attn_gain.reshape(col_count, -1)
-    keys_0, values_0, own_w, att_0, res_0 = early(
-        meta, (mine_0, swapped_0, crossed_0, relayed_0), gain, w_qkv, quarter
+    gain = attn_gain.reshape(2, -1)
+    keys_0, values_0, att_0, res_0 = early(
+        lengths, (mine_0, swapped_0, crossed_0, relayed_0), gain, w_qkv, quarter
     )
     keys_1, values_1, q, att_1a, res_1 = late(
-        meta, (mine_1, swapped_1, crossed_1, relayed_1), gain, own_w, keys_0, values_0, quarter
+        lengths, (mine_1, swapped_1, crossed_1, relayed_1), gain, w_qkv, keys_0, values_0, quarter
     )
     weights = (w_out, mlp_gain.reshape(1, -1), w_in, w_down)
-    sent_a = mlp(False, 0, meta, res_1, att_0, res_0, res_1, (att_1a,), weights)
+    sent_a = mlp(False, 0, res_1, att_0, res_0, res_1, (att_1a,), weights)
     came_a = exchange(sent_a, CROSS)
-    att_1b = last(meta, q, keys_0, values_0, keys_1, values_1, sent_a)
-    sent_b = mlp(False, quarter // 2, meta, att_1b, att_0, res_0, res_1, (att_1b,), weights)
+    att_1b = last(lengths, q, keys_0, values_0, keys_1, values_1, sent_a)
+    sent_b = mlp(False, quarter // 2, att_1b, att_0, res_0, res_1, (att_1b,), weights)
     came_b = exchange(sent_b, CROSS)
-    kept = mlp(True, 0, meta, sent_b, att_0, res_0, res_1, (att_1a, att_1b), weights)
+    kept = mlp(True, 0, sent_b, att_0, res_0, res_1, (att_1a, att_1b), weights)
     which = lax.broadcasted_iota(I32, (batch_dev, quarter // 2, D), 0) == h
     return jnp.concatenate(
         [

time: 139 us -> 138 us (level)
  Pallas kernels: 53.1 us -> 48.9 us
  waiting for transfers between devices: 44.2 us -> 47.8 us
    all_to_all x1, waiting for transfers between devices: 36.5 us -> 38.3 us  [local(): lax.all_to_all(looked, 'rows', split_axis=0, concat_axis=0, tiled=True)]
    pallas_call x3, Pallas kernels: 12.1 us -> 10.3 us  [mlp(): pl.pallas_call(functools.partial(mlp_kernel, kept, start), out_shape=jax....]
    ppermute x8, waiting for transfers between devices: 7.71 us -> 9.51 us  [exchange(): return lax.ppermute(x, 'cols', pairs)]
    pallas_call x3, Pallas kernels: 6.38 us -> 4.76 us  [pick_more(): pl.pallas_call(functools.partial(pick_more_kernel, which), out_shape=[jax...]
  transfers between devices with their start and end apart: 9 -> 9, of which waited for: 6 -> 6; matrix products, arithmetic and copies ran while one was open for 1% -> 0% of each run, Pallas kernels for 21% -> 18%
where the time goes in v4:
time: 138 us
  Pallas kernels  48.9 us (35%)
  waiting for transfers between devices  47.8 us (35%)
  blocking collectives  25.2 us (18%)
  starting transfers between devices  13.3 us (10%)
    all_to_all x1, waiting for transfers between devices, local(): lax.all_to_all(looked, 'rows', split_axis=0, concat_axis=0, tiled=True)  38.3 us
    all_to_all x1, blocking collectives, local(): lax.all_to_all(requests.reshape(owners, REQ), 'rows', split_axis=0, conca...  14.7 us
    all_to_all x1, blocking collectives, local(): lax.all_to_all(copies, 'cols', split_axis=0, concat_axis=0, tiled=True)  10.6 us
    pallas_call x3, Pallas kernels, mlp(): pl.pallas_call(functools.partial(mlp_kernel, kept, start), out_shape=jax....  10.3 us
    pallas_call x1, Pallas kernels, lookup(): pl.pallas_call(lookup_kernel, out_shape=jax.ShapeDtypeStruct((owners, CAP...  10.1 us
    ppermute x8, waiting for transfers between devices, exchange(): return lax.ppermute(x, 'cols', pairs)  9.51 us
    ppermute x8, starting transfers between devices, exchange(): return lax.ppermute(x, 'cols', pairs)  9.19 us
    pallas_call x1, Pallas kernels, late(): pl.pallas_call(late_kernel, out_shape=(jax.ShapeDtypeStruct((4, half, 128...  7.78 us
  transfers between devices with their start and end apart: 9, of which 6 were waited for; matrix products, arithmetic and copies ran while one was open for 0% of the time, Pallas kernels for 18%

profile of v4, /device:TPU:0, one launch (start us, length us, event | category | flops | bytes accessed | tf_op | source)
XLA Modules:
  0.0 137.5 jit_solution(4472573700153713929)
XLA Ops:
  0.7 10.6 %all_to_all.19 = s32[4,2,512]{2,1,0:T(2,128)S(1)} all-to-all(s32[4,2,512]{2,1,0:T(2,128)S(1)} %broadcast_in_dim.33), channel_id=1, replica_groups=mesh['rows'=32,'cols'=4] {'cols'}, dimensions={0} | all-to-all | bytes 32768 | tf_op jit(solution)/shard_map/all_to_all | solution.py:539
  11.3 1.7 %route.1 = (s32[8,512]{1,0:T(8,128)S(1)}, s32[96,128]{1,0:T(8,128)S(1)}) custom-call(s32[8,512]{1,0:T(8,128)S(1)} %reshape.27.ids_ref), custom_call_target="tpu_custom_call" | custom-call | tf_op jit(solution)/shard_map/route/pallas_call | solution.py:84
  13.0 14.7 %all_to_all.20 = s32[32,1,384]{2,1,0:T(1,128)} all-to-all(s32[32,1,384]{2,1,0:T(1,128)S(1)} %bitcast.8), channel_id=1, replica_groups=mesh['rows'=32,'cols'=4] {'rows'}, dimensions={0} | all-to-all | bytes 98304 | tf_op jit(solution)/shard_map/all_to_all | solution.py:542
  27.7 10.1 %lookup.1 = bf16[32,344,128]{2,1,0:T(8,128)(2,1)} custom-call(s32[12288]{0:T(1024)} %bitcast.18, bf16[16384,128]{1,0:T(8,128)(2,1)} %table_ref.1), custom_call_target="tpu_custom_call" | custom-call | flops 6000000000 | bytes 4000000 | tf_op jit(solution)/shard_map/lookup/pallas_call | solution.py:173
  37.8 4.1 %all-to-all-start.2 = ((bf16[32,344,128]{2,1,0:T(8,128)(2,1)}), bf16[32,344,128]{2,1,0:T(8,128)(2,1)S(1)}, u32[]{:S(2)}, u32[]{:S(2)}) async-start(bf16[32,344,128]{2,1,0:T(8,128)(2,1)} %lookup.1), calls=%async_computation.2 | async-start | bytes 5636096 | tf_op jit(solution)/shard_map/all_to_all | solution.py:546
  41.9 38.3 %all-to-all-done.2 = bf16[32,344,128]{2,1,0:T(8,128)(2,1)S(1)} async-done(((bf16[32,344,128]{2,1,0:T(8,128)(2,1)}), bf16[32,344,128]{2,1,0:T(8,128)(2,1)S(1)}, u32[]{:S(2)}, u32[]{:S(2)}) %all-to-all-start.2) | async-done | bytes 2818080 | tf_op jit(solution)/shard_map/all_to_all | solution.py:546
  80.2 1.6 %pick_first.1 = (bf16[1024,128]{1,0:T(8,128)(2,1)S(1)}, f32[11008,128]{1,0:T(8,128)S(1)}) custom-call(s32[4096]{0:T(1024)S(1)} %bitcast.10, bf16[11008,128]{1,0:T(8,128)(2,1)S(1)} %bitcast.7), custom_call_target="tpu_custom_call" | custom-call | flops 3000000000 | bytes 4000000 | tf_op jit(solution)/shard_map/pick_first/pallas_call | solution.py:248
  81.8 1.2 collective-permute-start
  83.1 1.6 %pick_more.4.after_ref.s0 = bf16[1024,128]{1,0:T(8,128)(2,1)S(1)} custom-call(s32[4096]{0:T(1024)S(1)} %bitcast.11, f32[11008,128]{1,0:T(8,128)S(1)} %get-tuple-element.22.wide_ref, bf16[1024,128]{1,0:T(8,128)(2,1)S(1)} %get-tuple-element.23.after_ref), custom_call_target="tpu_custom_call" | custom-call | flops 2000000000 | bytes 4000000 | tf_op jit(solution)/shard_map/pick_more/pallas_call | solution.py:269
  84.7 1.6 %pick_more.5 = bf16[1024,128]{1,0:T(8,128)(2,1)S(1)} custom-call(s32[4096]{0:T(1024)S(1)} %bitcast.12, f32[11008,128]{1,0:T(8,128)S(1)} %get-tuple-element.22.wide_ref, bf16[1024,128]{1,0:T(8,128)(2,1)S(1)} %pick_more.4.after_ref.s0), custom_call_target="tpu_custom_call" | custom-call | flops 2000000000 | bytes 4000000 | tf_op jit(solution)/shard_map/pick_more/pallas_call | solution.py:269
  86.3 2.1 %collective-permute-start.3 = (bf16[1024,128]{1,0:T(8,128)(2,1)S(1)}, bf16[1024,128]{1,0:T(8,128)(2,1)S(1)}, u32[]{:S(2)}, u32[]{:S(2)}) collective-permute-start(bf16[1024,128]{1,0:T(8,128)(2,1)S(1)} %pick_more.5), channel_id=1, source_target_pairs={{0,3},{3,0},{1,2},{2,1},{4,7},{7,4},{5,6},{6,5},{8,11},{11,8},{9,1... | collective-permute-start | bytes 786440 | tf_op jit(solution)/shard_map/ppermute | solution.py:526
  88.5 2.7 %collective-permute-done.after_ref.s2 = bf16[1024,128]{1,0:T(8,128)(2,1)S(1)} collective-permute-done((bf16[1024,128]{1,0:T(8,128)(2,1)S(1)}, bf16[1024,128]{1,0:T(8,128)(2,1)S(1)}, u32[]{:S(2)}, u32[]{:S(2)}) %collective-permute-start) | collective-permute-done | bytes 262176 | tf_op jit(solution)/shard_map/ppermute | solution.py:526
  91.2 1.6 %pick_more.3.s0 = bf16[1024,128]{1,0:T(8,128)(2,1)S(1)} custom-call(s32[4096]{0:T(1024)S(1)} %bitcast.13, f32[11008,128]{1,0:T(8,128)S(1)} %get-tuple-element.22.wide_ref, bf16[1024,128]{1,0:T(8,128)(2,1)S(1)} %collective-permute-done.after_ref.s2), custom_call_target="tpu_custom_call" | custom-call | flops 2000000000 | bytes 4000000 | tf_op jit(solution)/shard_map/pick_more/pallas_call | solution.py:269
  92.8 2.1 %collective-permute-start.1 = (bf16[1024,128]{1,0:T(8,128)(2,1)S(1)}, bf16[1024,128]{1,0:T(8,128)(2,1)S(1)}, u32[]{:S(2)}, u32[]{:S(2)}) collective-permute-start(bf16[1024,128]{1,0:T(8,128)(2,1)S(1)} %pick_more.3.s0), channel_id=1, source_target_pairs={{0,1},{1,0},{2,3},{3,2},{4,5},{5,4},{6,7},{7,6},{8,9},{9,8},{10,11... | collective-permute-start | bytes 786440 | tf_op jit(solution)/shard_map/ppermute | solution.py:526
  95.1 5.2 %collective-permute-done.2.s3 = bf16[1024,128]{1,0:T(8,128)(2,1)S(1)} collective-permute-done((bf16[1024,128]{1,0:T(8,128)(2,1)S(1)}, bf16[1024,128]{1,0:T(8,128)(2,1)S(1)}, u32[]{:S(2)}, u32[]{:S(2)}) %collective-permute-start.2) | collective-permute-done | bytes 262176 | tf_op jit(solution)/shard_map/ppermute | solution.py:526
  100.4 7.3 %early.1 = (bf16[4,1024,128]{2,1,0:T(8,128)(2,1)S(1)}, bf16[4,1024,256]{2,1,0:T(8,128)(2,1)S(1)}, bf16[4,512,128]{2,1,0:T(8,128)(2,1)S(1)}, bf16[512,512]{1,0:T(8,128)(2,1)S(1)}) custom-call(s32[2]{0:T(128)S(1)} %copy-done.5, bf16[1024,128]{1,0:T(8,128)(2,1)S(1)} %pick_more.4.after_ref.s0, bf16[1024,128]{1,0:T(8,128)(2,1)S(1)} %collective-permute-done.5.s1, ...), custom_call_target="tpu_custom_call" | custom-call | flops 7000000000 | bytes 6000000 | tf_op jit(solution)/shard_map/early/pallas_call | solution.py:417
  108.0 7.8 %late.1 = (bf16[4,1024,128]{2,1,0:T(8,128)(2,1)S(1)}, bf16[4,1024,256]{2,1,0:T(8,128)(2,1)S(1)}, bf16[4,512,128]{2,1,0:T(8,128)(2,1)S(1)}, bf16[4,256,128]{2,1,0:T(8,128)(2,1)S(1)}, bf16[512,512]{1,0:T(8,128)(2,1)S(1)}) custom-call(s32[2]{0:T(128)S(1)} %copy-done.5, bf16[1024,128]{1,0:T(8,128)(2,1)S(1)} %pick_more.3.s0, ...), custom_call_target="tpu_custom_call" | custom-call | flops 7000000000 | bytes 6000000 | tf_op jit(solution)/shard_map/late/pallas_call | solution.py:440
  115.8 2.7 %mlp.3.after_ref = bf16[256,512]{1,0:T(8,128)(2,1)S(1)} custom-call(bf16[512,512]{1,0:T(8,128)(2,1)S(1)} %get-tuple-element.31.after_ref.res1_ref, bf16[4,512,128]{2,1,0:T(8,128)(2,1)S(1)} %get-tuple-element.32.early_ref, bf16[512,512]{1,0:T(8,128)(2,1)S(1)} %get-tuple-element.33.res0_ref, bf16[512,512]{1,0:T(8,128)(2,1)S(1)} %get-tuple-element.31.after_ref.res1_ref, ...), custom_call_target="tpu_custom_call" | custom-call | flops 1792000000 | bytes 6000000 | tf_op jit(solution)/shard_map/mlp/pallas_call | solution.py:513
  118.5 1.9 %collective-permute-start.6 = (bf16[256,512]{1,0:T(8,128)(2,1)S(1)}, bf16[256,512]{1,0:T(8,128)(2,1)S(1)}, u32[]{:S(2)}, u32[]{:S(2)}) collective-permute-start(bf16[256,512]{1,0:T(8,128)(2,1)S(1)} %mlp.3.after_ref), channel_id=1, source_target_pairs={{0,3},{3,0},{1,2},{2,1},{4,7},{7,4},{5,6},{6,5},{8,11},{11,8},{9,1... | collective-permute-start | bytes 786440 | tf_op jit(solution)/shard_map/ppermute | solution.py:526
  120.4 5.5 %last.1.after_ref.refs_0_.refs_1_ = bf16[4,256,128]{2,1,0:T(8,128)(2,1)S(1)} custom-call(s32[2]{0:T(128)S(1)} %copy-done.5, bf16[4,512,128]{2,1,0:T(8,128)(2,1)S(1)} %get-tuple-element.28.q_ref, bf16[4,1024,128]{2,1,0:T(8,128)(2,1)S(1)} %get-tuple-element.26.k0_ref, bf16[4,1024,256]{2,1,0:T(8,128)(2,1)S(1)} %get-tuple-element.27.v0_ref, ...), custom_call_target="tpu_custom_call" | custom-call | flops 5000000000 | bytes 6000000 | tf_op jit(solution)/shard_map/last/pallas_call | solution.py:463
  125.9 2.7 %mlp.4.after_ref = bf16[256,512]{1,0:T(8,128)(2,1)S(1)} custom-call(bf16[4,256,128]{2,1,0:T(8,128)(2,1)S(1)} %last.1.after_ref.refs_0_.refs_1_, bf16[4,512,128]{2,1,0:T(8,128)(2,1)S(1)} %get-tuple-element.32.early_ref, bf16[512,512]{1,0:T(8,128)(2,1)S(1)} %get-tuple-element.33.res0_ref, bf16[512,512]{1,0:T(8,128)(2,1)S(1)} %get-tuple-element.31.after_ref.res1_ref, ...), custom_call_target="tpu_custom_call" | custom-call | flops 1792000000 | bytes 6000000 | tf_op jit(solution)/shard_map/mlp/pallas_call | solution.py:513
  128.6 1.7 %collective-permute-start.7 = (bf16[256,512]{1,0:T(8,128)(2,1)S(1)}, bf16[256,512]{1,0:T(8,128)(2,1)S(1)}, u32[]{:S(2)}, u32[]{:S(2)}) collective-permute-start(bf16[256,512]{1,0:T(8,128)(2,1)S(1)} %mlp.4.after_ref), channel_id=1, source_target_pairs={{0,3},{3,0},{1,2},{2,1},{4,7},{7,4},{5,6},{6,5},{8,11},{11,8},{9,1... | collective-permute-start | bytes 786440 | tf_op jit(solution)/shard_map/ppermute | solution.py:526
  130.3 4.9 %mlp.5 = bf16[512,512]{1,0:T(8,128)(2,1)S(1)} custom-call(bf16[256,512]{1,0:T(8,128)(2,1)S(1)} %mlp.4.after_ref, bf16[4,512,128]{2,1,0:T(8,128)(2,1)S(1)} %get-tuple-element.32.early_ref, bf16[512,512]{1,0:T(8,128)(2,1)S(1)} %get-tuple-element.33.res0_ref, bf16[512,512]{1,0:T(8,128)(2,1)S(1)} %get-tuple-element.31.after_ref.res1_ref, ...), custom_call_target="tpu_custom_call" | custom-call | flops 3584000000 | bytes 6000000 | tf_op jit(solution)/shard_map/mlp/pallas_call | solution.py:513
  135.2 1.1 collective-permute-done.7
  (31 shorter events, 2.6 us)
Async XLA Ops:
  37.7 4.1 %copy-start.6 = (f32[512]{0:T(512)S(1)}, f32[512]{0:T(512)}, u32[]{:S(2)}) copy-start(f32[512]{0:T(512)} %param.12) | copy-start | bytes 6148
  37.8 42.5 %all-to-all-start.2 = ((bf16[32,344,128]{2,1,0:T(8,128)(2,1)}), bf16[32,344,128]{2,1,0:T(8,128)(2,1)S(1)}, u32[]{:S(2)}, u32[]{:S(2)}) async-start(bf16[32,344,128]{2,1,0:T(8,128)(2,1)} %lookup.1), calls=%async_computation.2 | async-start | bytes 5636096 | tf_op jit(solution)/shard_map/all_to_all | solution.py:546
  81.8 9.3 %collective-permute-start = (bf16[1024,128]{1,0:T(8,128)(2,1)S(1)}, bf16[1024,128]{1,0:T(8,128)(2,1)S(1)}, u32[]{:S(2)}, u32[]{:S(2)}) collective-permute-start(bf16[1024,128]{1,0:T(8,128)(2,1)S(1)} %get-tuple-element.23.after_ref), channel_id=1, source_target_pairs={{0,3},{3,0},{1,2},{2,1},{4,7},{7,4},{5,6},{6,5},{8,11},{11,8},{9,1... | collective-permute-start | bytes 786440 | tf_op jit(solution)/shard_map/ppermute | solution.py:526
  84.6 15.7 %collective-permute-start.5 = (bf16[1024,128]{1,0:T(8,128)(2,1)S(1)}, bf16[1024,128]{1,0:T(8,128)(2,1)S(1)}, u32[]{:S(2)}, u32[]{:S(2)}) collective-permute-start(bf16[1024,128]{1,0:T(8,128)(2,1)S(1)} %pick_more.4.after_ref.s0), channel_id=1, source_target_pairs={{0,1},{1,0},{2,3},{3,2},{4,5},{5,4},{6,7},{7,6},{8,9},{9,8},{10,11... | collective-permute-start | bytes 786440 | tf_op jit(solution)/shard_map/ppermute | solution.py:526
  86.3 8.8 %collective-permute-start.3 = (bf16[1024,128]{1,0:T(8,128)(2,1)S(1)}, bf16[1024,128]{1,0:T(8,128)(2,1)S(1)}, u32[]{:S(2)}, u32[]{:S(2)}) collective-permute-start(bf16[1024,128]{1,0:T(8,128)(2,1)S(1)} %pick_more.5), channel_id=1, source_target_pairs={{0,3},{3,0},{1,2},{2,1},{4,7},{7,4},{5,6},{6,5},{8,11},{11,8},{9,1... | collective-permute-start | bytes 786440 | tf_op jit(solution)/shard_map/ppermute | solution.py:526
  91.2 9.2 %collective-permute-start.2 = (bf16[1024,128]{1,0:T(8,128)(2,1)S(1)}, bf16[1024,128]{1,0:T(8,128)(2,1)S(1)}, u32[]{:S(2)}, u32[]{:S(2)}) collective-permute-start(bf16[1024,128]{1,0:T(8,128)(2,1)S(1)} %collective-permute-done.after_ref.s2), channel_id=1, source_target_pairs={{0,1},{1,0},{2,3},{3,2},{4,5},{5,4},{6,7},{7,6},{8,9},{9,8},{10,11... | collective-permute-start | bytes 786440 | tf_op jit(solution)/shard_map/ppermute | solution.py:526
  91.2 9.2 %copy-start.4 = (bf16[512,1536]{1,0:T(8,128)(2,1)S(1)}, bf16[512,1536]{1,0:T(8,128)(2,1)}, u32[]{:S(2)}) copy-start(bf16[512,1536]{1,0:T(8,128)(2,1)} %w_ref.3) | copy-start | bytes 4718596
  91.2 9.2 %copy-start.5 = (s32[2]{0:T(128)S(1)}, s32[2]{0:T(128)}, u32[]{:S(2)}) copy-start(s32[2]{0:T(128)} %length_ref.5) | copy-start | bytes 28
  92.8 14.9 %collective-permute-start.1 = (bf16[1024,128]{1,0:T(8,128)(2,1)S(1)}, bf16[1024,128]{1,0:T(8,128)(2,1)S(1)}, u32[]{:S(2)}, u32[]{:S(2)}) collective-permute-start(bf16[1024,128]{1,0:T(8,128)(2,1)S(1)} %pick_more.3.s0), channel_id=1, source_target_pairs={{0,1},{1,0},{2,3},{3,2},{4,5},{5,4},{6,7},{7,6},{8,9},{9,8},{10,11... | collective-permute-start | bytes 786440 | tf_op jit(solution)/shard_map/ppermute | solution.py:526
  100.3 7.6 %collective-permute-start.4 = (bf16[1024,128]{1,0:T(8,128)(2,1)S(1)}, bf16[1024,128]{1,0:T(8,128)(2,1)S(1)}, u32[]{:S(2)}, u32[]{:S(2)}) collective-permute-start(bf16[1024,128]{1,0:T(8,128)(2,1)S(1)} %collective-permute-done.3.s2), channel_id=1, source_target_pairs={{0,1},{1,0},{2,3},{3,2},{4,5},{5,4},{6,7},{7,6},{8,9},{9,8},{10,11... | collective-permute-start | bytes 786440 | tf_op jit(solution)/shard_map/ppermute | solution.py:526
  107.9 7.8 %copy-start = (bf16[512,4096]{1,0:T(8,128)(2,1)S(1)}, bf16[512,4096]{1,0:T(8,128)(2,1)}, u32[]{:S(2)}) copy-start(bf16[512,4096]{1,0:T(8,128)(2,1)} %refs_4_.5) | copy-start | bytes 12582916
  108.0 7.8 %copy-start.1 = (bf16[2048,512]{1,0:T(8,128)(2,1)S(1)}, bf16[2048,512]{1,0:T(8,128)(2,1)}, u32[]{:S(2)}) copy-start(bf16[2048,512]{1,0:T(8,128)(2,1)} %refs_5_.1) | copy-start | bytes 6291460
  108.0 7.8 %copy-start.2 = (bf16[512,512]{1,0:T(8,128)(2,1)S(1)}, bf16[512,512]{1,0:T(8,128)(2,1)}, u32[]{:S(2)}) copy-start(bf16[512,512]{1,0:T(8,128)(2,1)} %refs_2_.1) | copy-start | bytes 1572868
  108.0 7.8 %copy-start.3 = (f32[512]{0:T(512)S(1)}, f32[512]{0:T(512)}, u32[]{:S(2)}) copy-start(f32[512]{0:T(512)} %param.15) | copy-start | bytes 6148
  118.5 17.8 %collective-permute-start.6 = (bf16[256,512]{1,0:T(8,128)(2,1)S(1)}, bf16[256,512]{1,0:T(8,128)(2,1)S(1)}, u32[]{:S(2)}, u32[]{:S(2)}) collective-permute-start(bf16[256,512]{1,0:T(8,128)(2,1)S(1)} %mlp.3.after_ref), channel_id=1, source_target_pairs={{0,3},{3,0},{1,2},{2,1},{4,7},{7,4},{5,6},{6,5},{8,11},{11,8},{9,1... | collective-permute-start | bytes 786440 | tf_op jit(solution)/shard_map/ppermute | solution.py:526
  128.6 7.7 %collective-permute-start.7 = (bf16[256,512]{1,0:T(8,128)(2,1)S(1)}, bf16[256,512]{1,0:T(8,128)(2,1)S(1)}, u32[]{:S(2)}, u32[]{:S(2)}) collective-permute-start(bf16[256,512]{1,0:T(8,128)(2,1)S(1)} %mlp.4.after_ref), channel_id=1, source_target_pairs={{0,3},{3,0},{1,2},{2,1},{4,7},{7,4},{5,6},{6,5},{8,11},{11,8},{9,1... | collective-permute-start | bytes 786440 | tf_op jit(solution)/shard_map/ppermute | solution.py:526

commit v5 on v4

--- a/solution.py
+++ b/solution.py
@@ -132,21 +132,20 @@
         start = d * REQ
         groups = lax.shift_right_logical(ask_ref[start] + 31, 5)
 
+        def narrow(i):
+            at = pl.ds(pl.multiple_of(i * 32, 32), 32)
+            send_ref[d, at, :] = row_ref[at, :].astype(BF)
+
         def some(i, _):
             base = pl.multiple_of(i * 32, 32)
             first = start + base + 1
+            narrow(jnp.maximum(i - 1, 0))
             for k in range(32):
                 row_ref[pl.ds(base + k, 1), :] = wide_ref[pl.ds(ask_ref[first + k], 1), :]
             return 0
 
         lax.fori_loop(0, groups, some, 0)
-
-        def narrow(i, _):
-            at = pl.ds(pl.multiple_of(i * 32, 32), 32)
-            send_ref[d, at, :] = row_ref[at, :].astype(BF)
-            return 0
-
-        lax.fori_loop(0, jnp.minimum(groups, CAP // 32), narrow, 0)
+        narrow(jnp.clip(groups - 1, 0, CAP // 32 - 1))
 
         @pl.when(groups > CAP // 32)
         def _():
@@ -282,7 +281,7 @@
     )(slots, wide, after)
 
 
-def project(c, slices, gain_ref, w_ref, norm_ref, k_ref, v_ref, res_ref, mine):
+def project(c, slices, gain_ref, w_ref, wv_ref, norm_ref, k_ref, v_ref, res_ref, mine):
     n = norm_ref.shape[1]
     odd = c & 1
     first = lax.shift_right_logical(c, 1)
@@ -312,14 +311,17 @@
         ]
         norm_ref[b, :, 0:256] = normed[0]
         norm_ref[b, :, 256:512] = normed[1]
-        for pair in range(4):
-            if pair % 2 == 0:
-                keys = project_rows(normed, slice(D + pair * 128, D + pair * 128 + 256))
-                values = project_rows(normed, slice(2 * D + pair * 128, 2 * D + pair * 128 + 256))
-            part = slice(pair % 2 * 128, pair % 2 * 128 + 128)
-            k_ref[pair, rows, :] = keys[:, part].astype(BF)
-            v_ref[pair, rows, 0:128] = values[:, part].astype(BF)
-            v_ref[pair, rows, 128:256] = jnp.ones((n, 128), BF)
+        for pair in range(0, 4, 2):
+            keys = project_rows(normed, slice(D + pair * 128, D + pair * 128 + 256))
+            k_ref[pair, rows, :] = keys[:, 0:128].astype(BF)
+            k_ref[pair + 1, rows, :] = keys[:, 128:256].astype(BF)
+            cols = slice(pair * 128, pair * 128 + 256)
+            values = dot_t(wv_ref[cols, w_rows[0]], normed[0]) + dot_t(
+                wv_ref[cols, w_rows[1]], normed[1]
+            )
+            for i in range(4):
+                v_ref[2 * pair + i, 0:64, rows] = values[64 * i : 64 * i + 64, :].astype(BF)
+                v_ref[2 * pair + i, 64:80, rows] = jnp.ones((16, n), BF)
     chosen = (norm_ref[mine, :, 0:256], norm_ref[mine, :, 256:512])
     return (project_rows(chosen, slice(0, D)) * (0.125 * LOG2E)).astype(BF)
 
@@ -348,30 +350,30 @@
 
         def body(n):
             qp = q_ref[pair, rows, :]
-            limit = jnp.minimum(block * size + row + 1, length) - (n - 1) * size
+            limit = jnp.minimum(block * size + col + 1, length) - (n - 1) * size
             tops = []
             for head in range(2):
                 qh = jnp.where((lane < 64) == (head == 0), qp, jnp.zeros_like(qp))
                 m = None
                 for j in range(n):
                     at = slice(j % per_half * size, j % per_half * size + size)
-                    s = dot_t(qh, keys[j // per_half][pair, at, :])
+                    s = dot_t(keys[j // per_half][pair, at, :], qh)
                     if j == n - 1:
-                        s = jnp.where(col < limit, s, -1e30)
+                        s = jnp.where(row < limit, s, -1e30)
                     s_ref[head, j] = s
-                    t = jnp.maximum(s[:, 0:128], s[:, 128:256])
+                    t = jnp.max(s.reshape(size // 8, 8, size), axis=0)
                     m = t if m is None else jnp.maximum(m, t)
-                tops.append(jnp.max(m, axis=1, keepdims=True))
+                tops.append(jnp.max(m, axis=0, keepdims=True))
             outs = []
             for head in range(2):
                 acc = None
                 for j in range(n):
                     at = slice(j % per_half * size, j % per_half * size + size)
                     p = jnp.exp2(s_ref[head, j] - tops[head]).astype(BF)
-                    d = dot(p, values[j // per_half][pair, at, :])
+                    d = dot(values[j // per_half][2 * pair + head, :, at], p)
                     acc = d if acc is None else acc + d
-                outs.append(acc[:, :128] / acc[:, 128:])
-            out_ref[pair, put, :] = jnp.where(lane < 64, outs[0], outs[1]).astype(BF)
+                outs.append(acc[0:64, :] / acc[64:65, :])
+            out_ref[pair, put, :] = jnp.transpose(jnp.concatenate(outs, axis=0)).astype(BF)
 
         for n in range(1, s_ref.shape[1] + 1):
             pl.when(need == n)(functools.partial(body, n))
@@ -381,23 +383,25 @@
 
 
 def early_kernel(
-    length_ref, s0, s1, s2, s3, gain_ref, w_ref,
+    length_ref, s0, s1, s2, s3, gain_ref, w_ref, wv_ref,
     k_ref, v_ref, att_ref, res_ref, norm_ref, q_ref, s_ref,
 ):
     c = lax.axis_index("cols")
     quarter = jnp.minimum(c, 3 - c)
-    q = project(c, (s0, s1, s2, s3), gain_ref, w_ref, norm_ref, k_ref, v_ref, res_ref, quarter)
+    q = project(c, (s0, s1, s2, s3), gain_ref, w_ref, wv_ref, norm_ref, k_ref, v_ref, res_ref, quarter)
     keep_queries(q, q_ref)
     attend(quarter, length_ref[c // 2], q_ref, (k_ref,), (v_ref,), s_ref, att_ref)
 
 
 def late_kernel(
-    length_ref, s0, s1, s2, s3, gain_ref, w_ref, k0_ref, v0_ref,
+    length_ref, s0, s1, s2, s3, gain_ref, w_ref, wv_ref, k0_ref, v0_ref,
     k_ref, v_ref, q_ref, att_ref, res_ref, norm_ref, s_ref,
 ):
     c = lax.axis_index("cols")
     quarter = jnp.maximum(c, 3 - c)
-    q = project(c, (s0, s1, s2, s3), gain_ref, w_ref, norm_ref, k_ref, v_ref, res_ref, quarter - 2)
+    q = project(
+        c, (s0, s1, s2, s3), gain_ref, w_ref, wv_ref, norm_ref, k_ref, v_ref, res_ref, quarter - 2
+    )
     keep_queries(q, q_ref)
     attend(
         quarter, length_ref[c // 2], q_ref, (k0_ref, k_ref), (v0_ref, v_ref), s_ref, att_ref
@@ -412,17 +416,17 @@
     )
 
 
-def early(lengths, slices, gain, w_qkv, quarter):
+def early(lengths, slices, gain, w_qkv, w_values, quarter):
     half = 2 * quarter
     return pl.pallas_call(
         early_kernel,
         out_shape=(
             jax.ShapeDtypeStruct((4, half, 128), BF),
-            jax.ShapeDtypeStruct((4, half, 256), BF),
+            jax.ShapeDtypeStruct((8, 80, half), BF),
             jax.ShapeDtypeStruct((4, quarter, 128), BF),
             jax.ShapeDtypeStruct((quarter, D), BF),
         ),
-        in_specs=[SM] + [VM] * 6,
+        in_specs=[SM] + [VM] * 7,
         out_specs=(VM,) * 4,
         scratch_shapes=[
             pltpu.VMEM((2, quarter, D), BF),
@@ -432,21 +436,21 @@
         compiler_params=params(20),
         cost_estimate=cost(7e9, 6e6),
         name="early",
-    )(lengths, *slices, gain, w_qkv)
-
-
-def late(lengths, slices, gain, w_qkv, keys, values, quarter):
+    )(lengths, *slices, gain, w_qkv, w_values)
+
+
+def late(lengths, slices, gain, w_qkv, w_values, keys, values, quarter):
     half = 2 * quarter
     return pl.pallas_call(
         late_kernel,
         out_shape=(
             jax.ShapeDtypeStruct((4, half, 128), BF),
-            jax.ShapeDtypeStruct((4, half, 256), BF),
+            jax.ShapeDtypeStruct((8, 80, half), BF),
             jax.ShapeDtypeStruct((4, quarter, 128), BF),
             jax.ShapeDtypeStruct((4, quarter // 2, 128), BF),
             jax.ShapeDtypeStruct((quarter, D), BF),
         ),
-        in_specs=[SM] + [VM] * 8,
+        in_specs=[SM] + [VM] * 9,
         out_specs=(VM,) * 5,
         scratch_shapes=[
             pltpu.VMEM((2, quarter, D), BF),
@@ -455,7 +459,7 @@
         compiler_params=params(22),
         cost_estimate=cost(7e9, 6e6),
         name="late",
-    )(lengths, *slices, gain, w_qkv, keys, values)
+    )(lengths, *slices, gain, w_qkv, w_values, keys, values)
 
 
 def last(lengths, q, keys_0, values_0, keys_1, values_1, after):
@@ -560,11 +564,12 @@
     relayed_1 = exchange(crossed_1, SWAP)
 
     gain = attn_gain.reshape(2, -1)
+    w_values = jnp.transpose(w_qkv[:, 2 * D :])
     keys_0, values_0, att_0, res_0 = early(
-        lengths, (mine_0, swapped_0, crossed_0, relayed_0), gain, w_qkv, quarter
+        lengths, (mine_0, swapped_0, crossed_0, relayed_0), gain, w_qkv, w_values, quarter
     )
     keys_1, values_1, q, att_1a, res_1 = late(
-        lengths, (mine_1, swapped_1, crossed_1, relayed_1), gain, w_qkv, keys_0, values_0, quarter
+        lengths, (mine_1, swapped_1, crossed_1, relayed_1), gain, w_qkv, w_values, keys_0, values_0, quarter
     )
     weights = (w_out, mlp_gain.reshape(1, -1), w_in, w_down)
     sent_a = mlp(False, 0, res_1, att_0, res_0, res_1, (att_1a,), weights)

time: 138 us -> 136 us (0.986)
  waiting for transfers between devices: 47.8 us -> 44.5 us
  local copies, waits for them, and re-layouts: 0.8 us -> 3.92 us
  Pallas kernels: 48.9 us -> 46.4 us
    all_to_all x1, waiting for transfers between devices: 38.3 us -> 35.2 us  [local(): lax.all_to_all(looked, 'rows', split_axis=0, concat_axis=0, tiled=True)]
    slice x0 -> x1, local copies, waits for them, and re-layouts: none -> 1.87 us  [local(): w_values = jnp.transpose(w_qkv[:, 2 * D:])]
  transfers between devices with their start and end apart: 9 -> 9, of which waited for: 6 -> 6; matrix products, arithmetic and copies ran while one was open for 0% -> 2% of each run, Pallas kernels for 18% -> 18%
where the time goes in v5:
time: 136 us
  Pallas kernels  46.4 us (34%)
  waiting for transfers between devices  44.5 us (33%)
  blocking collectives  25.2 us (19%)
  starting transfers between devices  14.2 us (10%)
  local copies, waits for them, and re-layouts  3.92 us (3%)
    all_to_all x1, waiting for transfers between devices, local(): lax.all_to_all(looked, 'rows', split_axis=0, concat_axis=0, tiled=True)  35.2 us
    all_to_all x1, blocking collectives, local(): lax.all_to_all(requests.reshape(owners, REQ), 'rows', split_axis=0, conca...  14.7 us
    all_to_all x1, blocking collectives, local(): lax.all_to_all(copies, 'cols', split_axis=0, concat_axis=0, tiled=True)  10.6 us
    ppermute x8, starting transfers between devices, exchange(): return lax.ppermute(x, 'cols', pairs)  10.1 us
    pallas_call x3, Pallas kernels, mlp(): pl.pallas_call(functools.partial(mlp_kernel, kept, start), out_shape=jax....  9.94 us
    ppermute x8, waiting for transfers between devices, exchange(): return lax.ppermute(x, 'cols', pairs)  9.27 us
    pallas_call x1, Pallas kernels, lookup(): pl.pallas_call(lookup_kernel, out_shape=jax.ShapeDtypeStruct((owners, CAP...  8.83 us
    pallas_call x1, Pallas kernels, early(): pl.pallas_call(early_kernel, out_shape=(jax.ShapeDtypeStruct((4, half, 12...  7.45 us
  transfers between devices with their start and end apart: 9, of which 6 were waited for; matrix products, arithmetic and copies ran while one was open for 2% of the time, Pallas kernels for 18%

profile of v5, /device:TPU:0, one launch (start us, length us, event | category | flops | bytes accessed | tf_op | source)
XLA Modules:
  0.0 135.7 jit_solution(4546894586915990722)
XLA Ops:
  0.7 10.6 %all_to_all.19 = s32[4,2,512]{2,1,0:T(2,128)S(1)} all-to-all(s32[4,2,512]{2,1,0:T(2,128)S(1)} %broadcast_in_dim.33), channel_id=1, replica_groups=mesh['rows'=32,'cols'=4] {'cols'}, dimensions={0} | all-to-all | bytes 32768 | tf_op jit(solution)/shard_map/all_to_all | solution.py:543
  11.3 1.7 %route.1 = (s32[8,512]{1,0:T(8,128)S(1)}, s32[96,128]{1,0:T(8,128)S(1)}) custom-call(s32[8,512]{1,0:T(8,128)S(1)} %reshape.27.ids_ref), custom_call_target="tpu_custom_call" | custom-call | tf_op jit(solution)/shard_map/route/pallas_call | solution.py:84
  13.0 14.7 %all_to_all.20 = s32[32,1,384]{2,1,0:T(1,128)} all-to-all(s32[32,1,384]{2,1,0:T(1,128)S(1)} %bitcast.11), channel_id=1, replica_groups=mesh['rows'=32,'cols'=4] {'rows'}, dimensions={0} | all-to-all | bytes 98304 | tf_op jit(solution)/shard_map/all_to_all | solution.py:546
  27.7 8.8 %lookup.1 = bf16[32,344,128]{2,1,0:T(8,128)(2,1)} custom-call(s32[12288]{0:T(1024)} %bitcast.21, bf16[16384,128]{1,0:T(8,128)(2,1)} %table_ref.1), custom_call_target="tpu_custom_call" | custom-call | flops 6000000000 | bytes 4000000 | tf_op jit(solution)/shard_map/lookup/pallas_call | solution.py:172
  36.5 4.1 %all-to-all-start.2 = ((bf16[32,344,128]{2,1,0:T(8,128)(2,1)}), bf16[32,344,128]{2,1,0:T(8,128)(2,1)S(1)}, u32[]{:S(2)}, u32[]{:S(2)}) async-start(bf16[32,344,128]{2,1,0:T(8,128)(2,1)} %lookup.1), calls=%async_computation.2 | async-start | bytes 5636096 | tf_op jit(solution)/shard_map/all_to_all | solution.py:550
  40.6 1.9 %slice.9 = bf16[512,512]{1,0:T(8,128)(2,1)} slice(bf16[512,1536]{1,0:T(8,128)(2,1)} %w_ref.3), slice={[0:512], [1024:1536]} | slice | bytes 1048576 | tf_op jit(solution)/shard_map/slice | solution.py:567
  42.5 1.3 copy.14
  43.8 35.2 %all-to-all-done.2 = bf16[32,344,128]{2,1,0:T(8,128)(2,1)S(1)} async-done(((bf16[32,344,128]{2,1,0:T(8,128)(2,1)}), bf16[32,344,128]{2,1,0:T(8,128)(2,1)S(1)}, u32[]{:S(2)}, u32[]{:S(2)}) %all-to-all-start.2) | async-done | bytes 2818080 | tf_op jit(solution)/shard_map/all_to_all | solution.py:550
  79.0 1.6 %pick_first.1 = (bf16[1024,128]{1,0:T(8,128)(2,1)S(1)}, f32[11008,128]{1,0:T(8,128)S(1)}) custom-call(s32[4096]{0:T(1024)S(1)} %bitcast.13, bf16[11008,128]{1,0:T(8,128)(2,1)S(1)} %bitcast.8), custom_call_target="tpu_custom_call" | custom-call | flops 3000000000 | bytes 4000000 | tf_op jit(solution)/shard_map/pick_first/pallas_call | solution.py:247
  81.8 1.6 %pick_more.4.after_ref.s0 = bf16[1024,128]{1,0:T(8,128)(2,1)S(1)} custom-call(s32[4096]{0:T(1024)S(1)} %bitcast.14, f32[11008,128]{1,0:T(8,128)S(1)} %get-tuple-element.22.wide_ref, bf16[1024,128]{1,0:T(8,128)(2,1)S(1)} %get-tuple-element.23.after_ref), custom_call_target="tpu_custom_call" | custom-call | flops 2000000000 | bytes 4000000 | tf_op jit(solution)/shard_map/pick_more/pallas_call | solution.py:268
  83.5 1.6 %pick_more.5 = bf16[1024,128]{1,0:T(8,128)(2,1)S(1)} custom-call(s32[4096]{0:T(1024)S(1)} %bitcast.15, f32[11008,128]{1,0:T(8,128)S(1)} %get-tuple-element.22.wide_ref, bf16[1024,128]{1,0:T(8,128)(2,1)S(1)} %pick_more.4.after_ref.s0), custom_call_target="tpu_custom_call" | custom-call | flops 2000000000 | bytes 4000000 | tf_op jit(solution)/shard_map/pick_more/pallas_call | solution.py:268
  85.1 2.1 %collective-permute-start.3 = (bf16[1024,128]{1,0:T(8,128)(2,1)S(1)}, bf16[1024,128]{1,0:T(8,128)(2,1)S(1)}, u32[]{:S(2)}, u32[]{:S(2)}) collective-permute-start(bf16[1024,128]{1,0:T(8,128)(2,1)S(1)} %pick_more.5), channel_id=1, source_target_pairs={{0,3},{3,0},{1,2},{2,1},{4,7},{7,4},{5,6},{6,5},{8,11},{11,8},{9,1... | collective-permute-start | bytes 786440 | tf_op jit(solution)/shard_map/ppermute | solution.py:530
  87.3 2.7 %collective-permute-done.after_ref.s2 = bf16[1024,128]{1,0:T(8,128)(2,1)S(1)} collective-permute-done((bf16[1024,128]{1,0:T(8,128)(2,1)S(1)}, bf16[1024,128]{1,0:T(8,128)(2,1)S(1)}, u32[]{:S(2)}, u32[]{:S(2)}) %collective-permute-start) | collective-permute-done | bytes 262176 | tf_op jit(solution)/shard_map/ppermute | solution.py:530
  90.0 1.6 %pick_more.3.s0 = bf16[1024,128]{1,0:T(8,128)(2,1)S(1)} custom-call(s32[4096]{0:T(1024)S(1)} %bitcast.16, f32[11008,128]{1,0:T(8,128)S(1)} %get-tuple-element.22.wide_ref, bf16[1024,128]{1,0:T(8,128)(2,1)S(1)} %collective-permute-done.after_ref.s2), custom_call_target="tpu_custom_call" | custom-call | flops 2000000000 | bytes 4000000 | tf_op jit(solution)/shard_map/pick_more/pallas_call | solution.py:268
  91.6 2.1 %collective-permute-start.1 = (bf16[1024,128]{1,0:T(8,128)(2,1)S(1)}, bf16[1024,128]{1,0:T(8,128)(2,1)S(1)}, u32[]{:S(2)}, u32[]{:S(2)}) collective-permute-start(bf16[1024,128]{1,0:T(8,128)(2,1)S(1)} %pick_more.3.s0), channel_id=1, source_target_pairs={{0,1},{1,0},{2,3},{3,2},{4,5},{5,4},{6,7},{7,6},{8,9},{9,8},{10,11... | collective-permute-start | bytes 786440 | tf_op jit(solution)/shard_map/ppermute | solution.py:530
  93.9 5.2 %collective-permute-done.2.s3 = bf16[1024,128]{1,0:T(8,128)(2,1)S(1)} collective-permute-done((bf16[1024,128]{1,0:T(8,128)(2,1)S(1)}, bf16[1024,128]{1,0:T(8,128)(2,1)S(1)}, u32[]{:S(2)}, u32[]{:S(2)}) %collective-permute-start.2) | collective-permute-done | bytes 262176 | tf_op jit(solution)/shard_map/ppermute | solution.py:530
  99.1 7.4 %early.1 = (bf16[4,1024,128]{2,1,0:T(8,128)(2,1)S(1)}, bf16[8,80,1024]{2,1,0:T(8,128)(2,1)S(1)}, bf16[4,512,128]{2,1,0:T(8,128)(2,1)S(1)}, bf16[512,512]{1,0:T(8,128)(2,1)S(1)}) custom-call(s32[2]{0:T(128)S(1)} %copy-done.5, bf16[1024,128]{1,0:T(8,128)(2,1)S(1)} %pick_more.4.after_ref.s0, bf16[1024,128]{1,0:T(8,128)(2,1)S(1)} %collective-permute-done.5.s1, ...), custom_call_target="tpu_custom_call" | custom-call | flops 7000000000 | bytes 6000000 | tf_op jit(solution)/shard_map/early/pallas_call | solution.py:421
  106.7 7.1 %late.1 = (bf16[4,1024,128]{2,1,0:T(8,128)(2,1)S(1)}, bf16[8,80,1024]{2,1,0:T(8,128)(2,1)S(1)}, bf16[4,512,128]{2,1,0:T(8,128)(2,1)S(1)}, bf16[4,256,128]{2,1,0:T(8,128)(2,1)S(1)}, bf16[512,512]{1,0:T(8,128)(2,1)S(1)}) custom-call(s32[2]{0:T(128)S(1)} %copy-done.5, bf16[1024,128]{1,0:T(8,128)(2,1)S(1)} %pick_more.3.s0, ...), custom_call_target="tpu_custom_call" | custom-call | flops 7000000000 | bytes 6000000 | tf_op jit(solution)/shard_map/late/pallas_call | solution.py:444
  113.9 2.7 %mlp.3.after_ref = bf16[256,512]{1,0:T(8,128)(2,1)S(1)} custom-call(bf16[512,512]{1,0:T(8,128)(2,1)S(1)} %get-tuple-element.31.after_ref.res1_ref, bf16[4,512,128]{2,1,0:T(8,128)(2,1)S(1)} %get-tuple-element.32.early_ref, bf16[512,512]{1,0:T(8,128)(2,1)S(1)} %get-tuple-element.33.res0_ref, bf16[512,512]{1,0:T(8,128)(2,1)S(1)} %get-tuple-element.31.after_ref.res1_ref, ...), custom_call_target="tpu_custom_call" | custom-call | flops 1792000000 | bytes 6000000 | tf_op jit(solution)/shard_map/mlp/pallas_call | solution.py:517
  116.6 2.5 %collective-permute-start.6 = (bf16[256,512]{1,0:T(8,128)(2,1)S(1)}, bf16[256,512]{1,0:T(8,128)(2,1)S(1)}, u32[]{:S(2)}, u32[]{:S(2)}) collective-permute-start(bf16[256,512]{1,0:T(8,128)(2,1)S(1)} %mlp.3.after_ref), channel_id=1, source_target_pairs={{0,3},{3,0},{1,2},{2,1},{4,7},{7,4},{5,6},{6,5},{8,11},{11,8},{9,1... | collective-permute-start | bytes 786440 | tf_op jit(solution)/shard_map/ppermute | solution.py:530
  119.1 5.0 %last.1.after_ref.refs_0_.refs_1_ = bf16[4,256,128]{2,1,0:T(8,128)(2,1)S(1)} custom-call(s32[2]{0:T(128)S(1)} %copy-done.5, bf16[4,512,128]{2,1,0:T(8,128)(2,1)S(1)} %get-tuple-element.28.q_ref, bf16[4,1024,128]{2,1,0:T(8,128)(2,1)S(1)} %get-tuple-element.26.k0_ref, bf16[8,80,1024]{2,1,0:T(8,128)(2,1)S(1)} %get-tuple-element.27.v0_ref, ...), custom_call_target="tpu_custom_call" | custom-call | flops 5000000000 | bytes 6000000 | tf_op jit(solution)/shard_map/last/pallas_call | solution.py:467
  124.1 2.7 %mlp.4.after_ref = bf16[256,512]{1,0:T(8,128)(2,1)S(1)} custom-call(bf16[4,256,128]{2,1,0:T(8,128)(2,1)S(1)} %last.1.after_ref.refs_0_.refs_1_, bf16[4,512,128]{2,1,0:T(8,128)(2,1)S(1)} %get-tuple-element.32.early_ref, bf16[512,512]{1,0:T(8,128)(2,1)S(1)} %get-tuple-element.33.res0_ref, bf16[512,512]{1,0:T(8,128)(2,1)S(1)} %get-tuple-element.31.after_ref.res1_ref, ...), custom_call_target="tpu_custom_call" | custom-call | flops 1792000000 | bytes 6000000 | tf_op jit(solution)/shard_map/mlp/pallas_call | solution.py:517
  126.8 2.0 %collective-permute-start.7 = (bf16[256,512]{1,0:T(8,128)(2,1)S(1)}, bf16[256,512]{1,0:T(8,128)(2,1)S(1)}, u32[]{:S(2)}, u32[]{:S(2)}) collective-permute-start(bf16[256,512]{1,0:T(8,128)(2,1)S(1)} %mlp.4.after_ref), channel_id=1, source_target_pairs={{0,3},{3,0},{1,2},{2,1},{4,7},{7,4},{5,6},{6,5},{8,11},{11,8},{9,1... | collective-permute-start | bytes 786440 | tf_op jit(solution)/shard_map/ppermute | solution.py:530
  128.8 4.6 %mlp.5 = bf16[512,512]{1,0:T(8,128)(2,1)S(1)} custom-call(bf16[256,512]{1,0:T(8,128)(2,1)S(1)} %mlp.4.after_ref, bf16[4,512,128]{2,1,0:T(8,128)(2,1)S(1)} %get-tuple-element.32.early_ref, bf16[512,512]{1,0:T(8,128)(2,1)S(1)} %get-tuple-element.33.res0_ref, bf16[512,512]{1,0:T(8,128)(2,1)S(1)} %get-tuple-element.31.after_ref.res1_ref, ...), custom_call_target="tpu_custom_call" | custom-call | flops 3584000000 | bytes 6000000 | tf_op jit(solution)/shard_map/mlp/pallas_call | solution.py:517
  (33 shorter events, 4.7 us)
Async XLA Ops:
  36.5 4.1 %copy-start.6 = (f32[512]{0:T(512)S(1)}, f32[512]{0:T(512)}, u32[]{:S(2)}) copy-start(f32[512]{0:T(512)} %param.12) | copy-start | bytes 6148
  36.5 42.5 %all-to-all-start.2 = ((bf16[32,344,128]{2,1,0:T(8,128)(2,1)}), bf16[32,344,128]{2,1,0:T(8,128)(2,1)S(1)}, u32[]{:S(2)}, u32[]{:S(2)}) async-start(bf16[32,344,128]{2,1,0:T(8,128)(2,1)} %lookup.1), calls=%async_computation.2 | async-start | bytes 5636096 | tf_op jit(solution)/shard_map/all_to_all | solution.py:550
  80.6 9.3 %collective-permute-start = (bf16[1024,128]{1,0:T(8,128)(2,1)S(1)}, bf16[1024,128]{1,0:T(8,128)(2,1)S(1)}, u32[]{:S(2)}, u32[]{:S(2)}) collective-permute-start(bf16[1024,128]{1,0:T(8,128)(2,1)S(1)} %get-tuple-element.23.after_ref), channel_id=1, source_target_pairs={{0,3},{3,0},{1,2},{2,1},{4,7},{7,4},{5,6},{6,5},{8,11},{11,8},{9,1... | collective-permute-start | bytes 786440 | tf_op jit(solution)/shard_map/ppermute | solution.py:530
  83.4 15.7 %collective-permute-start.5 = (bf16[1024,128]{1,0:T(8,128)(2,1)S(1)}, bf16[1024,128]{1,0:T(8,128)(2,1)S(1)}, u32[]{:S(2)}, u32[]{:S(2)}) collective-permute-start(bf16[1024,128]{1,0:T(8,128)(2,1)S(1)} %pick_more.4.after_ref.s0), channel_id=1, source_target_pairs={{0,1},{1,0},{2,3},{3,2},{4,5},{5,4},{6,7},{7,6},{8,9},{9,8},{10,11... | collective-permute-start | bytes 786440 | tf_op jit(solution)/shard_map/ppermute | solution.py:530
  85.1 8.8 %collective-permute-start.3 = (bf16[1024,128]{1,0:T(8,128)(2,1)S(1)}, bf16[1024,128]{1,0:T(8,128)(2,1)S(1)}, u32[]{:S(2)}, u32[]{:S(2)}) collective-permute-start(bf16[1024,128]{1,0:T(8,128)(2,1)S(1)} %pick_more.5), channel_id=1, source_target_pairs={{0,3},{3,0},{1,2},{2,1},{4,7},{7,4},{5,6},{6,5},{8,11},{11,8},{9,1... | collective-permute-start | bytes 786440 | tf_op jit(solution)/shard_map/ppermute | solution.py:530
  89.9 9.2 %collective-permute-start.2 = (bf16[1024,128]{1,0:T(8,128)(2,1)S(1)}, bf16[1024,128]{1,0:T(8,128)(2,1)S(1)}, u32[]{:S(2)}, u32[]{:S(2)}) collective-permute-start(bf16[1024,128]{1,0:T(8,128)(2,1)S(1)} %collective-permute-done.after_ref.s2), channel_id=1, source_target_pairs={{0,1},{1,0},{2,3},{3,2},{4,5},{5,4},{6,7},{7,6},{8,9},{9,8},{10,11... | collective-permute-start | bytes 786440 | tf_op jit(solution)/shard_map/ppermute | solution.py:530
  89.9 9.2 %copy-start.3 = (bf16[512,1536]{1,0:T(8,128)(2,1)S(1)}, bf16[512,1536]{1,0:T(8,128)(2,1)}, u32[]{:S(2)}) copy-start(bf16[512,1536]{1,0:T(8,128)(2,1)} %w_ref.3) | copy-start | bytes 4718596
  90.0 9.2 %copy-start.5 = (s32[2]{0:T(128)S(1)}, s32[2]{0:T(128)}, u32[]{:S(2)}) copy-start(s32[2]{0:T(128)} %length_ref.5) | copy-start | bytes 28
  91.6 15.0 %collective-permute-start.1 = (bf16[1024,128]{1,0:T(8,128)(2,1)S(1)}, bf16[1024,128]{1,0:T(8,128)(2,1)S(1)}, u32[]{:S(2)}, u32[]{:S(2)}) collective-permute-start(bf16[1024,128]{1,0:T(8,128)(2,1)S(1)} %pick_more.3.s0), channel_id=1, source_target_pairs={{0,1},{1,0},{2,3},{3,2},{4,5},{5,4},{6,7},{7,6},{8,9},{9,8},{10,11... | collective-permute-start | bytes 786440 | tf_op jit(solution)/shard_map/ppermute | solution.py:530
  99.1 7.6 %collective-permute-start.4 = (bf16[1024,128]{1,0:T(8,128)(2,1)S(1)}, bf16[1024,128]{1,0:T(8,128)(2,1)S(1)}, u32[]{:S(2)}, u32[]{:S(2)}) collective-permute-start(bf16[1024,128]{1,0:T(8,128)(2,1)S(1)} %collective-permute-done.3.s2), channel_id=1, source_target_pairs={{0,1},{1,0},{2,3},{3,2},{4,5},{5,4},{6,7},{7,6},{8,9},{9,8},{10,11... | collective-permute-start | bytes 786440 | tf_op jit(solution)/shard_map/ppermute | solution.py:530
  106.7 7.2 %copy-start = (bf16[512,4096]{1,0:T(8,128)(2,1)S(1)}, bf16[512,4096]{1,0:T(8,128)(2,1)}, u32[]{:S(2)}) copy-start(bf16[512,4096]{1,0:T(8,128)(2,1)} %refs_4_.5) | copy-start | bytes 12582916
  106.7 7.2 %copy-start.1 = (bf16[2048,512]{1,0:T(8,128)(2,1)S(1)}, bf16[2048,512]{1,0:T(8,128)(2,1)}, u32[]{:S(2)}) copy-start(bf16[2048,512]{1,0:T(8,128)(2,1)} %refs_5_.1) | copy-start | bytes 6291460
  106.7 7.2 %copy-start.2 = (bf16[512,512]{1,0:T(8,128)(2,1)S(1)}, bf16[512,512]{1,0:T(8,128)(2,1)}, u32[]{:S(2)}) copy-start(bf16[512,512]{1,0:T(8,128)(2,1)} %refs_2_.1) | copy-start | bytes 1572868
  106.7 7.2 %copy-start.4 = (f32[512]{0:T(512)S(1)}, f32[512]{0:T(512)}, u32[]{:S(2)}) copy-start(f32[512]{0:T(512)} %param.15) | copy-start | bytes 6148
  116.6 16.8 %collective-permute-start.6 = (bf16[256,512]{1,0:T(8,128)(2,1)S(1)}, bf16[256,512]{1,0:T(8,128)(2,1)S(1)}, u32[]{:S(2)}, u32[]{:S(2)}) collective-permute-start(bf16[256,512]{1,0:T(8,128)(2,1)S(1)} %mlp.3.after_ref), channel_id=1, source_target_pairs={{0,3},{3,0},{1,2},{2,1},{4,7},{7,4},{5,6},{6,5},{8,11},{11,8},{9,1... | collective-permute-start | bytes 786440 | tf_op jit(solution)/shard_map/ppermute | solution.py:530
  126.8 7.7 %collective-permute-start.7 = (bf16[256,512]{1,0:T(8,128)(2,1)S(1)}, bf16[256,512]{1,0:T(8,128)(2,1)S(1)}, u32[]{:S(2)}, u32[]{:S(2)}) collective-permute-start(bf16[256,512]{1,0:T(8,128)(2,1)S(1)} %mlp.4.after_ref), channel_id=1, source_target_pairs={{0,3},{3,0},{1,2},{2,1},{4,7},{7,4},{5,6},{6,5},{8,11},{11,8},{9,1... | collective-permute-start | bytes 786440 | tf_op jit(solution)/shard_map/ppermute | solution.py:530

commit v6 on v5

--- a/solution.py
+++ b/solution.py
@@ -48,7 +48,7 @@
     group_iota = lax.broadcasted_iota(I32, (owners * parts, width), 0)
     lane_iota = lax.broadcasted_iota(I32, (128, width), 0)
     carry = jnp.zeros((owners, 1), F32)
-    total = jnp.zeros((owners * parts, 256), F32)
+    total = jnp.zeros((2 * owners * parts, 128), F32)
     for r in range(rows):
         ids = ids_ref[r : r + 1, :]
         owner = lax.shift_right_logical(ids, row_bits)
@@ -60,24 +60,25 @@
         slot_ref[r : r + 1, :] = owner * CAP + rank
         place = rank + 1
         group = owner * parts + lax.shift_right_logical(place, 7)
-        in_group = (group_iota == group).astype(BF)
-        at_lane = lane_iota == (place & 127)
-        high = jnp.where(at_lane, lax.shift_right_logical(offset, 7), 0).astype(F32).astype(BF)
-        low = jnp.where(at_lane, offset & 127, 0).astype(F32).astype(BF)
-        total = total + dot_t(in_group, jnp.concatenate([high, low], axis=0))
+        in_group = group_iota == group
+        at_lane = (lane_iota == (place & 127)).astype(F32).astype(BF)
+        high = jnp.where(in_group, lax.shift_right_logical(offset, 7).astype(F32), 0.0).astype(BF)
+        low = jnp.where(in_group, (offset & 127).astype(F32), 0.0).astype(BF)
+        total = total + dot_t(jnp.concatenate([high, low], axis=0), at_lane)
     count = carry.astype(I32)
     first_group = (
         lax.broadcasted_iota(I32, (owners * parts, owners), 0)
         == lax.broadcasted_iota(I32, (owners * parts, owners), 1) * parts
     ).astype(BF)
-    lane = lax.broadcasted_iota(I32, (owners, 256), 1)
-    digits = jnp.where(
-        lane == 0,
-        lax.shift_right_logical(count, 7),
-        jnp.where(lane == 128, count & 127, 0),
-    )
-    total = total + dot(first_group, digits.astype(F32).astype(BF))
-    req_ref[...] = total[:, :128].astype(I32) * 128 + total[:, 128:].astype(I32)
+    lane = lax.broadcasted_iota(I32, (owners, 128), 1)
+    digits = [
+        jnp.where(lane == 0, digit, 0).astype(F32).astype(BF)
+        for digit in (lax.shift_right_logical(count, 7), count & 127)
+    ]
+    half = owners * parts
+    high = total[:half, :] + dot(first_group, digits[0])
+    low = total[half:, :] + dot(first_group, digits[1])
+    req_ref[...] = high.astype(I32) * 128 + low.astype(I32)
 
 
 def route(ids, row_bits, owners):
@@ -168,7 +169,7 @@
 
 def lookup(asked, table, owners):
     rows, width = table.shape
-    chunks = 8
+    chunks = 16
     return pl.pallas_call(
         lookup_kernel,
         out_shape=jax.ShapeDtypeStruct((owners, CAP, width), BF),
@@ -578,14 +579,9 @@
     sent_b = mlp(False, quarter // 2, att_1b, att_0, res_0, res_1, (att_1b,), weights)
     came_b = exchange(sent_b, CROSS)
     kept = mlp(True, 0, sent_b, att_0, res_0, res_1, (att_1a, att_1b), weights)
-    which = lax.broadcasted_iota(I32, (batch_dev, quarter // 2, D), 0) == h
-    return jnp.concatenate(
-        [
-            jnp.where(which, kept[None, : quarter // 2], came_a[None]),
-            jnp.where(which, kept[None, quarter // 2 :], came_b[None]),
-        ],
-        axis=1,
-    )
+    came = jnp.concatenate([came_a, came_b], axis=0)
+    which = lax.broadcasted_iota(I32, (batch_dev, quarter, D), 0) == h
+    return jnp.where(which, kept[None], came[None])
 
 
 def solution(mesh):

time: 136 us -> 135 us (level); the launches traced: 136 us -> 133 us
  Pallas kernels: 46.4 us -> 43.2 us
  transfers between devices with their start and end apart: 9 -> 9, of which waited for: 6 -> 6; matrix products, arithmetic and copies ran while one was open for 2% -> 2% of each run, Pallas kernels for 18% -> 17%
where the time goes in v6:
time: 135 us; the launch traced here: 133 us
  waiting for transfers between devices  44.9 us (33%)
  Pallas kernels  43.2 us (32%)
  blocking collectives  25.2 us (19%)
  starting transfers between devices  14.5 us (11%)
  local copies, waits for them, and re-layouts  3.88 us (3%)
    all_to_all x1, waiting for transfers between devices, local(): lax.all_to_all(looked, 'rows', split_axis=0, concat_axis=0, tiled=True)  35.2 us
    all_to_all x1, blocking collectives, local(): lax.all_to_all(requests.reshape(owners, REQ), 'rows', split_axis=0, conca...  14.7 us
    all_to_all x1, blocking collectives, local(): lax.all_to_all(copies, 'cols', split_axis=0, concat_axis=0, tiled=True)  10.6 us
    ppermute x8, starting transfers between devices, exchange(): return lax.ppermute(x, 'cols', pairs)  10.4 us
    pallas_call x3, Pallas kernels, mlp(): pl.pallas_call(functools.partial(mlp_kernel, kept, start), out_shape=jax....  9.92 us
    ppermute x8, waiting for transfers between devices, exchange(): return lax.ppermute(x, 'cols', pairs)  9.68 us
    pallas_call x1, Pallas kernels, lookup(): pl.pallas_call(lookup_kernel, out_shape=jax.ShapeDtypeStruct((owners, CAP...  8.39 us
    pallas_call x1, Pallas kernels, early(): pl.pallas_call(early_kernel, out_shape=(jax.ShapeDtypeStruct((4, half, 12...  7.44 us
  transfers between devices with their start and end apart: 9, of which 6 were waited for; matrix products, arithmetic and copies ran while one was open for 2% of the time, Pallas kernels for 17%

profile of v6, /device:TPU:0, one launch (start us, length us, event | category | flops | bytes accessed | tf_op | source)
XLA Modules:
  0.0 133.1 jit_solution(16857275491574207344)
XLA Ops:
  0.7 10.6 %all_to_all.19 = s32[4,2,512]{2,1,0:T(2,128)S(1)} all-to-all(s32[4,2,512]{2,1,0:T(2,128)S(1)} %broadcast_in_dim.21), channel_id=1, replica_groups=mesh['rows'=32,'cols'=4] {'cols'}, dimensions={0} | all-to-all | bytes 32768 | tf_op jit(solution)/shard_map/all_to_all | solution.py:544
  11.3 1.4 %route.1 = (s32[8,512]{1,0:T(8,128)S(1)}, s32[96,128]{1,0:T(8,128)S(1)}) custom-call(s32[8,512]{1,0:T(8,128)S(1)} %reshape.25.ids_ref), custom_call_target="tpu_custom_call" | custom-call | tf_op jit(solution)/shard_map/route/pallas_call | solution.py:85
  12.7 14.7 %all_to_all.20 = s32[32,1,384]{2,1,0:T(1,128)} all-to-all(s32[32,1,384]{2,1,0:T(1,128)S(1)} %bitcast.11), channel_id=1, replica_groups=mesh['rows'=32,'cols'=4] {'rows'}, dimensions={0} | all-to-all | bytes 98304 | tf_op jit(solution)/shard_map/all_to_all | solution.py:547
  27.4 8.4 %lookup.1 = bf16[32,344,128]{2,1,0:T(8,128)(2,1)} custom-call(s32[12288]{0:T(1024)} %bitcast.21, bf16[16384,128]{1,0:T(8,128)(2,1)} %table_ref.1), custom_call_target="tpu_custom_call" | custom-call | flops 6000000000 | bytes 4000000 | tf_op jit(solution)/shard_map/lookup/pallas_call | solution.py:173
  35.8 4.1 %all-to-all-start.2 = ((bf16[32,344,128]{2,1,0:T(8,128)(2,1)}), bf16[32,344,128]{2,1,0:T(8,128)(2,1)S(1)}, u32[]{:S(2)}, u32[]{:S(2)}) async-start(bf16[32,344,128]{2,1,0:T(8,128)(2,1)} %lookup.1), calls=%async_computation.2 | async-start | bytes 5636096 | tf_op jit(solution)/shard_map/all_to_all | solution.py:551
  39.9 1.9 %slice.3 = bf16[512,512]{1,0:T(8,128)(2,1)} slice(bf16[512,1536]{1,0:T(8,128)(2,1)} %w_ref.3), slice={[0:512], [1024:1536]} | slice | bytes 1048576 | tf_op jit(solution)/shard_map/slice | solution.py:568
  43.0 35.2 %all-to-all-done.2 = bf16[32,344,128]{2,1,0:T(8,128)(2,1)S(1)} async-done(((bf16[32,344,128]{2,1,0:T(8,128)(2,1)}), bf16[32,344,128]{2,1,0:T(8,128)(2,1)S(1)}, u32[]{:S(2)}, u32[]{:S(2)}) %all-to-all-start.2) | async-done | bytes 2818080 | tf_op jit(solution)/shard_map/all_to_all | solution.py:551
  78.2 1.6 %pick_first.1 = (bf16[1024,128]{1,0:T(8,128)(2,1)S(1)}, f32[11008,128]{1,0:T(8,128)S(1)}) custom-call(s32[4096]{0:T(1024)S(1)} %bitcast.13, bf16[11008,128]{1,0:T(8,128)(2,1)S(1)} %bitcast.8), custom_call_target="tpu_custom_call" | custom-call | flops 3000000000 | bytes 4000000 | tf_op jit(solution)/shard_map/pick_first/pallas_call | solution.py:248
  81.1 1.6 %pick_more.4.after_ref.s0 = bf16[1024,128]{1,0:T(8,128)(2,1)S(1)} custom-call(s32[4096]{0:T(1024)S(1)} %bitcast.14, f32[11008,128]{1,0:T(8,128)S(1)} %get-tuple-element.22.wide_ref, bf16[1024,128]{1,0:T(8,128)(2,1)S(1)} %get-tuple-element.23.after_ref), custom_call_target="tpu_custom_call" | custom-call | flops 2000000000 | bytes 4000000 | tf_op jit(solution)/shard_map/pick_more/pallas_call | solution.py:269
  82.8 1.6 %pick_more.5 = bf16[1024,128]{1,0:T(8,128)(2,1)S(1)} custom-call(s32[4096]{0:T(1024)S(1)} %bitcast.15, f32[11008,128]{1,0:T(8,128)S(1)} %get-tuple-element.22.wide_ref, bf16[1024,128]{1,0:T(8,128)(2,1)S(1)} %pick_more.4.after_ref.s0), custom_call_target="tpu_custom_call" | custom-call | flops 2000000000 | bytes 4000000 | tf_op jit(solution)/shard_map/pick_more/pallas_call | solution.py:269
  84.4 2.1 %collective-permute-start.3 = (bf16[1024,128]{1,0:T(8,128)(2,1)S(1)}, bf16[1024,128]{1,0:T(8,128)(2,1)S(1)}, u32[]{:S(2)}, u32[]{:S(2)}) collective-permute-start(bf16[1024,128]{1,0:T(8,128)(2,1)S(1)} %pick_more.5), channel_id=1, source_target_pairs={{0,3},{3,0},{1,2},{2,1},{4,7},{7,4},{5,6},{6,5},{8,11},{11,8},{9,1... | collective-permute-start | bytes 786440 | tf_op jit(solution)/shard_map/ppermute | solution.py:531
  86.5 2.7 %collective-permute-done.after_ref.s2 = bf16[1024,128]{1,0:T(8,128)(2,1)S(1)} collective-permute-done((bf16[1024,128]{1,0:T(8,128)(2,1)S(1)}, bf16[1024,128]{1,0:T(8,128)(2,1)S(1)}, u32[]{:S(2)}, u32[]{:S(2)}) %collective-permute-start) | collective-permute-done | bytes 262176 | tf_op jit(solution)/shard_map/ppermute | solution.py:531
  89.2 1.6 %pick_more.3.s0 = bf16[1024,128]{1,0:T(8,128)(2,1)S(1)} custom-call(s32[4096]{0:T(1024)S(1)} %bitcast.16, f32[11008,128]{1,0:T(8,128)S(1)} %get-tuple-element.22.wide_ref, bf16[1024,128]{1,0:T(8,128)(2,1)S(1)} %collective-permute-done.after_ref.s2), custom_call_target="tpu_custom_call" | custom-call | flops 2000000000 | bytes 4000000 | tf_op jit(solution)/shard_map/pick_more/pallas_call | solution.py:269
  90.8 2.1 %collective-permute-start.1 = (bf16[1024,128]{1,0:T(8,128)(2,1)S(1)}, bf16[1024,128]{1,0:T(8,128)(2,1)S(1)}, u32[]{:S(2)}, u32[]{:S(2)}) collective-permute-start(bf16[1024,128]{1,0:T(8,128)(2,1)S(1)} %pick_more.3.s0), channel_id=1, source_target_pairs={{0,1},{1,0},{2,3},{3,2},{4,5},{5,4},{6,7},{7,6},{8,9},{9,8},{10,11... | collective-permute-start | bytes 786440 | tf_op jit(solution)/shard_map/ppermute | solution.py:531
  93.1 5.2 %collective-permute-done.2.s3 = bf16[1024,128]{1,0:T(8,128)(2,1)S(1)} collective-permute-done((bf16[1024,128]{1,0:T(8,128)(2,1)S(1)}, bf16[1024,128]{1,0:T(8,128)(2,1)S(1)}, u32[]{:S(2)}, u32[]{:S(2)}) %collective-permute-start.2) | collective-permute-done | bytes 262176 | tf_op jit(solution)/shard_map/ppermute | solution.py:531
  98.4 7.4 %early.1 = (bf16[4,1024,128]{2,1,0:T(8,128)(2,1)S(1)}, bf16[8,80,1024]{2,1,0:T(8,128)(2,1)S(1)}, bf16[4,512,128]{2,1,0:T(8,128)(2,1)S(1)}, bf16[512,512]{1,0:T(8,128)(2,1)S(1)}) custom-call(s32[2]{0:T(128)S(1)} %copy-done.5, bf16[1024,128]{1,0:T(8,128)(2,1)S(1)} %pick_more.4.after_ref.s0, bf16[1024,128]{1,0:T(8,128)(2,1)S(1)} %collective-permute-done.5.s1, ...), custom_call_target="tpu_custom_call" | custom-call | flops 7000000000 | bytes 6000000 | tf_op jit(solution)/shard_map/early/pallas_call | solution.py:422
  106.0 6.0 %late.1 = (bf16[4,1024,128]{2,1,0:T(8,128)(2,1)S(1)}, bf16[8,80,1024]{2,1,0:T(8,128)(2,1)S(1)}, bf16[4,512,128]{2,1,0:T(8,128)(2,1)S(1)}, bf16[4,256,128]{2,1,0:T(8,128)(2,1)S(1)}, bf16[512,512]{1,0:T(8,128)(2,1)S(1)}) custom-call(s32[2]{0:T(128)S(1)} %copy-done.5, bf16[1024,128]{1,0:T(8,128)(2,1)S(1)} %pick_more.3.s0, ...), custom_call_target="tpu_custom_call" | custom-call | flops 7000000000 | bytes 6000000 | tf_op jit(solution)/shard_map/late/pallas_call | solution.py:445
  112.0 2.7 %mlp.3.after_ref = bf16[256,512]{1,0:T(8,128)(2,1)S(1)} custom-call(bf16[512,512]{1,0:T(8,128)(2,1)S(1)} %get-tuple-element.31.after_ref.res1_ref, bf16[4,512,128]{2,1,0:T(8,128)(2,1)S(1)} %get-tuple-element.32.early_ref, bf16[512,512]{1,0:T(8,128)(2,1)S(1)} %get-tuple-element.33.res0_ref, bf16[512,512]{1,0:T(8,128)(2,1)S(1)} %get-tuple-element.31.after_ref.res1_ref, ...), custom_call_target="tpu_custom_call" | custom-call | flops 1792000000 | bytes 6000000 | tf_op jit(solution)/shard_map/mlp/pallas_call | solution.py:518
  114.7 3.1 %collective-permute-start.6 = (bf16[256,512]{1,0:T(8,128)(2,1)S(1)}, bf16[256,512]{1,0:T(8,128)(2,1)S(1)}, u32[]{:S(2)}, u32[]{:S(2)}) collective-permute-start(bf16[256,512]{1,0:T(8,128)(2,1)S(1)} %mlp.3.after_ref), channel_id=1, source_target_pairs={{0,3},{3,0},{1,2},{2,1},{4,7},{7,4},{5,6},{6,5},{8,11},{11,8},{9,1... | collective-permute-start | bytes 786440 | tf_op jit(solution)/shard_map/ppermute | solution.py:531
  117.8 3.8 %last.1.after_ref.refs_0_.refs_1_ = bf16[4,256,128]{2,1,0:T(8,128)(2,1)S(1)} custom-call(s32[2]{0:T(128)S(1)} %copy-done.5, bf16[4,512,128]{2,1,0:T(8,128)(2,1)S(1)} %get-tuple-element.28.q_ref, bf16[4,1024,128]{2,1,0:T(8,128)(2,1)S(1)} %get-tuple-element.26.k0_ref, bf16[8,80,1024]{2,1,0:T(8,128)(2,1)S(1)} %get-tuple-element.27.v0_ref, ...), custom_call_target="tpu_custom_call" | custom-call | flops 5000000000 | bytes 6000000 | tf_op jit(solution)/shard_map/last/pallas_call | solution.py:468
  121.6 2.7 %mlp.4.after_ref = bf16[256,512]{1,0:T(8,128)(2,1)S(1)} custom-call(bf16[4,256,128]{2,1,0:T(8,128)(2,1)S(1)} %last.1.after_ref.refs_0_.refs_1_, bf16[4,512,128]{2,1,0:T(8,128)(2,1)S(1)} %get-tuple-element.32.early_ref, bf16[512,512]{1,0:T(8,128)(2,1)S(1)} %get-tuple-element.33.res0_ref, bf16[512,512]{1,0:T(8,128)(2,1)S(1)} %get-tuple-element.31.after_ref.res1_ref, ...), custom_call_target="tpu_custom_call" | custom-call | flops 1792000000 | bytes 6000000 | tf_op jit(solution)/shard_map/mlp/pallas_call | solution.py:518
  124.3 1.7 %collective-permute-start.7 = (bf16[256,512]{1,0:T(8,128)(2,1)S(1)}, bf16[256,512]{1,0:T(8,128)(2,1)S(1)}, u32[]{:S(2)}, u32[]{:S(2)}) collective-permute-start(bf16[256,512]{1,0:T(8,128)(2,1)S(1)} %mlp.4.after_ref), channel_id=1, source_target_pairs={{0,3},{3,0},{1,2},{2,1},{4,7},{7,4},{5,6},{6,5},{8,11},{11,8},{9,1... | collective-permute-start | bytes 786440 | tf_op jit(solution)/shard_map/ppermute | solution.py:531
  126.0 4.6 %mlp.5 = bf16[512,512]{1,0:T(8,128)(2,1)S(1)} custom-call(bf16[256,512]{1,0:T(8,128)(2,1)S(1)} %mlp.4.after_ref, bf16[4,512,128]{2,1,0:T(8,128)(2,1)S(1)} %get-tuple-element.32.early_ref, bf16[512,512]{1,0:T(8,128)(2,1)S(1)} %get-tuple-element.33.res0_ref, bf16[512,512]{1,0:T(8,128)(2,1)S(1)} %get-tuple-element.31.after_ref.res1_ref, ...), custom_call_target="tpu_custom_call" | custom-call | flops 3584000000 | bytes 6000000 | tf_op jit(solution)/shard_map/mlp/pallas_call | solution.py:518
  130.5 1.4 %collective-permute-done.7 = bf16[256,512]{1,0:T(8,128)(2,1)S(1)} collective-permute-done((bf16[256,512]{1,0:T(8,128)(2,1)S(1)}, bf16[256,512]{1,0:T(8,128)(2,1)S(1)}, u32[]{:S(2)}, u32[]{:S(2)}) %collective-permute-start.7) | collective-permute-done | bytes 262176 | tf_op jit(solution)/shard_map/ppermute | solution.py:531
  (32 shorter events, 4.9 us)
Async XLA Ops:
  35.8 4.1 %copy-start.6 = (f32[512]{0:T(512)S(1)}, f32[512]{0:T(512)}, u32[]{:S(2)}) copy-start(f32[512]{0:T(512)} %param.12) | copy-start | bytes 6148
  35.8 42.5 %all-to-all-start.2 = ((bf16[32,344,128]{2,1,0:T(8,128)(2,1)}), bf16[32,344,128]{2,1,0:T(8,128)(2,1)S(1)}, u32[]{:S(2)}, u32[]{:S(2)}) async-start(bf16[32,344,128]{2,1,0:T(8,128)(2,1)} %lookup.1), calls=%async_computation.2 | async-start | bytes 5636096 | tf_op jit(solution)/shard_map/all_to_all | solution.py:551
  79.8 9.3 %collective-permute-start = (bf16[1024,128]{1,0:T(8,128)(2,1)S(1)}, bf16[1024,128]{1,0:T(8,128)(2,1)S(1)}, u32[]{:S(2)}, u32[]{:S(2)}) collective-permute-start(bf16[1024,128]{1,0:T(8,128)(2,1)S(1)} %get-tuple-element.23.after_ref), channel_id=1, source_target_pairs={{0,3},{3,0},{1,2},{2,1},{4,7},{7,4},{5,6},{6,5},{8,11},{11,8},{9,1... | collective-permute-start | bytes 786440 | tf_op jit(solution)/shard_map/ppermute | solution.py:531
  82.7 15.7 %collective-permute-start.5 = (bf16[1024,128]{1,0:T(8,128)(2,1)S(1)}, bf16[1024,128]{1,0:T(8,128)(2,1)S(1)}, u32[]{:S(2)}, u32[]{:S(2)}) collective-permute-start(bf16[1024,128]{1,0:T(8,128)(2,1)S(1)} %pick_more.4.after_ref.s0), channel_id=1, source_target_pairs={{0,1},{1,0},{2,3},{3,2},{4,5},{5,4},{6,7},{7,6},{8,9},{9,8},{10,11... | collective-permute-start | bytes 786440 | tf_op jit(solution)/shard_map/ppermute | solution.py:531
  84.4 8.7 %collective-permute-start.3 = (bf16[1024,128]{1,0:T(8,128)(2,1)S(1)}, bf16[1024,128]{1,0:T(8,128)(2,1)S(1)}, u32[]{:S(2)}, u32[]{:S(2)}) collective-permute-start(bf16[1024,128]{1,0:T(8,128)(2,1)S(1)} %pick_more.5), channel_id=1, source_target_pairs={{0,3},{3,0},{1,2},{2,1},{4,7},{7,4},{5,6},{6,5},{8,11},{11,8},{9,1... | collective-permute-start | bytes 786440 | tf_op jit(solution)/shard_map/ppermute | solution.py:531
  89.2 9.2 %collective-permute-start.2 = (bf16[1024,128]{1,0:T(8,128)(2,1)S(1)}, bf16[1024,128]{1,0:T(8,128)(2,1)S(1)}, u32[]{:S(2)}, u32[]{:S(2)}) collective-permute-start(bf16[1024,128]{1,0:T(8,128)(2,1)S(1)} %collective-permute-done.after_ref.s2), channel_id=1, source_target_pairs={{0,1},{1,0},{2,3},{3,2},{4,5},{5,4},{6,7},{7,6},{8,9},{9,8},{10,11... | collective-permute-start | bytes 786440 | tf_op jit(solution)/shard_map/ppermute | solution.py:531
  89.2 9.2 %copy-start.3 = (bf16[512,1536]{1,0:T(8,128)(2,1)S(1)}, bf16[512,1536]{1,0:T(8,128)(2,1)}, u32[]{:S(2)}) copy-start(bf16[512,1536]{1,0:T(8,128)(2,1)} %w_ref.3) | copy-start | bytes 4718596
  89.2 9.2 %copy-start.5 = (s32[2]{0:T(128)S(1)}, s32[2]{0:T(128)}, u32[]{:S(2)}) copy-start(s32[2]{0:T(128)} %length_ref.5) | copy-start | bytes 28
  90.8 15.0 %collective-permute-start.1 = (bf16[1024,128]{1,0:T(8,128)(2,1)S(1)}, bf16[1024,128]{1,0:T(8,128)(2,1)S(1)}, u32[]{:S(2)}, u32[]{:S(2)}) collective-permute-start(bf16[1024,128]{1,0:T(8,128)(2,1)S(1)} %pick_more.3.s0), channel_id=1, source_target_pairs={{0,1},{1,0},{2,3},{3,2},{4,5},{5,4},{6,7},{7,6},{8,9},{9,8},{10,11... | collective-permute-start | bytes 786440 | tf_op jit(solution)/shard_map/ppermute | solution.py:531
  98.3 7.6 %collective-permute-start.4 = (bf16[1024,128]{1,0:T(8,128)(2,1)S(1)}, bf16[1024,128]{1,0:T(8,128)(2,1)S(1)}, u32[]{:S(2)}, u32[]{:S(2)}) collective-permute-start(bf16[1024,128]{1,0:T(8,128)(2,1)S(1)} %collective-permute-done.3.s2), channel_id=1, source_target_pairs={{0,1},{1,0},{2,3},{3,2},{4,5},{5,4},{6,7},{7,6},{8,9},{9,8},{10,11... | collective-permute-start | bytes 786440 | tf_op jit(solution)/shard_map/ppermute | solution.py:531
  106.0 6.0 %copy-start = (bf16[512,4096]{1,0:T(8,128)(2,1)S(1)}, bf16[512,4096]{1,0:T(8,128)(2,1)}, u32[]{:S(2)}) copy-start(bf16[512,4096]{1,0:T(8,128)(2,1)} %refs_4_.5) | copy-start | bytes 12582916
  106.0 6.0 %copy-start.1 = (bf16[2048,512]{1,0:T(8,128)(2,1)S(1)}, bf16[2048,512]{1,0:T(8,128)(2,1)}, u32[]{:S(2)}) copy-start(bf16[2048,512]{1,0:T(8,128)(2,1)} %refs_5_.1) | copy-start | bytes 6291460
  106.0 6.0 %copy-start.2 = (bf16[512,512]{1,0:T(8,128)(2,1)S(1)}, bf16[512,512]{1,0:T(8,128)(2,1)}, u32[]{:S(2)}) copy-start(bf16[512,512]{1,0:T(8,128)(2,1)} %refs_2_.1) | copy-start | bytes 1572868
  106.0 6.0 %copy-start.4 = (f32[512]{0:T(512)S(1)}, f32[512]{0:T(512)}, u32[]{:S(2)}) copy-start(f32[512]{0:T(512)} %param.15) | copy-start | bytes 6148
  114.7 17.2 %collective-permute-start.6 = (bf16[256,512]{1,0:T(8,128)(2,1)S(1)}, bf16[256,512]{1,0:T(8,128)(2,1)S(1)}, u32[]{:S(2)}, u32[]{:S(2)}) collective-permute-start(bf16[256,512]{1,0:T(8,128)(2,1)S(1)} %mlp.3.after_ref), channel_id=1, source_target_pairs={{0,3},{3,0},{1,2},{2,1},{4,7},{7,4},{5,6},{6,5},{8,11},{11,8},{9,1... | collective-permute-start | bytes 786440 | tf_op jit(solution)/shard_map/ppermute | solution.py:531
  124.3 7.7 %collective-permute-start.7 = (bf16[256,512]{1,0:T(8,128)(2,1)S(1)}, bf16[256,512]{1,0:T(8,128)(2,1)S(1)}, u32[]{:S(2)}, u32[]{:S(2)}) collective-permute-start(bf16[256,512]{1,0:T(8,128)(2,1)S(1)} %mlp.4.after_ref), channel_id=1, source_target_pairs={{0,3},{3,0},{1,2},{2,1},{4,7},{7,4},{5,6},{6,5},{8,11},{11,8},{9,1... | collective-permute-start | bytes 786440 | tf_op jit(solution)/shard_map/ppermute | solution.py:531
